TPU v7x, 32 devices: a whole 2x2x4 slice. The times are simulated.
32 devices in a mesh: grp: 4 (over x, core), row: 4 (over z), col: 2 (over y).
Axes of the slice: x: 2, y: 2, z: 4, core: 2. Of those that a mesh axis runs over, the one named last changes fastest.
Arguments:
- fields: bfloat16 [4, 4, 192, 1536], P('grp', None, 'row', 'col'), may hold values from -12 to 12
- offset: int32 [1], replicated, may hold values from 0 to 191
- level_index: int32 [4], replicated, may hold values from 0 to 3, each once
- nudge_rate: float32 [4], replicated, may hold values from 0.2 to 0.9
- driving: float32 [4, 64, 64], replicated, may hold values from -4 to 4
Outputs:
- nudged: bfloat16 [4, 4, 192, 1536], P('grp', None, 'row', 'col')
Inputs may be any that keep to these rules, and one draw needn't show every extreme that they name: `offset`: the footprint covers a third of the parent rows from there on, wrapping around the periodic domain. `level_index`: each parent level is fed by exactly one child level.
All inputs are finite; a program needn't handle non-finite values.
Results may differ from a plain program's by a relative error of at most 0.0034.
Values may be sent and summed in bfloat16 or wider, within the bound.
No kernel may reach another device: no remote copies, remote signals or barrier semaphores. Data moves between devices by JAX's collectives and lax.ppermute only.
A program may use at most 64 MiB of HBM per device.

v0:
```python
import functools
import math

import jax
import jax.numpy as jnp
import numpy as np
from jax import lax
from jax.experimental import pallas as pl
from jax.experimental.pallas import tpu as pltpu
from jax.sharding import PartitionSpec as P

MAX_WAVE = 32
BASIS = 2 * MAX_WAVE
AXES = ("grp", "row", "col")
VMEM = pl.BlockSpec(memory_space=pltpu.VMEM)
SMEM = pl.BlockSpec(memory_space=pltpu.SMEM)
ANY = pl.BlockSpec(memory_space=pl.ANY)


def basis_table(positions, cell_count):
    period = 3 * cell_count
    orders = np.arange(1, MAX_WAVE + 1)
    angles = (np.asarray(positions)[:, None] * orders % period) * (2.0 * math.pi / period)
    scale = math.sqrt(2.0 / cell_count)
    constant = np.full((len(positions), 1), 1.0 / math.sqrt(cell_count))
    table = np.concatenate([constant, scale * np.cos(angles), scale * np.sin(angles[:, :-1])], 1)
    return table.astype(np.float32)


def halves(table):
    high = table.astype(jnp.bfloat16)
    return high, (table - high.astype(np.float32)).astype(jnp.bfloat16)


def split(value):
    high = value.astype(jnp.bfloat16)
    return high, (value - high.astype(jnp.float32)).astype(jnp.bfloat16)


def dot(a, b, contract=((1,), (0,))):
    return lax.dot_general(a, b, (contract, ((), ())), preferred_element_type=jnp.float32)


def parity_of_device():
    bits = lax.axis_index("grp") ^ lax.axis_index("row") ^ lax.axis_index("col")
    for shift in (8, 4, 2, 1):
        bits = bits ^ (bits >> shift)
    return bits & 1


def inverse_of(level_ref, parent_level, levels):
    found = jnp.int32(0)
    for level in range(levels):
        found = found + jnp.where(level_ref[level] == parent_level, level, 0)
    return found


def first_kernel(
    full_rows, amplitude, groups, columns, offset, level_index, tile_hbm, cols_hbm, rows_hbm,
    spread_hbm, child_rows_hbm, parent_rows_hbm, driving_hbm,
    averaged, keep, send, tile, spread, weights, target,
    cols, rows, sums, coeffs, turn_rows, driving, sems,
):
    levels, tile_rows, tile_cols = tile.shape
    third_rows, third_cols = tile_rows // 3, tile_cols // 3
    group, row, col = (lax.axis_index(a) for a in AXES)
    is_parent = group == groups - 1
    child_count = child_rows_hbm.shape[0]
    slot = jnp.where(is_parent, (groups - 1) * columns + col, col * (groups - 1) + group)
    copies = [
        pltpu.make_async_copy(tile_hbm, tile, sems.at[0]),
        pltpu.make_async_copy(cols_hbm.at[col], cols, sems.at[1]),
        pltpu.make_async_copy(rows_hbm, rows, sems.at[2]),
    ]
    later = [
        pltpu.make_async_copy(
            spread_hbm.at[slot, part // 2], spread.at[pl.ds(part * BASIS, BASIS)], sems.at[3 + part]
        )
        for part in range(4)
    ] + [
        pltpu.make_async_copy(driving_hbm, driving, sems.at[7]),
        pltpu.make_async_copy(child_rows_hbm, turn_rows.at[pl.ds(0, child_count)], sems.at[8]),
        pltpu.make_async_copy(
            parent_rows_hbm,
            turn_rows.at[pl.ds(child_count, parent_rows_hbm.shape[0])],
            sems.at[9],
        ),
    ]
    for copy in copies + later:
        copy.start()
    shift = offset[0]
    lanes = sums.shape[-1]
    depth = 3 * lanes
    cell = lax.broadcasted_iota(jnp.int32, (depth, lanes), 0)
    block = 3 * lax.broadcasted_iota(jnp.int32, (depth, lanes), 1)
    pick = jnp.where((cell >= block) & (cell < block + 3), 1.0, 0.0).astype(jnp.bfloat16)
    for copy in copies:
        copy.wait()

    def project(blocks, table, weights):
        left = lax.broadcasted_iota(jnp.int32, table.shape, 1) < BASIS
        zero = jnp.zeros_like(table)
        first, second = jnp.where(left, table, zero), jnp.where(left, zero, table)
        for pair in range(levels // 2):
            projected = dot(blocks[2 * pair], first) + dot(blocks[2 * pair + 1], second)
            high, low = split(projected)
            rows_first = ((0,), (0,))
            coeffs[pair] = dot(weights, high, rows_first) + dot(weights, low, rows_first)

    @pl.when(jnp.logical_not(is_parent))
    def _():
        flat = tile[...].reshape(levels * tile_rows, tile_cols)
        for part in range(third_cols // lanes):
            piece = dot(flat[:, part * depth : (part + 1) * depth], pick)
            sums[part] = piece.reshape(levels, tile_rows, lanes)
        blocks = []
        for parent_level in range(levels):
            level = inverse_of(level_index, parent_level, levels)
            totals = [
                sum(sums[part, level, pl.ds(a, third_rows, 3), :] for a in range(3))
                for part in range(third_cols // lanes)
            ]
            block = (jnp.concatenate(totals, axis=1) * (1.0 / 9.0)).astype(jnp.bfloat16)
            averaged[:, parent_level * third_cols : (parent_level + 1) * third_cols] = block
            blocks.append(block)
        table = cols[pl.ds(pl.multiple_of(group * third_cols, third_cols), third_cols), :]
        start = lax.rem(row * third_rows + shift, full_rows)
        project(blocks, table, rows[pl.ds(start, third_rows), :].astype(jnp.bfloat16))

    @pl.when(is_parent)
    def _():
        averaged[...] = jnp.zeros_like(averaged)
        cell = lax.broadcasted_iota(jnp.int32, (tile_rows, BASIS), 0)
        strip = lax.rem(row * tile_rows + cell - shift + full_rows, full_rows)
        weights = rows[pl.ds(pl.multiple_of(row * tile_rows, 8), tile_rows), :]
        weights = jnp.where(strip < full_rows // 3, 0.0, weights).astype(jnp.bfloat16)
        project([tile[level] for level in range(levels)], cols[...], weights)

    half = parity_of_device()
    keep[...] = coeffs[half]
    send[...] = coeffs[1 - half]
    for copy in later:
        copy.wait()
    period = 3 * full_rows
    child_start = lax.rem(3 * shift + row * tile_rows - 1 + period, period)
    start = jnp.where(is_parent, child_count + row * tile_rows, child_start)
    weights[...] = turn_rows[pl.ds(start, tile_rows), :]
    for pair in range(levels // 2):
        target[pair] = amplitude * jnp.concatenate(
            [driving[2 * pair], driving[2 * pair + 1]], axis=1
        )


def select_kernel(full_rows, third_rows, offset, first, second, out):
    tile_rows = out.shape[0]
    row = lax.axis_index("row")
    shape = (tile_rows, first.shape[0] + second.shape[0])
    cell = lax.broadcasted_iota(jnp.int32, shape, 0)
    wanted = lax.rem(row * tile_rows + cell - offset[0] + full_rows, full_rows)
    place = lax.broadcasted_iota(jnp.int32, shape, 1)
    held = (row ^ (place // third_rows)) * third_rows + place % third_rows
    pick = jnp.where(wanted == held, 1.0, 0.0).astype(jnp.bfloat16)
    strip = jnp.concatenate([first[...], second[...]], axis=0)
    out[...] = dot(pick, strip).astype(jnp.bfloat16)


def final_kernel(
    full_rows, groups, offset, level_index, rate, mine, other, tile, spread, weights, target,
    block_0, block_1, block_2, out_hbm, deficit, left, base, result, sems,
):
    levels, tile_rows, tile_cols = base.shape
    third_cols = tile_cols // 3
    group, row = lax.axis_index("grp"), lax.axis_index("row")
    is_parent = group == groups - 1
    half = parity_of_device()
    deficit[half] = target[half] - mine[...]
    deficit[1 - half] = target[1 - half] - other[...]
    is_left = lax.broadcasted_iota(jnp.int32, (tile_rows, 2 * BASIS), 1) < BASIS
    for pair in range(levels // 2):
        turned = jnp.dot(
            weights[...], deficit[pair], precision=lax.Precision.HIGHEST,
            preferred_element_type=jnp.float32,
        )
        for side in range(2):
            parent_level = 2 * pair + side
            high, low = split(turned * rate[parent_level])
            low = pltpu.roll(low.astype(jnp.float32), BASIS, 1).astype(jnp.bfloat16)
            here = is_left if side == 0 else ~is_left
            span = pl.ds(parent_level * tile_rows, tile_rows)
            left[span, : 2 * BASIS] = jnp.where(here, high, low)
            left[span, 2 * BASIS :] = jnp.where(here, high, jnp.zeros_like(high))
    increment = dot(left[...], spread[...])

    @pl.when(is_parent)
    def _():
        cell = lax.broadcasted_iota(jnp.int32, (tile_rows, third_cols), 0)
        strip = lax.rem(row * tile_rows + cell - offset[0] + full_rows, full_rows)
        covered = strip < full_rows // 3
        for level in range(levels):
            for third, block in enumerate((block_0, block_1, block_2)):
                span = slice(third * third_cols, (third + 1) * third_cols)
                arrived = block[:, level * third_cols : (level + 1) * third_cols]
                base[level, :, span] = jnp.where(
                    covered, arrived.astype(jnp.float32), tile[level, :, span].astype(jnp.float32)
                )

    @pl.when(jnp.logical_not(is_parent))
    def _():
        base[...] = tile[...].astype(jnp.float32)

    copies = []
    for parent_level in range(levels):
        level = jnp.where(is_parent, parent_level, inverse_of(level_index, parent_level, levels))
        rows = increment[parent_level * tile_rows : (parent_level + 1) * tile_rows]
        result[level] = (base[level] + rows).astype(jnp.bfloat16)
        copy = pltpu.make_async_copy(
            result.at[level], out_hbm.at[level], sems.at[parent_level]
        )
        copy.start()
        copies.append(copy)
    for copy in copies:
        copy.wait()


def per_device(sizes, fields, offset, level_index, nudge_rate, driving):
    groups, row_count, col_count = sizes
    tile_in = fields[0]
    levels, tile_rows, tile_cols = tile_in.shape
    third_rows, third_cols = tile_rows // 3, tile_cols // 3
    full_rows, full_cols = row_count * tile_rows, col_count * tile_cols
    f32, bf16 = jnp.float32, jnp.bfloat16

    cols = basis_table(3 * np.arange(full_cols), full_cols)
    cols_twice = np.concatenate([cols, cols], 1).reshape(col_count, tile_cols, 2 * BASIS)
    cols_twice = cols_twice.astype(bf16)
    parent_rows = basis_table(3 * np.arange(full_rows), full_rows)
    rounded = parent_rows.astype(bf16).astype(np.float32)
    rounded = np.concatenate([rounded, rounded[:third_rows]], 0)
    child_rows = basis_table(np.arange(3 * full_rows), full_rows)
    child_rows = np.concatenate([child_rows, child_rows[:tile_rows]], 0)
    child_cols = basis_table((np.arange(3 * full_cols) - 1) % (3 * full_cols), full_cols)
    spread_rows = np.concatenate([child_cols, cols], 0).reshape(-1, tile_cols, BASIS)
    spread_rows = spread_rows.transpose(0, 2, 1)
    spread_table = np.stack(halves(spread_rows), 1)
    amplitude = math.sqrt(full_rows * full_cols) / BASIS

    def mask_of(group_bits, row_bits, col_bits):
        return (group_bits * row_count + row_bits) * col_count + col_bits

    def exchange(value, mask):
        count = groups * row_count * col_count
        return lax.ppermute(value, AXES, [(i, i ^ mask) for i in range(count)])

    flip = mask_of(1, 0, 0)
    rounds = [mask_of(1 << k, 0, 0) ^ flip for k in range(1, groups.bit_length() - 1)]
    rounds += [mask_of(0, 0, 1 << k) ^ flip for k in range(col_count.bit_length() - 1)]
    rounds += [mask_of(0, 1 << k, 0) ^ flip for k in range(row_count.bit_length() - 1)]

    averaged, keep, send, tile, spread, weights, target = pl.pallas_call(
        functools.partial(first_kernel, full_rows, amplitude, groups, col_count),
        out_shape=(
            pltpu.VMEM((third_rows, levels * third_cols), bf16),
            pltpu.VMEM((BASIS, 2 * BASIS), f32),
            pltpu.VMEM((BASIS, 2 * BASIS), f32),
            pltpu.VMEM(tile_in.shape, bf16),
            pltpu.VMEM((4 * BASIS, tile_cols), bf16),
            pltpu.VMEM((tile_rows, BASIS), f32),
            pltpu.VMEM((levels // 2, BASIS, 2 * BASIS), f32),
        ),
        in_specs=[SMEM, SMEM] + [ANY] * 7,
        out_specs=(VMEM,) * 7,
        scratch_shapes=[
            pltpu.VMEM((tile_cols, 2 * BASIS), bf16),
            pltpu.VMEM(rounded.shape, f32),
            pltpu.VMEM((third_cols // 128, levels, tile_rows, 128), f32),
            pltpu.VMEM((levels // 2, BASIS, 2 * BASIS), f32),
            pltpu.VMEM((child_rows.shape[0] + parent_rows.shape[0], BASIS), f32),
            pltpu.VMEM(driving.shape, f32),
            pltpu.SemaphoreType.DMA((10,)),
        ],
        name="first",
    )(
        offset, level_index, tile_in, jnp.asarray(cols_twice), jnp.asarray(rounded),
        jnp.asarray(spread_table), jnp.asarray(child_rows), jnp.asarray(parent_rows), driving,
    )

    mine = keep + exchange(send, flip)
    for mask in rounds:
        mine = mine + exchange(mine, mask)
    other = exchange(mine, flip)

    strips = [averaged]
    for k in range(row_count.bit_length() - 1):
        held = strips[0] if k == 0 else jnp.concatenate(strips, 0)
        strips = [held, exchange(held, mask_of(0, 1 << k, 0))]
    selected = pl.pallas_call(
        functools.partial(select_kernel, full_rows, third_rows),
        out_shape=pltpu.VMEM((tile_rows, levels * third_cols), bf16),
        in_specs=[SMEM, VMEM, VMEM],
        out_specs=VMEM,
        name="select",
    )(offset, *(pltpu.with_memory_space_constraint(strip, pltpu.VMEM) for strip in strips))
    block_0 = exchange(selected, mask_of(3, 0, 0))
    block_2 = exchange(selected, mask_of(1, 0, 0))
    block_1 = exchange(block_0, mask_of(1, 0, 0))

    result = pl.pallas_call(
        functools.partial(final_kernel, full_rows, groups),
        out_shape=jax.ShapeDtypeStruct(tile_in.shape, bf16),
        in_specs=[SMEM, SMEM, SMEM] + [VMEM] * 9,
        out_specs=ANY,
        scratch_shapes=[
            pltpu.VMEM((levels // 2, BASIS, 2 * BASIS), f32),
            pltpu.VMEM((levels * tile_rows, 4 * BASIS), bf16),
            pltpu.VMEM(tile_in.shape, f32),
            pltpu.VMEM(tile_in.shape, bf16),
            pltpu.SemaphoreType.DMA((levels,)),
        ],
        name="final",
    )(
        offset, level_index, nudge_rate,
        *(
            pltpu.with_memory_space_constraint(value, pltpu.VMEM)
            for value in (mine, other, tile, spread, weights, target, block_0, block_1, block_2)
        ),
    )
    return result[None]


def solution(mesh):
    placed = (P("grp", None, "row", "col"), P(), P(), P(), P())
    sizes = tuple(mesh.shape[axis] for axis in AXES)
    return jax.shard_map(
        functools.partial(per_device, sizes),
        mesh=mesh,
        in_specs=placed,
        out_specs=P("grp", None, "row", "col"),
        check_vma=False,
    )
```

profile of v0, /device:TPU:0, one launch (start us, length us, event | category | flops | bytes accessed | tf_op | source)
XLA Modules:
  0.0 34.2 jit_solution(9373185214436660727)
XLA Ops:
  0.7 2.6 %first.1 = (bf16[16,1024]{1,0:T(8,128)(2,1)S(1)}, f32[64,128]{1,0:T(8,128)S(1)}, f32[64,128]{1,0:T(8,128)S(1)}, bf16[4,48,768]{2,1,0:T(8,128)(2,1)S(1)}, bf16[25...) custom-call(s32[1]{0:T(128)S(6)} %copy.12.offset, s32[4]{0:T(128)} %level_index.3, ...), custom_call_target="tpu_custom_call" | custom-call | tf_op jit(solution)/shard_map/first/pallas_call | solution.py:259
  3.3 3.1 %collective-permute-start.6 = (bf16[16,1024]{1,0:T(8,128)(2,1)S(1)}, bf16[16,1024]{1,0:T(8,128)(2,1)S(1)}, u32[]{:S(2)}, u32[]{:S(2)}) collective-permute-start(bf16[16,1024]{1,0:T(8,128)(2,1)S(1)} %get-tuple-element.18), channel_id=1, source_target_pairs={{0,2},{1,3},{2,0},{3,1},{4,6},{5,7},{6,4},{7,5},{8,10},{9,11},{10,... | collective-permute-start | bytes 98312 | tf_op jit(solution)/shard_map/ppermute | solution.py:252
  6.4 1.9 %collective-permute-done.6 = bf16[16,1024]{1,0:T(8,128)(2,1)S(1)} collective-permute-done((bf16[16,1024]{1,0:T(8,128)(2,1)S(1)}, bf16[16,1024]{1,0:T(8,128)(2,1)S(1)}, u32[]{:S(2)}, u32[]{:S(2)}) %collective-permute-start.6) | collective-permute-done | bytes 32800 | tf_op jit(solution)/shard_map/ppermute | solution.py:252
  8.3 3.0 %collective-permute-start.7 = (bf16[32,1024]{1,0:T(8,128)(2,1)S(1)}, bf16[32,1024]{1,0:T(8,128)(2,1)S(1)}, u32[]{:S(2)}, u32[]{:S(2)}) collective-permute-start(bf16[32,1024]{1,0:T(8,128)(2,1)S(1)} %constant_dynamic-update-slice_fusion.first), channel_id=1, source_target_pairs={{0,4},{1,5},{2,6},{3,7},{4,0},{5,1},{6,2},{7,3},{8,12},{9,13},{10,... | collective-permute-start | bytes 196616 | tf_op jit(solution)/shard_map/ppermute | solution.py:252
  11.3 0.0 collective-permute-start
  11.3 2.2 %collective-permute-done.7.second = bf16[32,1024]{1,0:T(8,128)(2,1)S(1)} collective-permute-done((bf16[32,1024]{1,0:T(8,128)(2,1)S(1)}, bf16[32,1024]{1,0:T(8,128)(2,1)S(1)}, u32[]{:S(2)}, u32[]{:S(2)}) %collective-permute-start.7) | collective-permute-done | bytes 65568 | tf_op jit(solution)/shard_map/ppermute | solution.py:252
  13.5 0.2 select.1
  13.7 0.1 collective-permute-start.8
  13.8 0.0 collective-permute-done
  13.8 1.8 %collective-permute-start.1 = (f32[64,128]{1,0:T(8,128)S(1)}, f32[64,128]{1,0:T(8,128)S(1)}, u32[]{:S(2)}, u32[]{:S(2)}) collective-permute-start(f32[64,128]{1,0:T(8,128)S(1)} %add.15), channel_id=1, source_target_pairs={{0,24},{1,25},{2,26},{3,27},{4,28},{5,29},{6,30},{7,31},{8,16},{9,... | collective-permute-start | bytes 98312 | tf_op jit(solution)/shard_map/ppermute | solution.py:252
  15.6 3.6 %collective-permute-done.1 = f32[64,128]{1,0:T(8,128)S(1)} collective-permute-done((f32[64,128]{1,0:T(8,128)S(1)}, f32[64,128]{1,0:T(8,128)S(1)}, u32[]{:S(2)}, u32[]{:S(2)}) %collective-permute-start.1) | collective-permute-done | bytes 32800 | tf_op jit(solution)/shard_map/ppermute | solution.py:252
  19.2 1.9 %collective-permute-start.2 = (f32[64,128]{1,0:T(8,128)S(1)}, f32[64,128]{1,0:T(8,128)S(1)}, u32[]{:S(2)}, u32[]{:S(2)}) collective-permute-start(f32[64,128]{1,0:T(8,128)S(1)} %add.16), channel_id=1, source_target_pairs={{0,9},{1,8},{2,11},{3,10},{4,13},{5,12},{6,15},{7,14},{8,1},{9,0},... | collective-permute-start | bytes 98312 | tf_op jit(solution)/shard_map/ppermute | solution.py:252
  21.1 1.6 %collective-permute-done.2 = f32[64,128]{1,0:T(8,128)S(1)} collective-permute-done((f32[64,128]{1,0:T(8,128)S(1)}, f32[64,128]{1,0:T(8,128)S(1)}, u32[]{:S(2)}, u32[]{:S(2)}) %collective-permute-start.2) | collective-permute-done | bytes 32800 | tf_op jit(solution)/shard_map/ppermute | solution.py:252
  22.7 1.9 %collective-permute-start.3 = (f32[64,128]{1,0:T(8,128)S(1)}, f32[64,128]{1,0:T(8,128)S(1)}, u32[]{:S(2)}, u32[]{:S(2)}) collective-permute-start(f32[64,128]{1,0:T(8,128)S(1)} %add.17), channel_id=1, source_target_pairs={{0,10},{1,11},{2,8},{3,9},{4,14},{5,15},{6,12},{7,13},{8,2},{9,3},... | collective-permute-start | bytes 98312 | tf_op jit(solution)/shard_map/ppermute | solution.py:252
  24.6 0.4 %collective-permute-start.10 = (bf16[48,1024]{1,0:T(8,128)(2,1)S(1)}, bf16[48,1024]{1,0:T(8,128)(2,1)S(1)}, u32[]{:S(2)}, u32[]{:S(2)}) collective-permute-start(bf16[48,1024]{1,0:T(8,128)(2,1)S(1)} %select.1), channel_id=1, source_target_pairs={{0,8},{1,9},{2,10},{3,11},{4,12},{5,13},{6,14},{7,15},{8,0},{9,1},... | collective-permute-start | bytes 294920 | tf_op jit(solution)/shard_map/ppermute | solution.py:252
  25.0 0.0 collective-permute-done.8.block_0
  25.0 0.1 collective-permute-start.9
  25.1 1.1 %collective-permute-done.3 = f32[64,128]{1,0:T(8,128)S(1)} collective-permute-done((f32[64,128]{1,0:T(8,128)S(1)}, f32[64,128]{1,0:T(8,128)S(1)}, u32[]{:S(2)}, u32[]{:S(2)}) %collective-permute-start.3) | collective-permute-done | bytes 32800 | tf_op jit(solution)/shard_map/ppermute | solution.py:252
  26.2 3.2 %collective-permute-start.4 = (f32[64,128]{1,0:T(8,128)S(1)}, f32[64,128]{1,0:T(8,128)S(1)}, u32[]{:S(2)}, u32[]{:S(2)}) collective-permute-start(f32[64,128]{1,0:T(8,128)S(1)} %add.18), channel_id=1, source_target_pairs={{0,12},{1,13},{2,14},{3,15},{4,8},{5,9},{6,10},{7,11},{8,4},{9,5},... | collective-permute-start | bytes 98312 | tf_op jit(solution)/shard_map/ppermute | solution.py:252
  29.4 1.6 %collective-permute-done.4 = f32[64,128]{1,0:T(8,128)S(1)} collective-permute-done((f32[64,128]{1,0:T(8,128)S(1)}, f32[64,128]{1,0:T(8,128)S(1)}, u32[]{:S(2)}, u32[]{:S(2)}) %collective-permute-start.4) | collective-permute-done | bytes 32800 | tf_op jit(solution)/shard_map/ppermute | solution.py:252
  31.0 0.1 collective-permute-start.5
  31.1 0.0 collective-permute-done.10.block_2
  31.1 1.1 %collective-permute-done.5.other = f32[64,128]{1,0:T(8,128)S(1)} collective-permute-done((f32[64,128]{1,0:T(8,128)S(1)}, f32[64,128]{1,0:T(8,128)S(1)}, u32[]{:S(2)}, u32[]{:S(2)}) %collective-permute-start.5) | collective-permute-done | bytes 32800 | tf_op jit(solution)/shard_map/ppermute | solution.py:252
  32.2 0.0 collective-permute-done.9.block_1
  32.2 2.0 %final.1 = bf16[4,48,768]{2,1,0:T(8,128)(2,1)} custom-call(s32[1]{0:T(128)S(6)} %copy.12.offset, s32[4]{0:T(128)} %level_index.3, f32[4]{0:T(128)} %rate.1, f32[64,128]{1,0:T(8,128)S(1)} %add.19.mine, f32[64,128]{1,0:T(8,128)S(1)} %collective-permute-done.5.other, bf16[4,48,768]{2,1,0:T(8,128)(2,1)S(1)} %get-tuple-element.14.tile, ...), custom_call_target="tpu_custom_call" | custom-call | tf_op jit(solution)/shard_map/final/pallas_call | solution.py:307
  (7 shorter events, 0.0 us)
Async XLA Ops:
  3.3 5.0 %collective-permute-start.6 = (bf16[16,1024]{1,0:T(8,128)(2,1)S(1)}, bf16[16,1024]{1,0:T(8,128)(2,1)S(1)}, u32[]{:S(2)}, u32[]{:S(2)}) collective-permute-start(bf16[16,1024]{1,0:T(8,128)(2,1)S(1)} %get-tuple-element.18), channel_id=1, source_target_pairs={{0,2},{1,3},{2,0},{3,1},{4,6},{5,7},{6,4},{7,5},{8,10},{9,11},{10,... | collective-permute-start | bytes 98312 | tf_op jit(solution)/shard_map/ppermute | solution.py:252
  8.3 5.3 %collective-permute-start.7 = (bf16[32,1024]{1,0:T(8,128)(2,1)S(1)}, bf16[32,1024]{1,0:T(8,128)(2,1)S(1)}, u32[]{:S(2)}, u32[]{:S(2)}) collective-permute-start(bf16[32,1024]{1,0:T(8,128)(2,1)S(1)} %constant_dynamic-update-slice_fusion.first), channel_id=1, source_target_pairs={{0,4},{1,5},{2,6},{3,7},{4,0},{5,1},{6,2},{7,3},{8,12},{9,13},{10,... | collective-permute-start | bytes 196616 | tf_op jit(solution)/shard_map/ppermute | solution.py:252
  11.3 2.5 %collective-permute-start = (f32[64,128]{1,0:T(8,128)S(1)}, f32[64,128]{1,0:T(8,128)S(1)}, u32[]{:S(2)}, u32[]{:S(2)}) collective-permute-start(f32[64,128]{1,0:T(8,128)S(1)} %get-tuple-element.13), channel_id=1, source_target_pairs={{0,8},{1,9},{2,10},{3,11},{4,12},{5,13},{6,14},{7,15},{8,0},{9,1},... | collective-permute-start | bytes 98312 | tf_op jit(solution)/shard_map/ppermute | solution.py:252
  13.7 11.2 %collective-permute-start.8 = (bf16[48,1024]{1,0:T(8,128)(2,1)S(1)}, bf16[48,1024]{1,0:T(8,128)(2,1)S(1)}, u32[]{:S(2)}, u32[]{:S(2)}) collective-permute-start(bf16[48,1024]{1,0:T(8,128)(2,1)S(1)} %select.1), channel_id=1, source_target_pairs={{0,24},{1,25},{2,26},{3,27},{4,28},{5,29},{6,30},{7,31},{8,16},{9,... | collective-permute-start | bytes 294920 | tf_op jit(solution)/shard_map/ppermute | solution.py:252
  13.8 5.4 %collective-permute-start.1 = (f32[64,128]{1,0:T(8,128)S(1)}, f32[64,128]{1,0:T(8,128)S(1)}, u32[]{:S(2)}, u32[]{:S(2)}) collective-permute-start(f32[64,128]{1,0:T(8,128)S(1)} %add.15), channel_id=1, source_target_pairs={{0,24},{1,25},{2,26},{3,27},{4,28},{5,29},{6,30},{7,31},{8,16},{9,... | collective-permute-start | bytes 98312 | tf_op jit(solution)/shard_map/ppermute | solution.py:252
  19.2 3.5 %collective-permute-start.2 = (f32[64,128]{1,0:T(8,128)S(1)}, f32[64,128]{1,0:T(8,128)S(1)}, u32[]{:S(2)}, u32[]{:S(2)}) collective-permute-start(f32[64,128]{1,0:T(8,128)S(1)} %add.16), channel_id=1, source_target_pairs={{0,9},{1,8},{2,11},{3,10},{4,13},{5,12},{6,15},{7,14},{8,1},{9,0},... | collective-permute-start | bytes 98312 | tf_op jit(solution)/shard_map/ppermute | solution.py:252
  22.7 3.5 %collective-permute-start.3 = (f32[64,128]{1,0:T(8,128)S(1)}, f32[64,128]{1,0:T(8,128)S(1)}, u32[]{:S(2)}, u32[]{:S(2)}) collective-permute-start(f32[64,128]{1,0:T(8,128)S(1)} %add.17), channel_id=1, source_target_pairs={{0,10},{1,11},{2,8},{3,9},{4,14},{5,15},{6,12},{7,13},{8,2},{9,3},... | collective-permute-start | bytes 98312 | tf_op jit(solution)/shard_map/ppermute | solution.py:252
  24.6 6.6 %collective-permute-start.10 = (bf16[48,1024]{1,0:T(8,128)(2,1)S(1)}, bf16[48,1024]{1,0:T(8,128)(2,1)S(1)}, u32[]{:S(2)}, u32[]{:S(2)}) collective-permute-start(bf16[48,1024]{1,0:T(8,128)(2,1)S(1)} %select.1), channel_id=1, source_target_pairs={{0,8},{1,9},{2,10},{3,11},{4,12},{5,13},{6,14},{7,15},{8,0},{9,1},... | collective-permute-start | bytes 294920 | tf_op jit(solution)/shard_map/ppermute | solution.py:252
  25.0 7.3 %collective-permute-start.9 = (bf16[48,1024]{1,0:T(8,128)(2,1)S(1)}, bf16[48,1024]{1,0:T(8,128)(2,1)S(1)}, u32[]{:S(2)}, u32[]{:S(2)}) collective-permute-start(bf16[48,1024]{1,0:T(8,128)(2,1)S(1)} %collective-permute-done.8.block_0), channel_id=1, source_target_pairs={{0,8},{1,9},{2,10},{3,11},{4,12},{5,13},{6,14},{7,15},{8,0},{9,1},... | collective-permute-start | bytes 294920 | tf_op jit(solution)/shard_map/ppermute | solution.py:252
  26.2 4.8 %collective-permute-start.4 = (f32[64,128]{1,0:T(8,128)S(1)}, f32[64,128]{1,0:T(8,128)S(1)}, u32[]{:S(2)}, u32[]{:S(2)}) collective-permute-start(f32[64,128]{1,0:T(8,128)S(1)} %add.18), channel_id=1, source_target_pairs={{0,12},{1,13},{2,14},{3,15},{4,8},{5,9},{6,10},{7,11},{8,4},{9,5},... | collective-permute-start | bytes 98312 | tf_op jit(solution)/shard_map/ppermute | solution.py:252
  31.0 1.2 %collective-permute-start.5 = (f32[64,128]{1,0:T(8,128)S(1)}, f32[64,128]{1,0:T(8,128)S(1)}, u32[]{:S(2)}, u32[]{:S(2)}) collective-permute-start(f32[64,128]{1,0:T(8,128)S(1)} %add.19.mine), channel_id=1, source_target_pairs={{0,8},{1,9},{2,10},{3,11},{4,12},{5,13},{6,14},{7,15},{8,0},{9,1},... | collective-permute-start | bytes 98312 | tf_op jit(solution)/shard_map/ppermute | solution.py:252
where the time goes:
time: 34.4 us; the launch traced here: 34.2 us
  starting transfers between devices  15.6 us (45%)
  waiting for transfers between devices  13.1 us (38%)
  Pallas kernels  4.72 us (14%)
  between operations  0.71 us (2%)
    ppermute x11, starting transfers between devices, exchange(): return lax.ppermute(value, AXES, [(i, i ^ mask) for i in range(count)])  15.6 us
    ppermute x11, waiting for transfers between devices, exchange(): return lax.ppermute(value, AXES, [(i, i ^ mask) for i in range(count)])  13.1 us
    pallas_call x1, Pallas kernels, per_device(): pl.pallas_call(functools.partial(first_kernel, full_rows, amplitude, grou...  2.59 us
    pallas_call x1, Pallas kernels, per_device(): pl.pallas_call(functools.partial(final_kernel, full_rows, groups), out_sh...  1.98 us
  transfers between devices with their start and end apart: 11, of which 7 were waited for; matrix products, arithmetic and copies ran while one was open for 0% of the time, Pallas kernels for 0%

commit v1 on v0

--- a/solution.py
+++ b/solution.py
@@ -15,6 +15,14 @@
 VMEM = pl.BlockSpec(memory_space=pltpu.VMEM)
 SMEM = pl.BlockSpec(memory_space=pltpu.SMEM)
 ANY = pl.BlockSpec(memory_space=pl.ANY)
+
+
+def in_vmem(value):
+    return pltpu.with_memory_space_constraint(value, pltpu.VMEM)
+
+
+def in_hbm(value):
+    return pltpu.with_memory_space_constraint(value, pltpu.HBM)
 
 
 def basis_table(positions, cell_count):
@@ -56,10 +64,10 @@
 
 
 def first_kernel(
-    full_rows, amplitude, groups, columns, offset, level_index, tile_hbm, cols_hbm, rows_hbm,
-    spread_hbm, child_rows_hbm, parent_rows_hbm, driving_hbm,
-    averaged, keep, send, tile, spread, weights, target,
-    cols, rows, sums, coeffs, turn_rows, driving, sems,
+    full_rows, amplitude, groups, columns, tile_hbm, cols_hbm, rows_hbm, offset_hbm, level_hbm,
+    rate_hbm, spread_hbm, child_rows_hbm, parent_rows_hbm, driving_hbm,
+    averaged, keep, send, tile, spread, weights, target, whole_out, rate,
+    cols, rows, sums, coeffs, turn_rows, driving, offset, level_index, sems,
 ):
     levels, tile_rows, tile_cols = tile.shape
     third_rows, third_cols = tile_rows // 3, tile_cols // 3
@@ -71,6 +79,8 @@
         pltpu.make_async_copy(tile_hbm, tile, sems.at[0]),
         pltpu.make_async_copy(cols_hbm.at[col], cols, sems.at[1]),
         pltpu.make_async_copy(rows_hbm, rows, sems.at[2]),
+        pltpu.make_async_copy(offset_hbm, offset, sems.at[10]),
+        pltpu.make_async_copy(level_hbm, level_index, sems.at[11]),
     ]
     later = [
         pltpu.make_async_copy(
@@ -85,10 +95,10 @@
             turn_rows.at[pl.ds(child_count, parent_rows_hbm.shape[0])],
             sems.at[9],
         ),
+        pltpu.make_async_copy(rate_hbm, rate, sems.at[12]),
     ]
     for copy in copies + later:
         copy.start()
-    shift = offset[0]
     lanes = sums.shape[-1]
     depth = 3 * lanes
     cell = lax.broadcasted_iota(jnp.int32, (depth, lanes), 0)
@@ -96,6 +106,7 @@
     pick = jnp.where((cell >= block) & (cell < block + 3), 1.0, 0.0).astype(jnp.bfloat16)
     for copy in copies:
         copy.wait()
+    shift = offset[0]
 
     def project(blocks, table, weights):
         left = lax.broadcasted_iota(jnp.int32, table.shape, 1) < BASIS
@@ -136,6 +147,10 @@
         weights = jnp.where(strip < full_rows // 3, 0.0, weights).astype(jnp.bfloat16)
         project([tile[level] for level in range(levels)], cols[...], weights)
 
+    whole_out[0] = shift
+    for parent_level in range(levels):
+        found = inverse_of(level_index, parent_level, levels)
+        whole_out[1 + parent_level] = jnp.where(is_parent, parent_level, found)
     half = parity_of_device()
     keep[...] = coeffs[half]
     send[...] = coeffs[1 - half]
@@ -165,59 +180,71 @@
 
 
 def final_kernel(
-    full_rows, groups, offset, level_index, rate, mine, other, tile, spread, weights, target,
-    block_0, block_1, block_2, out_hbm, deficit, left, base, result, sems,
+    full_rows, groups, own_half, whole, rate, *refs,
 ):
-    levels, tile_rows, tile_cols = base.shape
+    coeffs, tile, spread, weights, target, block_0, block_1, block_2 = refs[:8]
+    if own_half:
+        result, left, base = refs[8:]
+    else:
+        earlier, out_hbm, left, base, result, sems = refs[8:]
+    _, tile_rows, tile_cols = tile.shape
     third_cols = tile_cols // 3
     group, row = lax.axis_index("grp"), lax.axis_index("row")
     is_parent = group == groups - 1
     half = parity_of_device()
-    deficit[half] = target[half] - mine[...]
-    deficit[1 - half] = target[1 - half] - other[...]
+    pair = half if own_half else 1 - half
+    copies = []
+
+    def write(source, pair):
+        for side in range(2):
+            target_level = out_hbm.at[whole[1 + 2 * pair + side]]
+            copies.append(
+                pltpu.make_async_copy(source.at[side], target_level, sems.at[len(copies)])
+            )
+            copies[-1].start()
+
+    if not own_half:
+        write(earlier, half)
     is_left = lax.broadcasted_iota(jnp.int32, (tile_rows, 2 * BASIS), 1) < BASIS
-    for pair in range(levels // 2):
-        turned = jnp.dot(
-            weights[...], deficit[pair], precision=lax.Precision.HIGHEST,
-            preferred_element_type=jnp.float32,
-        )
-        for side in range(2):
-            parent_level = 2 * pair + side
-            high, low = split(turned * rate[parent_level])
-            low = pltpu.roll(low.astype(jnp.float32), BASIS, 1).astype(jnp.bfloat16)
-            here = is_left if side == 0 else ~is_left
-            span = pl.ds(parent_level * tile_rows, tile_rows)
-            left[span, : 2 * BASIS] = jnp.where(here, high, low)
-            left[span, 2 * BASIS :] = jnp.where(here, high, jnp.zeros_like(high))
+    turned = jnp.dot(
+        weights[...], target[pair] - coeffs[...], precision=lax.Precision.HIGHEST,
+        preferred_element_type=jnp.float32,
+    )
+    for side in range(2):
+        high, low = split(turned * rate[2 * pair + side])
+        low = pltpu.roll(low.astype(jnp.float32), BASIS, 1).astype(jnp.bfloat16)
+        here = is_left if side == 0 else ~is_left
+        span = pl.ds(side * tile_rows, tile_rows)
+        left[span, : 2 * BASIS] = jnp.where(here, high, low)
+        left[span, 2 * BASIS :] = jnp.where(here, high, jnp.zeros_like(high))
     increment = dot(left[...], spread[...])
 
     @pl.when(is_parent)
     def _():
         cell = lax.broadcasted_iota(jnp.int32, (tile_rows, third_cols), 0)
-        strip = lax.rem(row * tile_rows + cell - offset[0] + full_rows, full_rows)
+        strip = lax.rem(row * tile_rows + cell - whole[0] + full_rows, full_rows)
         covered = strip < full_rows // 3
-        for level in range(levels):
+        for side in range(2):
+            level = 2 * pair + side
             for third, block in enumerate((block_0, block_1, block_2)):
                 span = slice(third * third_cols, (third + 1) * third_cols)
-                arrived = block[:, level * third_cols : (level + 1) * third_cols]
-                base[level, :, span] = jnp.where(
+                arrived = block[:, pl.ds(pl.multiple_of(level * third_cols, 128), third_cols)]
+                base[side, :, span] = jnp.where(
                     covered, arrived.astype(jnp.float32), tile[level, :, span].astype(jnp.float32)
                 )
 
+    levels_out = [whole[1 + 2 * pair + side] for side in range(2)]
+
     @pl.when(jnp.logical_not(is_parent))
     def _():
-        base[...] = tile[...].astype(jnp.float32)
-
-    copies = []
-    for parent_level in range(levels):
-        level = jnp.where(is_parent, parent_level, inverse_of(level_index, parent_level, levels))
-        rows = increment[parent_level * tile_rows : (parent_level + 1) * tile_rows]
-        result[level] = (base[level] + rows).astype(jnp.bfloat16)
-        copy = pltpu.make_async_copy(
-            result.at[level], out_hbm.at[level], sems.at[parent_level]
-        )
-        copy.start()
-        copies.append(copy)
+        for side in range(2):
+            base[side] = tile[levels_out[side]].astype(jnp.float32)
+
+    for side in range(2):
+        rows = increment[side * tile_rows : (side + 1) * tile_rows]
+        result[side] = (base[side] + rows).astype(jnp.bfloat16)
+    if not own_half:
+        write(result, pair)
     for copy in copies:
         copy.wait()
 
@@ -247,16 +274,23 @@
     def mask_of(group_bits, row_bits, col_bits):
         return (group_bits * row_count + row_bits) * col_count + col_bits
 
-    def exchange(value, mask):
+    def exchange(value, masks):
+        even, odd = masks if isinstance(masks, tuple) else (masks, masks)
         count = groups * row_count * col_count
-        return lax.ppermute(value, AXES, [(i, i ^ mask) for i in range(count)])
+        pairs = [(i, i ^ (odd if i.bit_count() % 2 else even)) for i in range(count)]
+        return lax.ppermute(value, AXES, pairs)
 
     flip = mask_of(1, 0, 0)
-    rounds = [mask_of(1 << k, 0, 0) ^ flip for k in range(1, groups.bit_length() - 1)]
-    rounds += [mask_of(0, 0, 1 << k) ^ flip for k in range(col_count.bit_length() - 1)]
-    rounds += [mask_of(0, 1 << k, 0) ^ flip for k in range(row_count.bit_length() - 1)]
-
-    averaged, keep, send, tile, spread, weights, target = pl.pallas_call(
+    across = [mask_of(1 << k, 0, 0) ^ flip for k in range(1, groups.bit_length() - 1)]
+    across += [mask_of(0, 0, 1 << k) ^ flip for k in range(col_count.bit_length() - 1)]
+    along = [mask_of(0, 1 << k, 0) ^ flip for k in range(row_count.bit_length() - 1)]
+    rounds = []
+    while across and along:
+        one, two = across.pop(0), along.pop(0)
+        rounds += [(one, two), (two, one)]
+    rounds += [(mask, mask) for mask in across + along]
+
+    averaged, keep, send, tile, spread, weights, target, whole, rate = pl.pallas_call(
         functools.partial(first_kernel, full_rows, amplitude, groups, col_count),
         out_shape=(
             pltpu.VMEM((third_rows, levels * third_cols), bf16),
@@ -266,9 +300,11 @@
             pltpu.VMEM((4 * BASIS, tile_cols), bf16),
             pltpu.VMEM((tile_rows, BASIS), f32),
             pltpu.VMEM((levels // 2, BASIS, 2 * BASIS), f32),
+            pltpu.SMEM((1 + levels,), jnp.int32),
+            pltpu.SMEM((levels,), f32),
         ),
-        in_specs=[SMEM, SMEM] + [ANY] * 7,
-        out_specs=(VMEM,) * 7,
+        in_specs=[ANY] * 10,
+        out_specs=(VMEM,) * 7 + (SMEM, SMEM),
         scratch_shapes=[
             pltpu.VMEM((tile_cols, 2 * BASIS), bf16),
             pltpu.VMEM(rounded.shape, f32),
@@ -276,17 +312,20 @@
             pltpu.VMEM((levels // 2, BASIS, 2 * BASIS), f32),
             pltpu.VMEM((child_rows.shape[0] + parent_rows.shape[0], BASIS), f32),
             pltpu.VMEM(driving.shape, f32),
-            pltpu.SemaphoreType.DMA((10,)),
+            pltpu.SMEM((1,), jnp.int32),
+            pltpu.SMEM((levels,), jnp.int32),
+            pltpu.SemaphoreType.DMA((13,)),
         ],
         name="first",
     )(
-        offset, level_index, tile_in, jnp.asarray(cols_twice), jnp.asarray(rounded),
+        tile_in, jnp.asarray(cols_twice), jnp.asarray(rounded), offset,
+        in_hbm(level_index), in_hbm(nudge_rate),
         jnp.asarray(spread_table), jnp.asarray(child_rows), jnp.asarray(parent_rows), driving,
     )
 
     mine = keep + exchange(send, flip)
-    for mask in rounds:
-        mine = mine + exchange(mine, mask)
+    for masks in rounds:
+        mine = mine + exchange(mine, masks)
     other = exchange(mine, flip)
 
     strips = [averaged]
@@ -299,32 +338,30 @@
         in_specs=[SMEM, VMEM, VMEM],
         out_specs=VMEM,
         name="select",
-    )(offset, *(pltpu.with_memory_space_constraint(strip, pltpu.VMEM) for strip in strips))
+    )(whole, *(in_vmem(strip) for strip in strips))
     block_0 = exchange(selected, mask_of(3, 0, 0))
     block_2 = exchange(selected, mask_of(1, 0, 0))
     block_1 = exchange(block_0, mask_of(1, 0, 0))
 
-    result = pl.pallas_call(
-        functools.partial(final_kernel, full_rows, groups),
-        out_shape=jax.ShapeDtypeStruct(tile_in.shape, bf16),
-        in_specs=[SMEM, SMEM, SMEM] + [VMEM] * 9,
-        out_specs=ANY,
-        scratch_shapes=[
-            pltpu.VMEM((levels // 2, BASIS, 2 * BASIS), f32),
-            pltpu.VMEM((levels * tile_rows, 4 * BASIS), bf16),
-            pltpu.VMEM(tile_in.shape, f32),
-            pltpu.VMEM(tile_in.shape, bf16),
-            pltpu.SemaphoreType.DMA((levels,)),
-        ],
-        name="final",
-    )(
-        offset, level_index, nudge_rate,
-        *(
-            pltpu.with_memory_space_constraint(value, pltpu.VMEM)
-            for value in (mine, other, tile, spread, weights, target, block_0, block_1, block_2)
-        ),
-    )
-    return result[None]
+    def finish(coeffs, earlier):
+        two_levels = (2, tile_rows, tile_cols)
+        scratch = [pltpu.VMEM((2 * tile_rows, 4 * BASIS), bf16), pltpu.VMEM(two_levels, f32)]
+        if earlier:
+            scratch += [pltpu.VMEM(two_levels, bf16), pltpu.SemaphoreType.DMA((4,))]
+            out_shape, out_spec = jax.ShapeDtypeStruct(tile_in.shape, bf16), ANY
+        else:
+            out_shape, out_spec = pltpu.VMEM(two_levels, bf16), VMEM
+        values = (coeffs, tile, spread, weights, target, block_0, block_1, block_2, *earlier)
+        return pl.pallas_call(
+            functools.partial(final_kernel, full_rows, groups, not earlier),
+            out_shape=out_shape,
+            in_specs=[SMEM, SMEM] + [VMEM] * len(values),
+            out_specs=out_spec,
+            scratch_shapes=scratch,
+        )(whole, rate, *(in_vmem(value) for value in values))
+
+    partly = finish(mine, ())
+    return finish(other, (partly,))[None]
 
 
 def solution(mesh):

time: 34.4 us -> 32.6 us (0.948)
  starting transfers between devices: 15.6 us -> 14.5 us
  Pallas kernels: 4.72 us -> 3.82 us
    ppermute x11, starting transfers between devices: 15.6 us -> 14.5 us  [exchange(): return lax.ppermute(value, AXES, pairs)]
    pallas_call x1, Pallas kernels: 2.59 us -> 1.99 us  [per_device(): pl.pallas_call(functools.partial(first_kernel, full_rows, amplitude, grou...]
    pallas_call x1 -> x2, Pallas kernels: 1.98 us -> 1.68 us  [finish(): pl.pallas_call(functools.partial(final_kernel, full_rows, groups, not ear...]
  transfers between devices with their start and end apart: 11 -> 11, of which waited for: 7 -> 7; matrix products, arithmetic and copies ran while one was open for 0% -> 0% of each run, Pallas kernels for 0% -> 2%
where the time goes in v1:
time: 32.6 us; the launch traced here: 32.4 us
  starting transfers between devices  14.5 us (44%)
  waiting for transfers between devices  13.4 us (41%)
  Pallas kernels  3.82 us (12%)
  between operations  0.73 us (2%)
    ppermute x11, starting transfers between devices, exchange(): return lax.ppermute(value, AXES, pairs)  14.5 us
    ppermute x11, waiting for transfers between devices, exchange(): return lax.ppermute(value, AXES, pairs)  13.4 us
    pallas_call x1, Pallas kernels, per_device(): pl.pallas_call(functools.partial(first_kernel, full_rows, amplitude, grou...  1.99 us
    pallas_call x2, Pallas kernels, finish(): pl.pallas_call(functools.partial(final_kernel, full_rows, groups, not ear...  1.68 us
  transfers between devices with their start and end apart: 11, of which 7 were waited for; matrix products, arithmetic and copies ran while one was open for 0% of the time, Pallas kernels for 2%

profile of v1, /device:TPU:0, one launch (start us, length us, event | category | flops | bytes accessed | tf_op | source)
XLA Modules:
  0.0 32.4 jit_solution(509687970484438832)
XLA Ops:
  0.7 2.0 %first.1 = (bf16[16,1024]{1,0:T(8,128)(2,1)S(1)}, f32[64,128]{1,0:T(8,128)S(1)}, f32[64,128]{1,0:T(8,128)S(1)}, bf16[4,48,768]{2,1,0:T(8,128)(2,1)S(1)}, bf16[25...) custom-call(bf16[4,48,768]{2,1,0:T(8,128)(2,1)} %bitcast.2, ...), custom_call_target="tpu_custom_call" | custom-call | tf_op jit(solution)/shard_map/first/pallas_call | solution.py:293
  2.6 3.1 %collective-permute-start.6 = (bf16[16,1024]{1,0:T(8,128)(2,1)S(1)}, bf16[16,1024]{1,0:T(8,128)(2,1)S(1)}, u32[]{:S(2)}, u32[]{:S(2)}) collective-permute-start(bf16[16,1024]{1,0:T(8,128)(2,1)S(1)} %get-tuple-element.22), channel_id=1, source_target_pairs={{0,2},{1,3},{2,0},{3,1},{4,6},{5,7},{6,4},{7,5},{8,10},{9,11},{10,... | collective-permute-start | bytes 98312 | tf_op jit(solution)/shard_map/ppermute | solution.py:281
  5.8 1.9 %collective-permute-done.6 = bf16[16,1024]{1,0:T(8,128)(2,1)S(1)} collective-permute-done((bf16[16,1024]{1,0:T(8,128)(2,1)S(1)}, bf16[16,1024]{1,0:T(8,128)(2,1)S(1)}, u32[]{:S(2)}, u32[]{:S(2)}) %collective-permute-start.6) | collective-permute-done | bytes 32800 | tf_op jit(solution)/shard_map/ppermute | solution.py:281
  7.7 3.0 %collective-permute-start.7 = (bf16[32,1024]{1,0:T(8,128)(2,1)S(1)}, bf16[32,1024]{1,0:T(8,128)(2,1)S(1)}, u32[]{:S(2)}, u32[]{:S(2)}) collective-permute-start(bf16[32,1024]{1,0:T(8,128)(2,1)S(1)} %constant_dynamic-update-slice_fusion.first), channel_id=1, source_target_pairs={{0,4},{1,5},{2,6},{3,7},{4,0},{5,1},{6,2},{7,3},{8,12},{9,13},{10,... | collective-permute-start | bytes 196616 | tf_op jit(solution)/shard_map/ppermute | solution.py:281
  10.7 0.0 collective-permute-start
  10.7 2.2 %collective-permute-done.7.second = bf16[32,1024]{1,0:T(8,128)(2,1)S(1)} collective-permute-done((bf16[32,1024]{1,0:T(8,128)(2,1)S(1)}, bf16[32,1024]{1,0:T(8,128)(2,1)S(1)}, u32[]{:S(2)}, u32[]{:S(2)}) %collective-permute-start.7) | collective-permute-done | bytes 65568 | tf_op jit(solution)/shard_map/ppermute | solution.py:281
  12.9 0.2 select.1
  13.1 0.1 collective-permute-start.8
  13.2 0.0 collective-permute-done
  13.2 1.8 %collective-permute-start.1 = (f32[64,128]{1,0:T(8,128)S(1)}, f32[64,128]{1,0:T(8,128)S(1)}, u32[]{:S(2)}, u32[]{:S(2)}) collective-permute-start(f32[64,128]{1,0:T(8,128)S(1)} %add.15), channel_id=1, source_target_pairs={{0,24},{1,11},{2,8},{3,27},{4,14},{5,29},{6,30},{7,13},{8,2},{9,17... | collective-permute-start | bytes 98312 | tf_op jit(solution)/shard_map/ppermute | solution.py:281
  15.0 3.6 %collective-permute-done.1 = f32[64,128]{1,0:T(8,128)S(1)} collective-permute-done((f32[64,128]{1,0:T(8,128)S(1)}, f32[64,128]{1,0:T(8,128)S(1)}, u32[]{:S(2)}, u32[]{:S(2)}) %collective-permute-start.1) | collective-permute-done | bytes 32800 | tf_op jit(solution)/shard_map/ppermute | solution.py:281
  18.6 1.3 %collective-permute-start.2 = (f32[64,128]{1,0:T(8,128)S(1)}, f32[64,128]{1,0:T(8,128)S(1)}, u32[]{:S(2)}, u32[]{:S(2)}) collective-permute-start(f32[64,128]{1,0:T(8,128)S(1)} %add.16), channel_id=1, source_target_pairs={{0,10},{1,25},{2,26},{3,9},{4,28},{5,15},{6,12},{7,31},{8,16},{9,3... | collective-permute-start | bytes 98312 | tf_op jit(solution)/shard_map/ppermute | solution.py:281
  19.9 0.0 collective-permute-start.10
  20.0 0.0 collective-permute-done.8.refs_5_
  20.0 0.5 %collective-permute-start.9 = (bf16[48,1024]{1,0:T(8,128)(2,1)S(1)}, bf16[48,1024]{1,0:T(8,128)(2,1)S(1)}, u32[]{:S(2)}, u32[]{:S(2)}) collective-permute-start(bf16[48,1024]{1,0:T(8,128)(2,1)S(1)} %collective-permute-done.8.refs_5_), channel_id=1, source_target_pairs={{0,8},{1,9},{2,10},{3,11},{4,12},{5,13},{6,14},{7,15},{8,0},{9,1},... | collective-permute-start | bytes 294920 | tf_op jit(solution)/shard_map/ppermute | solution.py:281
  20.5 1.5 %collective-permute-done.2 = f32[64,128]{1,0:T(8,128)S(1)} collective-permute-done((f32[64,128]{1,0:T(8,128)S(1)}, f32[64,128]{1,0:T(8,128)S(1)}, u32[]{:S(2)}, u32[]{:S(2)}) %collective-permute-start.2) | collective-permute-done | bytes 32800 | tf_op jit(solution)/shard_map/ppermute | solution.py:281
  21.9 1.4 %collective-permute-start.3 = (f32[64,128]{1,0:T(8,128)S(1)}, f32[64,128]{1,0:T(8,128)S(1)}, u32[]{:S(2)}, u32[]{:S(2)}) collective-permute-start(f32[64,128]{1,0:T(8,128)S(1)} %add.17), channel_id=1, source_target_pairs={{0,9},{1,13},{2,14},{3,10},{4,8},{5,12},{6,15},{7,11},{8,4},{9,0},... | collective-permute-start | bytes 98312 | tf_op jit(solution)/shard_map/ppermute | solution.py:281
  23.4 1.9 %collective-permute-done.3 = f32[64,128]{1,0:T(8,128)S(1)} collective-permute-done((f32[64,128]{1,0:T(8,128)S(1)}, f32[64,128]{1,0:T(8,128)S(1)}, u32[]{:S(2)}, u32[]{:S(2)}) %collective-permute-start.3) | collective-permute-done | bytes 32800 | tf_op jit(solution)/shard_map/ppermute | solution.py:281
  25.3 3.2 %collective-permute-start.4 = (f32[64,128]{1,0:T(8,128)S(1)}, f32[64,128]{1,0:T(8,128)S(1)}, u32[]{:S(2)}, u32[]{:S(2)}) collective-permute-start(f32[64,128]{1,0:T(8,128)S(1)} %add.18), channel_id=1, source_target_pairs={{0,12},{1,8},{2,11},{3,15},{4,13},{5,9},{6,10},{7,14},{8,1},{9,5},... | collective-permute-start | bytes 98312 | tf_op jit(solution)/shard_map/ppermute | solution.py:281
  28.5 1.6 %collective-permute-done.4 = f32[64,128]{1,0:T(8,128)S(1)} collective-permute-done((f32[64,128]{1,0:T(8,128)S(1)}, f32[64,128]{1,0:T(8,128)S(1)}, u32[]{:S(2)}, u32[]{:S(2)}) %collective-permute-start.4) | collective-permute-done | bytes 32800 | tf_op jit(solution)/shard_map/ppermute | solution.py:281
  30.1 0.0 collective-permute-start.5
  30.1 0.0 collective-permute-done.10.refs_7_
  30.1 0.0 collective-permute-done.9.refs_6_
  30.1 0.5 %shard_map.100.refs_8_ = bf16[2,48,768]{2,1,0:T(8,128)(2,1)S(1)} custom-call(s32[5]{0:T(128)S(4)} %get-tuple-element.14.offset.whole, f32[4]{0:T(128)S(4)} %get-tuple-element.15.rate, f32[64,128]{1,0:T(8,128)S(1)} %add.19.refs_0_, bf16[4,48,768]{2,1,0:T(8,128)(2,1)S(1)} %get-tuple-element.18.refs_1_, bf16[256,768]{1,0:T(8,128)(2,1)S(1)} %get-tuple-element.19.refs_2_, ...), custom_call_target="tpu_custom_call" | custom-call | tf_op jit(solution)/shard_map/pallas_call | solution.py:355
  30.6 0.7 %collective-permute-done.5.refs_0_ = f32[64,128]{1,0:T(8,128)S(1)} collective-permute-done((f32[64,128]{1,0:T(8,128)S(1)}, f32[64,128]{1,0:T(8,128)S(1)}, u32[]{:S(2)}, u32[]{:S(2)}) %collective-permute-start.5) | collective-permute-done | bytes 32800 | tf_op jit(solution)/shard_map/ppermute | solution.py:281
  31.3 1.2 %shard_map.101 = bf16[4,48,768]{2,1,0:T(8,128)(2,1)} custom-call(s32[5]{0:T(128)S(4)} %get-tuple-element.14.offset.whole, f32[4]{0:T(128)S(4)} %get-tuple-element.15.rate, f32[64,128]{1,0:T(8,128)S(1)} %collective-permute-done.5.refs_0_, bf16[4,48,768]{2,1,0:T(8,128)(2,1)S(1)} %get-tuple-element.18.refs_1_, bf16[256,768]{1,0:T(8,128)(2,1)S(1)} %get-tuple-element.19.refs_2_, ...), custom_call_target="tpu_custom_call" | custom-call | tf_op jit(solution)/shard_map/pallas_call | solution.py:355
  (7 shorter events, 0.0 us)
Async XLA Ops:
  2.6 5.0 %collective-permute-start.6 = (bf16[16,1024]{1,0:T(8,128)(2,1)S(1)}, bf16[16,1024]{1,0:T(8,128)(2,1)S(1)}, u32[]{:S(2)}, u32[]{:S(2)}) collective-permute-start(bf16[16,1024]{1,0:T(8,128)(2,1)S(1)} %get-tuple-element.22), channel_id=1, source_target_pairs={{0,2},{1,3},{2,0},{3,1},{4,6},{5,7},{6,4},{7,5},{8,10},{9,11},{10,... | collective-permute-start | bytes 98312 | tf_op jit(solution)/shard_map/ppermute | solution.py:281
  7.7 5.3 %collective-permute-start.7 = (bf16[32,1024]{1,0:T(8,128)(2,1)S(1)}, bf16[32,1024]{1,0:T(8,128)(2,1)S(1)}, u32[]{:S(2)}, u32[]{:S(2)}) collective-permute-start(bf16[32,1024]{1,0:T(8,128)(2,1)S(1)} %constant_dynamic-update-slice_fusion.first), channel_id=1, source_target_pairs={{0,4},{1,5},{2,6},{3,7},{4,0},{5,1},{6,2},{7,3},{8,12},{9,13},{10,... | collective-permute-start | bytes 196616 | tf_op jit(solution)/shard_map/ppermute | solution.py:281
  10.7 2.5 %collective-permute-start = (f32[64,128]{1,0:T(8,128)S(1)}, f32[64,128]{1,0:T(8,128)S(1)}, u32[]{:S(2)}, u32[]{:S(2)}) collective-permute-start(f32[64,128]{1,0:T(8,128)S(1)} %get-tuple-element.17), channel_id=1, source_target_pairs={{0,8},{1,9},{2,10},{3,11},{4,12},{5,13},{6,14},{7,15},{8,0},{9,1},... | collective-permute-start | bytes 98312 | tf_op jit(solution)/shard_map/ppermute | solution.py:281
  13.1 6.9 %collective-permute-start.8 = (bf16[48,1024]{1,0:T(8,128)(2,1)S(1)}, bf16[48,1024]{1,0:T(8,128)(2,1)S(1)}, u32[]{:S(2)}, u32[]{:S(2)}) collective-permute-start(bf16[48,1024]{1,0:T(8,128)(2,1)S(1)} %select.1), channel_id=1, source_target_pairs={{0,24},{1,25},{2,26},{3,27},{4,28},{5,29},{6,30},{7,31},{8,16},{9,... | collective-permute-start | bytes 294920 | tf_op jit(solution)/shard_map/ppermute | solution.py:281
  13.2 5.4 %collective-permute-start.1 = (f32[64,128]{1,0:T(8,128)S(1)}, f32[64,128]{1,0:T(8,128)S(1)}, u32[]{:S(2)}, u32[]{:S(2)}) collective-permute-start(f32[64,128]{1,0:T(8,128)S(1)} %add.15), channel_id=1, source_target_pairs={{0,24},{1,11},{2,8},{3,27},{4,14},{5,29},{6,30},{7,13},{8,2},{9,17... | collective-permute-start | bytes 98312 | tf_op jit(solution)/shard_map/ppermute | solution.py:281
  18.6 3.3 %collective-permute-start.2 = (f32[64,128]{1,0:T(8,128)S(1)}, f32[64,128]{1,0:T(8,128)S(1)}, u32[]{:S(2)}, u32[]{:S(2)}) collective-permute-start(f32[64,128]{1,0:T(8,128)S(1)} %add.16), channel_id=1, source_target_pairs={{0,10},{1,25},{2,26},{3,9},{4,28},{5,15},{6,12},{7,31},{8,16},{9,3... | collective-permute-start | bytes 98312 | tf_op jit(solution)/shard_map/ppermute | solution.py:281
  19.9 10.1 %collective-permute-start.10 = (bf16[48,1024]{1,0:T(8,128)(2,1)S(1)}, bf16[48,1024]{1,0:T(8,128)(2,1)S(1)}, u32[]{:S(2)}, u32[]{:S(2)}) collective-permute-start(bf16[48,1024]{1,0:T(8,128)(2,1)S(1)} %select.1), channel_id=1, source_target_pairs={{0,8},{1,9},{2,10},{3,11},{4,12},{5,13},{6,14},{7,15},{8,0},{9,1},... | collective-permute-start | bytes 294920 | tf_op jit(solution)/shard_map/ppermute | solution.py:281
  20.0 10.1 %collective-permute-start.9 = (bf16[48,1024]{1,0:T(8,128)(2,1)S(1)}, bf16[48,1024]{1,0:T(8,128)(2,1)S(1)}, u32[]{:S(2)}, u32[]{:S(2)}) collective-permute-start(bf16[48,1024]{1,0:T(8,128)(2,1)S(1)} %collective-permute-done.8.refs_5_), channel_id=1, source_target_pairs={{0,8},{1,9},{2,10},{3,11},{4,12},{5,13},{6,14},{7,15},{8,0},{9,1},... | collective-permute-start | bytes 294920 | tf_op jit(solution)/shard_map/ppermute | solution.py:281
  21.9 3.3 %collective-permute-start.3 = (f32[64,128]{1,0:T(8,128)S(1)}, f32[64,128]{1,0:T(8,128)S(1)}, u32[]{:S(2)}, u32[]{:S(2)}) collective-permute-start(f32[64,128]{1,0:T(8,128)S(1)} %add.17), channel_id=1, source_target_pairs={{0,9},{1,13},{2,14},{3,10},{4,8},{5,12},{6,15},{7,11},{8,4},{9,0},... | collective-permute-start | bytes 98312 | tf_op jit(solution)/shard_map/ppermute | solution.py:281
  25.3 4.8 %collective-permute-start.4 = (f32[64,128]{1,0:T(8,128)S(1)}, f32[64,128]{1,0:T(8,128)S(1)}, u32[]{:S(2)}, u32[]{:S(2)}) collective-permute-start(f32[64,128]{1,0:T(8,128)S(1)} %add.18), channel_id=1, source_target_pairs={{0,12},{1,8},{2,11},{3,15},{4,13},{5,9},{6,10},{7,14},{8,1},{9,5},... | collective-permute-start | bytes 98312 | tf_op jit(solution)/shard_map/ppermute | solution.py:281
  30.1 1.2 %collective-permute-start.5 = (f32[64,128]{1,0:T(8,128)S(1)}, f32[64,128]{1,0:T(8,128)S(1)}, u32[]{:S(2)}, u32[]{:S(2)}) collective-permute-start(f32[64,128]{1,0:T(8,128)S(1)} %add.19.refs_0_), channel_id=1, source_target_pairs={{0,8},{1,9},{2,10},{3,11},{4,12},{5,13},{6,14},{7,15},{8,0},{9,1},... | collective-permute-start | bytes 98312 | tf_op jit(solution)/shard_map/ppermute | solution.py:281

commit v2 on v1

v2 whole, which is shorter than its diff:
```python
import functools
import math

import jax
import jax.numpy as jnp
import numpy as np
from jax import lax
from jax.experimental import pallas as pl
from jax.experimental.pallas import tpu as pltpu
from jax.sharding import PartitionSpec as P

MAX_WAVE = 32
BASIS = 2 * MAX_WAVE
AXES = ("grp", "row", "col")
VMEM = pl.BlockSpec(memory_space=pltpu.VMEM)
SMEM = pl.BlockSpec(memory_space=pltpu.SMEM)
ANY = pl.BlockSpec(memory_space=pl.ANY)


def in_vmem(value):
    return pltpu.with_memory_space_constraint(value, pltpu.VMEM)


def in_hbm(value):
    return pltpu.with_memory_space_constraint(value, pltpu.HBM)


def basis_table(positions, cell_count):
    period = 3 * cell_count
    orders = np.arange(1, MAX_WAVE + 1)
    angles = (np.asarray(positions)[:, None] * orders % period) * (2.0 * math.pi / period)
    scale = math.sqrt(2.0 / cell_count)
    constant = np.full((len(positions), 1), 1.0 / math.sqrt(cell_count))
    table = np.concatenate([constant, scale * np.cos(angles), scale * np.sin(angles[:, :-1])], 1)
    return table.astype(np.float32)


def halves(table):
    high = table.astype(jnp.bfloat16)
    return high, (table - high.astype(np.float32)).astype(jnp.bfloat16)


def split(value):
    high = value.astype(jnp.bfloat16)
    return high, (value - high.astype(jnp.float32)).astype(jnp.bfloat16)


def dot(a, b, contract=((1,), (0,))):
    return lax.dot_general(a, b, (contract, ((), ())), preferred_element_type=jnp.float32)


def parity_of_device():
    bits = lax.axis_index("grp") ^ lax.axis_index("row") ^ lax.axis_index("col")
    for shift in (8, 4, 2, 1):
        bits = bits ^ (bits >> shift)
    return bits & 1


def inverse_of(level_ref, parent_level, levels):
    found = jnp.int32(0)
    for level in range(levels):
        found = found + jnp.where(level_ref[level] == parent_level, level, 0)
    return found


def first_kernel(
    groups, columns, tile_hbm, cols_hbm, level_hbm, rate_hbm, rows_hbm, spread_hbm,
    turns_hbm, driving_hbm,
    averaged, keep, send, tile, spread, target, rows, turns, places, rate,
    cols, sums, projected, driving, level_index, sems,
):
    levels, tile_rows, tile_cols = tile.shape
    third_rows, third_cols = tile_rows // 3, tile_cols // 3
    group, _, col = (lax.axis_index(a) for a in AXES)
    is_parent = group == groups - 1
    slot = jnp.where(is_parent, (groups - 1) * columns + col, col * (groups - 1) + group)
    copies = [
        pltpu.make_async_copy(tile_hbm, tile, sems.at[0]),
        pltpu.make_async_copy(cols_hbm.at[col], cols, sems.at[1]),
        pltpu.make_async_copy(level_hbm, level_index, sems.at[2]),
    ]
    later = [
        pltpu.make_async_copy(
            spread_hbm.at[slot, part // 2], spread.at[pl.ds(part * BASIS, BASIS)], sems.at[3 + part]
        )
        for part in range(4)
    ] + [
        pltpu.make_async_copy(driving_hbm, driving, sems.at[7]),
        pltpu.make_async_copy(turns_hbm, turns, sems.at[8]),
        pltpu.make_async_copy(rows_hbm, rows, sems.at[9]),
        pltpu.make_async_copy(rate_hbm, rate, sems.at[10]),
    ]
    for copy in copies + later:
        copy.start()
    lanes = sums.shape[-1]
    depth = 3 * lanes
    cell = lax.broadcasted_iota(jnp.int32, (depth, lanes), 0)
    block = 3 * lax.broadcasted_iota(jnp.int32, (depth, lanes), 1)
    pick = jnp.where((cell >= block) & (cell < block + 3), 1.0, 0.0).astype(jnp.bfloat16)
    for copy in copies:
        copy.wait()

    def project(blocks, table):
        left = lax.broadcasted_iota(jnp.int32, table.shape, 1) < BASIS
        zero = jnp.zeros_like(table)
        first, second = jnp.where(left, table, zero), jnp.where(left, zero, table)
        for pair in range(levels // 2):
            span = pl.ds(0, blocks[0].shape[0])
            projected[pair, span] = dot(blocks[2 * pair], first) + dot(blocks[2 * pair + 1], second)

    @pl.when(jnp.logical_not(is_parent))
    def _():
        flat = tile[...].reshape(levels * tile_rows, tile_cols)
        for part in range(third_cols // lanes):
            piece = dot(flat[:, part * depth : (part + 1) * depth], pick)
            sums[part] = piece.reshape(levels, tile_rows, lanes)
        blocks = []
        for parent_level in range(levels):
            level = inverse_of(level_index, parent_level, levels)
            totals = [
                sum(sums[part, level, pl.ds(a, third_rows, 3), :] for a in range(3))
                for part in range(third_cols // lanes)
            ]
            block = (jnp.concatenate(totals, axis=1) * (1.0 / 9.0)).astype(jnp.bfloat16)
            averaged[:, parent_level * third_cols : (parent_level + 1) * third_cols] = block
            blocks.append(block)
        projected[...] = jnp.zeros_like(projected)
        table = cols[pl.ds(pl.multiple_of(group * third_cols, third_cols), third_cols), :]
        project(blocks, table)

    @pl.when(is_parent)
    def _():
        averaged[...] = jnp.zeros_like(averaged)
        project([tile[level] for level in range(levels)], cols[...])

    half = parity_of_device()
    keep[...] = projected[half]
    send[...] = projected[1 - half]
    for parent_level in range(levels):
        found = inverse_of(level_index, parent_level, levels)
        places[parent_level] = jnp.where(is_parent, parent_level, found)
    for copy in later:
        copy.wait()
    for pair in range(levels // 2):
        target[pair] = jnp.concatenate([driving[2 * pair], driving[2 * pair + 1]], axis=1)


def coeffs_kernel(full_rows, groups, offset, mine, partner, rows, out):
    tile_rows = mine.shape[0]
    group, row = lax.axis_index("grp"), lax.axis_index("row")
    shift = offset[0]
    cell = lax.broadcasted_iota(jnp.int32, (tile_rows, BASIS), 0)
    strip = lax.rem(row * tile_rows + cell - shift + full_rows, full_rows)
    strip_start = lax.rem(row * (tile_rows // 3) + shift, full_rows)

    def weights(is_parent):
        start = jnp.where(is_parent, row * tile_rows, strip_start)
        counted = jnp.where(is_parent, strip - full_rows // 3, tile_rows // 3 - 1 - cell) >= 0
        return jnp.where(counted, rows[pl.ds(start, tile_rows), :], 0.0).astype(jnp.bfloat16)

    table = jnp.concatenate([weights(group == groups - 1), weights((group ^ 1) == groups - 1)], 0)
    high, low = split(jnp.concatenate([mine[...], partner[...]], axis=0))
    out[...] = dot(table, high, ((0,), (0,))) + dot(table, low, ((0,), (0,)))


def select_kernel(full_rows, groups, exchanges, offset, first, second, turns, out, weights):
    tile_rows = out.shape[0]
    third_rows = tile_rows // 3
    row = lax.axis_index("row")
    is_parent = lax.axis_index("grp") == groups - 1
    shape = (tile_rows, first.shape[0] + second.shape[0])
    cell = lax.broadcasted_iota(jnp.int32, shape, 0)
    wanted = lax.rem(row * tile_rows + cell - offset[0] + full_rows, full_rows)
    place = lax.broadcasted_iota(jnp.int32, shape, 1)
    block = place // third_rows
    source = jnp.zeros_like(block)
    for step in range(exchanges):
        source = source + ((block >> step) & 1) * (1 << (exchanges - 1 - step))
    held = (row ^ source) * third_rows + place % third_rows
    pick = jnp.where(wanted == held, 1.0, 0.0).astype(jnp.bfloat16)
    strip = jnp.concatenate([first[...], second[...]], axis=0)
    out[...] = dot(pick, strip).astype(jnp.bfloat16)
    period = 3 * full_rows
    child_start = lax.rem(3 * offset[0] + row * tile_rows - 1 + period, period)
    start = jnp.where(is_parent, period + tile_rows + row * tile_rows, child_start)
    weights[...] = turns[pl.ds(start, tile_rows), :]


def final_kernel(
    full_rows, groups, amplitude, own_half, offset, places, rate, *refs,
):
    coeffs, tile, spread, weights, target, block_0, block_1, block_2 = refs[:8]
    if own_half:
        result, left, base = refs[8:]
    else:
        earlier, out_hbm, left, base, result, sems = refs[8:]
    _, tile_rows, tile_cols = tile.shape
    third_cols = tile_cols // 3
    group, row = lax.axis_index("grp"), lax.axis_index("row")
    is_parent = group == groups - 1
    half = parity_of_device()
    pair = half if own_half else 1 - half
    copies = []

    def write(source, pair):
        for side in range(2):
            target_level = out_hbm.at[places[2 * pair + side]]
            copies.append(
                pltpu.make_async_copy(source.at[side], target_level, sems.at[len(copies)])
            )
            copies[-1].start()

    if not own_half:
        write(earlier, half)
    is_left = lax.broadcasted_iota(jnp.int32, (tile_rows, 2 * BASIS), 1) < BASIS
    turned = jnp.dot(
        weights[...], amplitude * target[pair] - coeffs[...], precision=lax.Precision.HIGHEST,
        preferred_element_type=jnp.float32,
    )
    for side in range(2):
        high, low = split(turned * rate[2 * pair + side])
        low = pltpu.roll(low.astype(jnp.float32), BASIS, 1).astype(jnp.bfloat16)
        here = is_left if side == 0 else ~is_left
        span = pl.ds(side * tile_rows, tile_rows)
        left[span, : 2 * BASIS] = jnp.where(here, high, low)
        left[span, 2 * BASIS :] = jnp.where(here, high, jnp.zeros_like(high))
    increment = dot(left[...], spread[...])

    @pl.when(is_parent)
    def _():
        cell = lax.broadcasted_iota(jnp.int32, (tile_rows, third_cols), 0)
        strip = lax.rem(row * tile_rows + cell - offset[0] + full_rows, full_rows)
        covered = strip < full_rows // 3
        for side in range(2):
            level = 2 * pair + side
            for third, block in enumerate((block_0, block_1, block_2)):
                span = slice(third * third_cols, (third + 1) * third_cols)
                arrived = block[:, pl.ds(pl.multiple_of(level * third_cols, 128), third_cols)]
                base[side, :, span] = jnp.where(
                    covered, arrived.astype(jnp.float32), tile[level, :, span].astype(jnp.float32)
                )

    levels_out = [places[2 * pair + side] for side in range(2)]

    @pl.when(jnp.logical_not(is_parent))
    def _():
        for side in range(2):
            base[side] = tile[levels_out[side]].astype(jnp.float32)

    for side in range(2):
        rows = increment[side * tile_rows : (side + 1) * tile_rows]
        result[side] = (base[side] + rows).astype(jnp.bfloat16)
    if not own_half:
        write(result, pair)
    for copy in copies:
        copy.wait()


def per_device(sizes, fields, offset, level_index, nudge_rate, driving):
    groups, row_count, col_count = sizes
    tile_in = fields[0]
    levels, tile_rows, tile_cols = tile_in.shape
    third_rows, third_cols = tile_rows // 3, tile_cols // 3
    full_rows, full_cols = row_count * tile_rows, col_count * tile_cols
    f32, bf16 = jnp.float32, jnp.bfloat16

    cols = basis_table(3 * np.arange(full_cols), full_cols)
    cols_twice = np.concatenate([cols, cols], 1).reshape(col_count, tile_cols, 2 * BASIS)
    cols_twice = cols_twice.astype(bf16)
    parent_rows = basis_table(3 * np.arange(full_rows), full_rows)
    rounded = parent_rows.astype(bf16).astype(np.float32)
    rounded = np.concatenate([rounded, rounded[:tile_rows]], 0)
    child_rows = basis_table(np.arange(3 * full_rows), full_rows)
    turns = np.concatenate([child_rows, child_rows[:tile_rows], parent_rows], 0)
    child_cols = basis_table((np.arange(3 * full_cols) - 1) % (3 * full_cols), full_cols)
    spread_rows = np.concatenate([child_cols, cols], 0).reshape(-1, tile_cols, BASIS)
    spread_rows = spread_rows.transpose(0, 2, 1)
    spread_table = np.stack(halves(spread_rows), 1)
    amplitude = math.sqrt(full_rows * full_cols) / BASIS

    def mask_of(group_bits, row_bits, col_bits):
        return (group_bits * row_count + row_bits) * col_count + col_bits

    def exchange(value, mask):
        count = groups * row_count * col_count
        return lax.ppermute(value, AXES, [(i, i ^ mask) for i in range(count)])

    flip = mask_of(1, 0, 0)
    across = [mask_of(1 << k, 0, 0) ^ flip for k in range(1, groups.bit_length() - 1)]
    across += [mask_of(0, 0, 1 << k) ^ flip for k in range(col_count.bit_length() - 1)]
    row_bits = [1 << k for k in reversed(range(row_count.bit_length() - 1))]
    along = [mask_of(0, bit, 0) ^ flip for bit in row_bits]
    rounds = across + along[::-1]

    averaged, keep, send, tile, spread, target, rows, turns, places, rate = pl.pallas_call(
        functools.partial(first_kernel, groups, col_count),
        out_shape=(
            pltpu.VMEM((third_rows, levels * third_cols), bf16),
            pltpu.VMEM((tile_rows, 2 * BASIS), f32),
            pltpu.VMEM((tile_rows, 2 * BASIS), f32),
            pltpu.VMEM(tile_in.shape, bf16),
            pltpu.VMEM((4 * BASIS, tile_cols), bf16),
            pltpu.VMEM((levels // 2, BASIS, 2 * BASIS), f32),
            pltpu.VMEM(rounded.shape, f32),
            pltpu.VMEM(turns.shape, f32),
            pltpu.SMEM((levels,), jnp.int32),
            pltpu.SMEM((levels,), f32),
        ),
        in_specs=[ANY] * 8,
        out_specs=(VMEM,) * 8 + (SMEM, SMEM),
        scratch_shapes=[
            pltpu.VMEM((tile_cols, 2 * BASIS), bf16),
            pltpu.VMEM((third_cols // 128, levels, tile_rows, 128), f32),
            pltpu.VMEM((levels // 2, tile_rows, 2 * BASIS), f32),
            pltpu.VMEM(driving.shape, f32),
            pltpu.SMEM((levels,), jnp.int32),
            pltpu.SemaphoreType.DMA((11,)),
        ],
        name="first",
    )(
        tile_in, jnp.asarray(cols_twice), in_hbm(level_index), in_hbm(nudge_rate),
        jnp.asarray(rounded), jnp.asarray(spread_table), jnp.asarray(turns), driving,
    )

    partner = exchange(send, flip)
    mine = pl.pallas_call(
        functools.partial(coeffs_kernel, full_rows, groups),
        out_shape=pltpu.VMEM((BASIS, 2 * BASIS), f32),
        in_specs=[SMEM, VMEM, VMEM, VMEM],
        out_specs=VMEM,
        name="coeffs",
    )(offset, in_vmem(keep), in_vmem(partner), in_vmem(rows))
    for mask in rounds:
        mine = mine + exchange(mine, mask)
    other = exchange(mine, flip)

    strips = [averaged]
    for step, bit in enumerate(row_bits):
        held = strips[0] if step == 0 else jnp.concatenate(strips, 0)
        strips = [held, exchange(held, mask_of(0, bit, 0))]
    selected, weights = pl.pallas_call(
        functools.partial(select_kernel, full_rows, groups, len(row_bits)),
        out_shape=(
            pltpu.VMEM((tile_rows, levels * third_cols), bf16),
            pltpu.VMEM((tile_rows, BASIS), f32),
        ),
        in_specs=[SMEM, VMEM, VMEM, VMEM],
        out_specs=(VMEM, VMEM),
        name="select",
    )(offset, *(in_vmem(value) for value in (*strips, turns)))
    block_0 = exchange(selected, mask_of(3, 0, 0))
    block_2 = exchange(selected, mask_of(1, 0, 0))
    block_1 = exchange(block_0, mask_of(1, 0, 0))

    def finish(coeffs, earlier):
        two_levels = (2, tile_rows, tile_cols)
        scratch = [pltpu.VMEM((2 * tile_rows, 4 * BASIS), bf16), pltpu.VMEM(two_levels, f32)]
        if earlier:
            scratch += [pltpu.VMEM(two_levels, bf16), pltpu.SemaphoreType.DMA((4,))]
            out_shape, out_spec = jax.ShapeDtypeStruct(tile_in.shape, bf16), ANY
        else:
            out_shape, out_spec = pltpu.VMEM(two_levels, bf16), VMEM
        values = (coeffs, tile, spread, weights, target, block_0, block_1, block_2, *earlier)
        return pl.pallas_call(
            functools.partial(final_kernel, full_rows, groups, amplitude, not earlier),
            out_shape=out_shape,
            in_specs=[SMEM] * 3 + [VMEM] * len(values),
            out_specs=out_spec,
            scratch_shapes=scratch,
        )(offset, places, rate, *(in_vmem(value) for value in values))

    partly = finish(mine, ())
    return finish(other, (partly,))[None]


def solution(mesh):
    placed = (P("grp", None, "row", "col"), P(), P(), P(), P())
    sizes = tuple(mesh.shape[axis] for axis in AXES)
    return jax.shard_map(
        functools.partial(per_device, sizes),
        mesh=mesh,
        in_specs=placed,
        out_specs=P("grp", None, "row", "col"),
        check_vma=False,
    )
```

time: 32.6 us -> 32.1 us (0.985)
  starting transfers between devices: 14.5 us -> 13.9 us
  waiting for transfers between devices: 13.4 us -> 13.8 us
    ppermute x11, starting transfers between devices: 14.5 us -> 13.9 us  [exchange(): return lax.ppermute(value, AXES, [(i, i ^ mask) for i in range(count)])]
    ppermute x11, waiting for transfers between devices: 13.4 us -> 13.8 us  [exchange(): return lax.ppermute(value, AXES, [(i, i ^ mask) for i in range(count)])]
    pallas_call x4 -> x5, Pallas kernels: 3.82 us -> 3.64 us  [the longest x2 1.67 us: finish(): pl.pallas_call(functools.partial(final_kernel, full_rows, groups, amplitu...]
  transfers between devices with their start and end apart: 11 -> 11, of which waited for: 7 -> 8; matrix products, arithmetic and copies ran while one was open for 0% -> 0% of each run, Pallas kernels for 2% -> 2%
where the time goes in v2:
time: 32.1 us; the launch traced here: 32 us
  starting transfers between devices  13.9 us (43%)
  waiting for transfers between devices  13.8 us (43%)
  Pallas kernels  3.64 us (11%)
  between operations  0.69 us (2%)
    ppermute x11, starting transfers between devices, exchange(): return lax.ppermute(value, AXES, [(i, i ^ mask) for i in range(count)])  13.9 us
    ppermute x11, waiting for transfers between devices, exchange(): return lax.ppermute(value, AXES, [(i, i ^ mask) for i in range(count)])  13.8 us
    pallas_call x2, Pallas kernels, finish(): pl.pallas_call(functools.partial(final_kernel, full_rows, groups, amplitu...  1.67 us
    pallas_call x1, Pallas kernels, per_device(): pl.pallas_call(functools.partial(first_kernel, groups, col_count), out_sh...  1.61 us
  transfers between devices with their start and end apart: 11, of which 8 were waited for; matrix products, arithmetic and copies ran while one was open for 0% of the time, Pallas kernels for 2%

profile of v2, /device:TPU:0, one launch (start us, length us, event | category | flops | bytes accessed | tf_op | source)
XLA Modules:
  0.0 32.0 jit_solution(11832524068867221355)
XLA Ops:
  0.0 1.6 %first.1 = (bf16[16,1024]{1,0:T(8,128)(2,1)S(1)}, f32[48,128]{1,0:T(8,128)S(1)}, f32[48,128]{1,0:T(8,128)S(1)}, bf16[4,48,768]{2,1,0:T(8,128)(2,1)S(1)}, bf16[25...) custom-call(bf16[4,48,768]{2,1,0:T(8,128)(2,1)} %bitcast.2, ...), custom_call_target="tpu_custom_call" | custom-call | tf_op jit(solution)/shard_map/first/pallas_call | solution.py:295
  1.6 4.1 %collective-permute-start.6 = (bf16[16,1024]{1,0:T(8,128)(2,1)S(1)}, bf16[16,1024]{1,0:T(8,128)(2,1)S(1)}, u32[]{:S(2)}, u32[]{:S(2)}) collective-permute-start(bf16[16,1024]{1,0:T(8,128)(2,1)S(1)} %get-tuple-element.24), channel_id=1, source_target_pairs={{0,4},{1,5},{2,6},{3,7},{4,0},{5,1},{6,2},{7,3},{8,12},{9,13},{10,... | collective-permute-start | bytes 98312 | tf_op jit(solution)/shard_map/ppermute | solution.py:286
  5.8 2.2 %collective-permute-done.6 = bf16[16,1024]{1,0:T(8,128)(2,1)S(1)} collective-permute-done((bf16[16,1024]{1,0:T(8,128)(2,1)S(1)}, bf16[16,1024]{1,0:T(8,128)(2,1)S(1)}, u32[]{:S(2)}, u32[]{:S(2)}) %collective-permute-start.6) | collective-permute-done | bytes 32800 | tf_op jit(solution)/shard_map/ppermute | solution.py:286
  8.0 1.6 %collective-permute-start.7 = (bf16[32,1024]{1,0:T(8,128)(2,1)S(1)}, bf16[32,1024]{1,0:T(8,128)(2,1)S(1)}, u32[]{:S(2)}, u32[]{:S(2)}) collective-permute-start(bf16[32,1024]{1,0:T(8,128)(2,1)S(1)} %constant_dynamic-update-slice_fusion.first), channel_id=1, source_target_pairs={{0,2},{1,3},{2,0},{3,1},{4,6},{5,7},{6,4},{7,5},{8,10},{9,11},{10,... | collective-permute-start | bytes 196616 | tf_op jit(solution)/shard_map/ppermute | solution.py:286
  10.2 2.1 %collective-permute-done.7.second = bf16[32,1024]{1,0:T(8,128)(2,1)S(1)} collective-permute-done((bf16[32,1024]{1,0:T(8,128)(2,1)S(1)}, bf16[32,1024]{1,0:T(8,128)(2,1)S(1)}, u32[]{:S(2)}, u32[]{:S(2)}) %collective-permute-start.7) | collective-permute-done | bytes 65568 | tf_op jit(solution)/shard_map/ppermute | solution.py:286
  12.3 0.2 select.1
  12.4 0.1 collective-permute-start.8
  12.5 1.8 %collective-permute-start = (f32[48,128]{1,0:T(8,128)S(1)}, f32[48,128]{1,0:T(8,128)S(1)}, u32[]{:S(2)}, u32[]{:S(2)}) collective-permute-start(f32[48,128]{1,0:T(8,128)S(1)} %get-tuple-element.20), channel_id=1, source_target_pairs={{0,8},{1,9},{2,10},{3,11},{4,12},{5,13},{6,14},{7,15},{8,0},{9,1},... | collective-permute-start | bytes 73736 | tf_op jit(solution)/shard_map/ppermute | solution.py:286
  14.3 0.8 %collective-permute-done.partner = f32[48,128]{1,0:T(8,128)S(1)} collective-permute-done((f32[48,128]{1,0:T(8,128)S(1)}, f32[48,128]{1,0:T(8,128)S(1)}, u32[]{:S(2)}, u32[]{:S(2)}) %collective-permute-start) | collective-permute-done | bytes 24608 | tf_op jit(solution)/shard_map/ppermute | solution.py:286
  15.1 0.2 coeffs.1
  15.3 0.3 collective-permute-start.1
  15.6 3.0 %collective-permute-done.1 = f32[64,128]{1,0:T(8,128)S(1)} collective-permute-done((f32[64,128]{1,0:T(8,128)S(1)}, f32[64,128]{1,0:T(8,128)S(1)}, u32[]{:S(2)}, u32[]{:S(2)}) %collective-permute-start.1) | collective-permute-done | bytes 32800 | tf_op jit(solution)/shard_map/ppermute | solution.py:286
  18.7 1.5 %collective-permute-start.2 = (f32[64,128]{1,0:T(8,128)S(1)}, f32[64,128]{1,0:T(8,128)S(1)}, u32[]{:S(2)}, u32[]{:S(2)}) collective-permute-start(f32[64,128]{1,0:T(8,128)S(1)} %add.12), channel_id=1, source_target_pairs={{0,9},{1,8},{2,11},{3,10},{4,13},{5,12},{6,15},{7,14},{8,1},{9,0},... | collective-permute-start | bytes 98312 | tf_op jit(solution)/shard_map/ppermute | solution.py:286
  20.1 0.2 collective-permute-start.10
  20.3 0.0 collective-permute-done.8.refs_5_
  20.3 0.3 %collective-permute-start.9 = (bf16[48,1024]{1,0:T(8,128)(2,1)S(1)}, bf16[48,1024]{1,0:T(8,128)(2,1)S(1)}, u32[]{:S(2)}, u32[]{:S(2)}) collective-permute-start(bf16[48,1024]{1,0:T(8,128)(2,1)S(1)} %collective-permute-done.8.refs_5_), channel_id=1, source_target_pairs={{0,8},{1,9},{2,10},{3,11},{4,12},{5,13},{6,14},{7,15},{8,0},{9,1},... | collective-permute-start | bytes 294920 | tf_op jit(solution)/shard_map/ppermute | solution.py:286
  20.7 1.4 %collective-permute-done.2 = f32[64,128]{1,0:T(8,128)S(1)} collective-permute-done((f32[64,128]{1,0:T(8,128)S(1)}, f32[64,128]{1,0:T(8,128)S(1)}, u32[]{:S(2)}, u32[]{:S(2)}) %collective-permute-start.2) | collective-permute-done | bytes 32800 | tf_op jit(solution)/shard_map/ppermute | solution.py:286
  22.0 1.3 %collective-permute-start.3 = (f32[64,128]{1,0:T(8,128)S(1)}, f32[64,128]{1,0:T(8,128)S(1)}, u32[]{:S(2)}, u32[]{:S(2)}) collective-permute-start(f32[64,128]{1,0:T(8,128)S(1)} %add.13), channel_id=1, source_target_pairs={{0,10},{1,11},{2,8},{3,9},{4,14},{5,15},{6,12},{7,13},{8,2},{9,3},... | collective-permute-start | bytes 98312 | tf_op jit(solution)/shard_map/ppermute | solution.py:286
  23.4 2.0 %collective-permute-done.3 = f32[64,128]{1,0:T(8,128)S(1)} collective-permute-done((f32[64,128]{1,0:T(8,128)S(1)}, f32[64,128]{1,0:T(8,128)S(1)}, u32[]{:S(2)}, u32[]{:S(2)}) %collective-permute-start.3) | collective-permute-done | bytes 32800 | tf_op jit(solution)/shard_map/ppermute | solution.py:286
  25.4 2.4 %collective-permute-start.4 = (f32[64,128]{1,0:T(8,128)S(1)}, f32[64,128]{1,0:T(8,128)S(1)}, u32[]{:S(2)}, u32[]{:S(2)}) collective-permute-start(f32[64,128]{1,0:T(8,128)S(1)} %add.14), channel_id=1, source_target_pairs={{0,12},{1,13},{2,14},{3,15},{4,8},{5,9},{6,10},{7,11},{8,4},{9,5},... | collective-permute-start | bytes 98312 | tf_op jit(solution)/shard_map/ppermute | solution.py:286
  27.7 1.9 %collective-permute-done.4 = f32[64,128]{1,0:T(8,128)S(1)} collective-permute-done((f32[64,128]{1,0:T(8,128)S(1)}, f32[64,128]{1,0:T(8,128)S(1)}, u32[]{:S(2)}, u32[]{:S(2)}) %collective-permute-start.4) | collective-permute-done | bytes 32800 | tf_op jit(solution)/shard_map/ppermute | solution.py:286
  29.6 0.3 %collective-permute-start.5 = (f32[64,128]{1,0:T(8,128)S(1)}, f32[64,128]{1,0:T(8,128)S(1)}, u32[]{:S(2)}, u32[]{:S(2)}) collective-permute-start(f32[64,128]{1,0:T(8,128)S(1)} %add.15.refs_0_), channel_id=1, source_target_pairs={{0,8},{1,9},{2,10},{3,11},{4,12},{5,13},{6,14},{7,15},{8,0},{9,1},... | collective-permute-start | bytes 98312 | tf_op jit(solution)/shard_map/ppermute | solution.py:286
  30.0 0.0 collective-permute-done.10.refs_7_
  30.0 0.0 collective-permute-done.9.refs_6_
  30.0 0.5 %shard_map.91.refs_8_ = bf16[2,48,768]{2,1,0:T(8,128)(2,1)S(1)} custom-call(s32[1]{0:T(128)S(6)} %copy.11.offset, s32[4]{0:T(128)S(4)} %get-tuple-element.17.places, f32[4]{0:T(128)S(4)} %get-tuple-element.18.rate, f32[64,128]{1,0:T(8,128)S(1)} %add.15.refs_0_, bf16[4,48,768]{2,1,0:T(8,128)(2,1)S(1)} %get-tuple-element.22.refs_1_, ...), custom_call_target="tpu_custom_call" | custom-call | tf_op jit(solution)/shard_map/pallas_call | solution.py:364
  30.5 0.4 %collective-permute-done.5.refs_0_ = f32[64,128]{1,0:T(8,128)S(1)} collective-permute-done((f32[64,128]{1,0:T(8,128)S(1)}, f32[64,128]{1,0:T(8,128)S(1)}, u32[]{:S(2)}, u32[]{:S(2)}) %collective-permute-start.5) | collective-permute-done | bytes 32800 | tf_op jit(solution)/shard_map/ppermute | solution.py:286
  30.8 1.2 %shard_map.92 = bf16[4,48,768]{2,1,0:T(8,128)(2,1)} custom-call(s32[1]{0:T(128)S(6)} %copy.11.offset, s32[4]{0:T(128)S(4)} %get-tuple-element.17.places, f32[4]{0:T(128)S(4)} %get-tuple-element.18.rate, f32[64,128]{1,0:T(8,128)S(1)} %collective-permute-done.5.refs_0_, bf16[4,48,768]{2,1,0:T(8,128)(2,1)S(1)} %get-tuple-element.22.refs_1_, ...), custom_call_target="tpu_custom_call" | custom-call | tf_op jit(solution)/shard_map/pallas_call | solution.py:364
  (6 shorter events, 0.0 us)
Async XLA Ops:
  1.6 6.4 %collective-permute-start.6 = (bf16[16,1024]{1,0:T(8,128)(2,1)S(1)}, bf16[16,1024]{1,0:T(8,128)(2,1)S(1)}, u32[]{:S(2)}, u32[]{:S(2)}) collective-permute-start(bf16[16,1024]{1,0:T(8,128)(2,1)S(1)} %get-tuple-element.24), channel_id=1, source_target_pairs={{0,4},{1,5},{2,6},{3,7},{4,0},{5,1},{6,2},{7,3},{8,12},{9,13},{10,... | collective-permute-start | bytes 98312 | tf_op jit(solution)/shard_map/ppermute | solution.py:286
  8.0 4.3 %collective-permute-start.7 = (bf16[32,1024]{1,0:T(8,128)(2,1)S(1)}, bf16[32,1024]{1,0:T(8,128)(2,1)S(1)}, u32[]{:S(2)}, u32[]{:S(2)}) collective-permute-start(bf16[32,1024]{1,0:T(8,128)(2,1)S(1)} %constant_dynamic-update-slice_fusion.first), channel_id=1, source_target_pairs={{0,2},{1,3},{2,0},{3,1},{4,6},{5,7},{6,4},{7,5},{8,10},{9,11},{10,... | collective-permute-start | bytes 196616 | tf_op jit(solution)/shard_map/ppermute | solution.py:286
  12.4 7.9 %collective-permute-start.8 = (bf16[48,1024]{1,0:T(8,128)(2,1)S(1)}, bf16[48,1024]{1,0:T(8,128)(2,1)S(1)}, u32[]{:S(2)}, u32[]{:S(2)}) collective-permute-start(bf16[48,1024]{1,0:T(8,128)(2,1)S(1)} %get-tuple-element.28), channel_id=1, source_target_pairs={{0,24},{1,25},{2,26},{3,27},{4,28},{5,29},{6,30},{7,31},{8,16},{9,... | collective-permute-start | bytes 294920 | tf_op jit(solution)/shard_map/ppermute | solution.py:286
  12.5 2.6 %collective-permute-start = (f32[48,128]{1,0:T(8,128)S(1)}, f32[48,128]{1,0:T(8,128)S(1)}, u32[]{:S(2)}, u32[]{:S(2)}) collective-permute-start(f32[48,128]{1,0:T(8,128)S(1)} %get-tuple-element.20), channel_id=1, source_target_pairs={{0,8},{1,9},{2,10},{3,11},{4,12},{5,13},{6,14},{7,15},{8,0},{9,1},... | collective-permute-start | bytes 73736 | tf_op jit(solution)/shard_map/ppermute | solution.py:286
  15.3 3.3 %collective-permute-start.1 = (f32[64,128]{1,0:T(8,128)S(1)}, f32[64,128]{1,0:T(8,128)S(1)}, u32[]{:S(2)}, u32[]{:S(2)}) collective-permute-start(f32[64,128]{1,0:T(8,128)S(1)} %coeffs.1), channel_id=1, source_target_pairs={{0,24},{1,25},{2,26},{3,27},{4,28},{5,29},{6,30},{7,31},{8,16},{9,... | collective-permute-start | bytes 98312 | tf_op jit(solution)/shard_map/ppermute | solution.py:286
  18.7 3.3 %collective-permute-start.2 = (f32[64,128]{1,0:T(8,128)S(1)}, f32[64,128]{1,0:T(8,128)S(1)}, u32[]{:S(2)}, u32[]{:S(2)}) collective-permute-start(f32[64,128]{1,0:T(8,128)S(1)} %add.12), channel_id=1, source_target_pairs={{0,9},{1,8},{2,11},{3,10},{4,13},{5,12},{6,15},{7,14},{8,1},{9,0},... | collective-permute-start | bytes 98312 | tf_op jit(solution)/shard_map/ppermute | solution.py:286
  20.1 9.8 %collective-permute-start.10 = (bf16[48,1024]{1,0:T(8,128)(2,1)S(1)}, bf16[48,1024]{1,0:T(8,128)(2,1)S(1)}, u32[]{:S(2)}, u32[]{:S(2)}) collective-permute-start(bf16[48,1024]{1,0:T(8,128)(2,1)S(1)} %get-tuple-element.28), channel_id=1, source_target_pairs={{0,8},{1,9},{2,10},{3,11},{4,12},{5,13},{6,14},{7,15},{8,0},{9,1},... | collective-permute-start | bytes 294920 | tf_op jit(solution)/shard_map/ppermute | solution.py:286
  20.3 9.7 %collective-permute-start.9 = (bf16[48,1024]{1,0:T(8,128)(2,1)S(1)}, bf16[48,1024]{1,0:T(8,128)(2,1)S(1)}, u32[]{:S(2)}, u32[]{:S(2)}) collective-permute-start(bf16[48,1024]{1,0:T(8,128)(2,1)S(1)} %collective-permute-done.8.refs_5_), channel_id=1, source_target_pairs={{0,8},{1,9},{2,10},{3,11},{4,12},{5,13},{6,14},{7,15},{8,0},{9,1},... | collective-permute-start | bytes 294920 | tf_op jit(solution)/shard_map/ppermute | solution.py:286
  22.0 3.3 %collective-permute-start.3 = (f32[64,128]{1,0:T(8,128)S(1)}, f32[64,128]{1,0:T(8,128)S(1)}, u32[]{:S(2)}, u32[]{:S(2)}) collective-permute-start(f32[64,128]{1,0:T(8,128)S(1)} %add.13), channel_id=1, source_target_pairs={{0,10},{1,11},{2,8},{3,9},{4,14},{5,15},{6,12},{7,13},{8,2},{9,3},... | collective-permute-start | bytes 98312 | tf_op jit(solution)/shard_map/ppermute | solution.py:286
  25.4 4.2 %collective-permute-start.4 = (f32[64,128]{1,0:T(8,128)S(1)}, f32[64,128]{1,0:T(8,128)S(1)}, u32[]{:S(2)}, u32[]{:S(2)}) collective-permute-start(f32[64,128]{1,0:T(8,128)S(1)} %add.14), channel_id=1, source_target_pairs={{0,12},{1,13},{2,14},{3,15},{4,8},{5,9},{6,10},{7,11},{8,4},{9,5},... | collective-permute-start | bytes 98312 | tf_op jit(solution)/shard_map/ppermute | solution.py:286
  29.6 1.2 %collective-permute-start.5 = (f32[64,128]{1,0:T(8,128)S(1)}, f32[64,128]{1,0:T(8,128)S(1)}, u32[]{:S(2)}, u32[]{:S(2)}) collective-permute-start(f32[64,128]{1,0:T(8,128)S(1)} %add.15.refs_0_), channel_id=1, source_target_pairs={{0,8},{1,9},{2,10},{3,11},{4,12},{5,13},{6,14},{7,15},{8,0},{9,1},... | collective-permute-start | bytes 98312 | tf_op jit(solution)/shard_map/ppermute | solution.py:286

commit v3 on v2

--- a/solution.py
+++ b/solution.py
@@ -64,33 +64,34 @@
 
 
 def first_kernel(
-    groups, columns, tile_hbm, cols_hbm, level_hbm, rate_hbm, rows_hbm, spread_hbm,
-    turns_hbm, driving_hbm,
-    averaged, keep, send, tile, spread, target, rows, turns, places, rate,
-    cols, sums, projected, driving, level_index, sems,
+    groups, columns, tile_hbm, cols_hbm, level_hbm, rate_hbm, spread_hbm, rows_hbm,
+    averaged, keep, send, tile, spread, rows, places, rate,
+    cols, sums, projected, level_index, sems,
 ):
     levels, tile_rows, tile_cols = tile.shape
     third_rows, third_cols = tile_rows // 3, tile_cols // 3
     group, _, col = (lax.axis_index(a) for a in AXES)
     is_parent = group == groups - 1
     slot = jnp.where(is_parent, (groups - 1) * columns + col, col * (groups - 1) + group)
+    own_third = pl.ds(pl.multiple_of(group * third_cols, third_cols), third_cols)
+    own_cols = pltpu.make_async_copy(
+        cols_hbm.at[col, own_third], cols.at[pl.ds(0, third_cols)], sems.at[1]
+    )
+    all_cols = pltpu.make_async_copy(cols_hbm.at[col], cols, sems.at[1])
     copies = [
         pltpu.make_async_copy(tile_hbm, tile, sems.at[0]),
-        pltpu.make_async_copy(cols_hbm.at[col], cols, sems.at[1]),
         pltpu.make_async_copy(level_hbm, level_index, sems.at[2]),
     ]
     later = [
-        pltpu.make_async_copy(
-            spread_hbm.at[slot, part // 2], spread.at[pl.ds(part * BASIS, BASIS)], sems.at[3 + part]
-        )
-        for part in range(4)
-    ] + [
-        pltpu.make_async_copy(driving_hbm, driving, sems.at[7]),
-        pltpu.make_async_copy(turns_hbm, turns, sems.at[8]),
-        pltpu.make_async_copy(rows_hbm, rows, sems.at[9]),
-        pltpu.make_async_copy(rate_hbm, rate, sems.at[10]),
+        pltpu.make_async_copy(spread_hbm.at[slot], spread, sems.at[3]),
+        pltpu.make_async_copy(rows_hbm, rows, sems.at[4]),
+        pltpu.make_async_copy(rate_hbm, rate, sems.at[6]),
     ]
-    for copy in copies + later:
+    for copy in copies:
+        copy.start()
+    pl.when(is_parent)(all_cols.start)
+    pl.when(jnp.logical_not(is_parent))(own_cols.start)
+    for copy in later:
         copy.start()
     lanes = sums.shape[-1]
     depth = 3 * lanes
@@ -125,12 +126,13 @@
             averaged[:, parent_level * third_cols : (parent_level + 1) * third_cols] = block
             blocks.append(block)
         projected[...] = jnp.zeros_like(projected)
-        table = cols[pl.ds(pl.multiple_of(group * third_cols, third_cols), third_cols), :]
-        project(blocks, table)
+        own_cols.wait()
+        project(blocks, cols[pl.ds(0, third_cols), :])
 
     @pl.when(is_parent)
     def _():
         averaged[...] = jnp.zeros_like(averaged)
+        all_cols.wait()
         project([tile[level] for level in range(levels)], cols[...])
 
     half = parity_of_device()
@@ -141,8 +143,6 @@
         places[parent_level] = jnp.where(is_parent, parent_level, found)
     for copy in later:
         copy.wait()
-    for pair in range(levels // 2):
-        target[pair] = jnp.concatenate([driving[2 * pair], driving[2 * pair + 1]], axis=1)
 
 
 def coeffs_kernel(full_rows, groups, offset, mine, partner, rows, out):
@@ -156,14 +156,18 @@
     def weights(is_parent):
         start = jnp.where(is_parent, row * tile_rows, strip_start)
         counted = jnp.where(is_parent, strip - full_rows // 3, tile_rows // 3 - 1 - cell) >= 0
-        return jnp.where(counted, rows[pl.ds(start, tile_rows), :], 0.0).astype(jnp.bfloat16)
+        return jnp.where(counted, rows[pl.ds(start, tile_rows), :][:, :BASIS], 0.0).astype(
+            jnp.bfloat16
+        )
 
     table = jnp.concatenate([weights(group == groups - 1), weights((group ^ 1) == groups - 1)], 0)
     high, low = split(jnp.concatenate([mine[...], partner[...]], axis=0))
     out[...] = dot(table, high, ((0,), (0,))) + dot(table, low, ((0,), (0,)))
 
 
-def select_kernel(full_rows, groups, exchanges, offset, first, second, turns, out, weights):
+def select_kernel(
+    full_rows, groups, exchanges, amplitude, offset, first, second, rows, driving, out, weights, target,
+):
     tile_rows = out.shape[0]
     third_rows = tile_rows // 3
     row = lax.axis_index("row")
@@ -182,41 +186,43 @@
     out[...] = dot(pick, strip).astype(jnp.bfloat16)
     period = 3 * full_rows
     child_start = lax.rem(3 * offset[0] + row * tile_rows - 1 + period, period)
-    start = jnp.where(is_parent, period + tile_rows + row * tile_rows, child_start)
-    weights[...] = turns[pl.ds(start, tile_rows), :]
-
-
-def final_kernel(
-    full_rows, groups, amplitude, own_half, offset, places, rate, *refs,
-):
-    coeffs, tile, spread, weights, target, block_0, block_1, block_2 = refs[:8]
-    if own_half:
-        result, left, base = refs[8:]
-    else:
-        earlier, out_hbm, left, base, result, sems = refs[8:]
-    _, tile_rows, tile_cols = tile.shape
-    third_cols = tile_cols // 3
+    own = pl.ds(pl.multiple_of(full_rows + (row + 1) * tile_rows, 8), tile_rows)
+    high, low = split(
+        jnp.where(
+            is_parent, rows[own, :][:, :BASIS], rows[pl.ds(child_start, tile_rows), :][:, BASIS:]
+        )
+    )
+    weights[...] = jnp.concatenate([high, low, high], axis=1)
+    for pair in range(target.shape[0]):
+        both = [driving[2 * pair], driving[2 * pair + 1]]
+        target[pair] = amplitude * jnp.concatenate(both, axis=1)
+
+
+def final_kernel(full_rows, groups, own_half, offset, places, rate, *refs):
+    coeffs, spread, weights, target = refs[:4]
     group, row = lax.axis_index("grp"), lax.axis_index("row")
     is_parent = group == groups - 1
     half = parity_of_device()
     pair = half if own_half else 1 - half
+    if own_half:
+        tile, block_0, block_1, block_2, result, later_base, left, base = refs[4:]
+    else:
+        earlier, base, out_hbm, left, result, sems = refs[4:]
+    _, tile_rows, tile_cols = base.shape
+    third_cols = tile_cols // 3
     copies = []
 
-    def write(source, pair):
-        for side in range(2):
-            target_level = out_hbm.at[places[2 * pair + side]]
-            copies.append(
-                pltpu.make_async_copy(source.at[side], target_level, sems.at[len(copies)])
-            )
-            copies[-1].start()
+    def write(source, side, pair):
+        place = out_hbm.at[places[2 * pair + side]]
+        copies.append(pltpu.make_async_copy(source.at[side], place, sems.at[len(copies)]))
+        copies[-1].start()
 
     if not own_half:
-        write(earlier, half)
+        write(earlier, 0, half)
+        write(earlier, 1, half)
+    high, low = split(target[pair] - coeffs[...])
+    turned = dot(weights[...], jnp.concatenate([high, high, low], axis=0))
     is_left = lax.broadcasted_iota(jnp.int32, (tile_rows, 2 * BASIS), 1) < BASIS
-    turned = jnp.dot(
-        weights[...], amplitude * target[pair] - coeffs[...], precision=lax.Precision.HIGHEST,
-        preferred_element_type=jnp.float32,
-    )
     for side in range(2):
         high, low = split(turned * rate[2 * pair + side])
         low = pltpu.roll(low.astype(jnp.float32), BASIS, 1).astype(jnp.bfloat16)
@@ -224,34 +230,37 @@
         span = pl.ds(side * tile_rows, tile_rows)
         left[span, : 2 * BASIS] = jnp.where(here, high, low)
         left[span, 2 * BASIS :] = jnp.where(here, high, jnp.zeros_like(high))
-    increment = dot(left[...], spread[...])
-
-    @pl.when(is_parent)
-    def _():
-        cell = lax.broadcasted_iota(jnp.int32, (tile_rows, third_cols), 0)
-        strip = lax.rem(row * tile_rows + cell - offset[0] + full_rows, full_rows)
-        covered = strip < full_rows // 3
-        for side in range(2):
-            level = 2 * pair + side
-            for third, block in enumerate((block_0, block_1, block_2)):
-                span = slice(third * third_cols, (third + 1) * third_cols)
-                arrived = block[:, pl.ds(pl.multiple_of(level * third_cols, 128), third_cols)]
-                base[side, :, span] = jnp.where(
-                    covered, arrived.astype(jnp.float32), tile[level, :, span].astype(jnp.float32)
-                )
-
-    levels_out = [places[2 * pair + side] for side in range(2)]
-
-    @pl.when(jnp.logical_not(is_parent))
-    def _():
-        for side in range(2):
-            base[side] = tile[levels_out[side]].astype(jnp.float32)
+    high, low = spread[0], spread[1]
+    increment = dot(left[...], jnp.concatenate([high, high, low, low], axis=0))
+
+    if own_half:
+
+        @pl.when(is_parent)
+        def _():
+            cell = lax.broadcasted_iota(jnp.int32, (tile_rows, third_cols), 0)
+            strip = lax.rem(row * tile_rows + cell - offset[0] + full_rows, full_rows)
+            covered = strip < full_rows // 3
+            for goal, goal_pair in ((base, half), (later_base, 1 - half)):
+                for side in range(2):
+                    level = 2 * goal_pair + side
+                    for third, block in enumerate((block_0, block_1, block_2)):
+                        span = slice(third * third_cols, (third + 1) * third_cols)
+                        lanes = pl.ds(pl.multiple_of(level * third_cols, 128), third_cols)
+                        arrived = block[:, lanes].astype(jnp.float32)
+                        own = tile[level, :, span].astype(jnp.float32)
+                        goal[side, :, span] = jnp.where(covered, arrived, own)
+
+        @pl.when(jnp.logical_not(is_parent))
+        def _():
+            for goal, goal_pair in ((base, half), (later_base, 1 - half)):
+                for side in range(2):
+                    goal[side] = tile[places[2 * goal_pair + side]].astype(jnp.float32)
 
     for side in range(2):
         rows = increment[side * tile_rows : (side + 1) * tile_rows]
         result[side] = (base[side] + rows).astype(jnp.bfloat16)
-    if not own_half:
-        write(result, pair)
+        if not own_half:
+            write(result, side, pair)
     for copy in copies:
         copy.wait()
 
@@ -271,7 +280,9 @@
     rounded = parent_rows.astype(bf16).astype(np.float32)
     rounded = np.concatenate([rounded, rounded[:tile_rows]], 0)
     child_rows = basis_table(np.arange(3 * full_rows), full_rows)
-    turns = np.concatenate([child_rows, child_rows[:tile_rows], parent_rows], 0)
+    row_table = np.zeros((3 * full_rows + tile_rows, 2 * BASIS), np.float32)
+    row_table[: 2 * full_rows + tile_rows, :BASIS] = np.concatenate([rounded, parent_rows], 0)
+    row_table[:, BASIS:] = np.concatenate([child_rows, child_rows[:tile_rows]], 0)
     child_cols = basis_table((np.arange(3 * full_cols) - 1) % (3 * full_cols), full_cols)
     spread_rows = np.concatenate([child_cols, cols], 0).reshape(-1, tile_cols, BASIS)
     spread_rows = spread_rows.transpose(0, 2, 1)
@@ -292,34 +303,31 @@
     along = [mask_of(0, bit, 0) ^ flip for bit in row_bits]
     rounds = across + along[::-1]
 
-    averaged, keep, send, tile, spread, target, rows, turns, places, rate = pl.pallas_call(
+    averaged, keep, send, tile, spread, rows, places, rate = pl.pallas_call(
         functools.partial(first_kernel, groups, col_count),
         out_shape=(
             pltpu.VMEM((third_rows, levels * third_cols), bf16),
             pltpu.VMEM((tile_rows, 2 * BASIS), f32),
             pltpu.VMEM((tile_rows, 2 * BASIS), f32),
             pltpu.VMEM(tile_in.shape, bf16),
-            pltpu.VMEM((4 * BASIS, tile_cols), bf16),
-            pltpu.VMEM((levels // 2, BASIS, 2 * BASIS), f32),
-            pltpu.VMEM(rounded.shape, f32),
-            pltpu.VMEM(turns.shape, f32),
+            pltpu.VMEM((2, BASIS, tile_cols), bf16),
+            pltpu.VMEM(row_table.shape, f32),
             pltpu.SMEM((levels,), jnp.int32),
             pltpu.SMEM((levels,), f32),
         ),
-        in_specs=[ANY] * 8,
-        out_specs=(VMEM,) * 8 + (SMEM, SMEM),
+        in_specs=[ANY] * 6,
+        out_specs=(VMEM,) * 6 + (SMEM, SMEM),
         scratch_shapes=[
             pltpu.VMEM((tile_cols, 2 * BASIS), bf16),
             pltpu.VMEM((third_cols // 128, levels, tile_rows, 128), f32),
             pltpu.VMEM((levels // 2, tile_rows, 2 * BASIS), f32),
-            pltpu.VMEM(driving.shape, f32),
             pltpu.SMEM((levels,), jnp.int32),
-            pltpu.SemaphoreType.DMA((11,)),
+            pltpu.SemaphoreType.DMA((7,)),
         ],
         name="first",
     )(
         tile_in, jnp.asarray(cols_twice), in_hbm(level_index), in_hbm(nudge_rate),
-        jnp.asarray(rounded), jnp.asarray(spread_table), jnp.asarray(turns), driving,
+        jnp.asarray(spread_table), jnp.asarray(row_table),
     )
 
     partner = exchange(send, flip)
@@ -338,39 +346,42 @@
     for step, bit in enumerate(row_bits):
         held = strips[0] if step == 0 else jnp.concatenate(strips, 0)
         strips = [held, exchange(held, mask_of(0, bit, 0))]
-    selected, weights = pl.pallas_call(
-        functools.partial(select_kernel, full_rows, groups, len(row_bits)),
+    selected, weights, target = pl.pallas_call(
+        functools.partial(select_kernel, full_rows, groups, len(row_bits), amplitude),
         out_shape=(
             pltpu.VMEM((tile_rows, levels * third_cols), bf16),
-            pltpu.VMEM((tile_rows, BASIS), f32),
+            pltpu.VMEM((tile_rows, 3 * BASIS), bf16),
+            pltpu.VMEM((levels // 2, BASIS, 2 * BASIS), f32),
         ),
-        in_specs=[SMEM, VMEM, VMEM, VMEM],
-        out_specs=(VMEM, VMEM),
+        in_specs=[SMEM] + [VMEM] * 4,
+        out_specs=(VMEM,) * 3,
         name="select",
-    )(offset, *(in_vmem(value) for value in (*strips, turns)))
+    )(offset, *(in_vmem(value) for value in (*strips, rows, driving)))
     block_0 = exchange(selected, mask_of(3, 0, 0))
     block_2 = exchange(selected, mask_of(1, 0, 0))
     block_1 = exchange(block_0, mask_of(1, 0, 0))
 
-    def finish(coeffs, earlier):
-        two_levels = (2, tile_rows, tile_cols)
-        scratch = [pltpu.VMEM((2 * tile_rows, 4 * BASIS), bf16), pltpu.VMEM(two_levels, f32)]
-        if earlier:
-            scratch += [pltpu.VMEM(two_levels, bf16), pltpu.SemaphoreType.DMA((4,))]
-            out_shape, out_spec = jax.ShapeDtypeStruct(tile_in.shape, bf16), ANY
-        else:
-            out_shape, out_spec = pltpu.VMEM(two_levels, bf16), VMEM
-        values = (coeffs, tile, spread, weights, target, block_0, block_1, block_2, *earlier)
+    def finish(name, coeffs, values, out_shape, out_spec, scratch):
+        values = (coeffs, spread, weights, target, *values)
         return pl.pallas_call(
-            functools.partial(final_kernel, full_rows, groups, amplitude, not earlier),
+            functools.partial(final_kernel, full_rows, groups, name == "final_own"),
             out_shape=out_shape,
             in_specs=[SMEM] * 3 + [VMEM] * len(values),
             out_specs=out_spec,
-            scratch_shapes=scratch,
+            scratch_shapes=[pltpu.VMEM((2 * tile_rows, 4 * BASIS), bf16), *scratch],
         )(offset, places, rate, *(in_vmem(value) for value in values))
 
-    partly = finish(mine, ())
-    return finish(other, (partly,))[None]
+    two_levels = (2, tile_rows, tile_cols)
+    earlier = finish(
+        "final_own", mine, (tile, block_0, block_1, block_2),
+        (pltpu.VMEM(two_levels, bf16), pltpu.VMEM(two_levels, f32)), (VMEM, VMEM),
+        [pltpu.VMEM(two_levels, f32)],
+    )
+    result = finish(
+        "final_other", other, earlier, jax.ShapeDtypeStruct(tile_in.shape, bf16), ANY,
+        [pltpu.VMEM(two_levels, bf16), pltpu.SemaphoreType.DMA((4,))],
+    )
+    return result[None]
 
 
 def solution(mesh):

time: 32.1 us -> 31.9 us (level)
  no operation moved by 1% of the time
where the time goes in v3:
time: 31.9 us; the launch traced here: 31.8 us
  starting transfers between devices  14 us (44%)
  waiting for transfers between devices  13.6 us (43%)
  Pallas kernels  3.46 us (11%)
  between operations  0.7 us (2%)
    ppermute x11, starting transfers between devices, exchange(): return lax.ppermute(value, AXES, [(i, i ^ mask) for i in range(count)])  14 us
    ppermute x11, waiting for transfers between devices, exchange(): return lax.ppermute(value, AXES, [(i, i ^ mask) for i in range(count)])  13.6 us
    pallas_call x2, Pallas kernels, finish(): pl.pallas_call(functools.partial(final_kernel, full_rows, groups, name ==...  1.58 us
    pallas_call x1, Pallas kernels, per_device(): pl.pallas_call(functools.partial(first_kernel, groups, col_count), out_sh...  1.5 us
  transfers between devices with their start and end apart: 11, of which 8 were waited for; matrix products, arithmetic and copies ran while one was open for 0% of the time, Pallas kernels for 2%

profile of v3, /device:TPU:0, one launch (start us, length us, event | category | flops | bytes accessed | tf_op | source)
XLA Modules:
  0.0 31.8 jit_solution(12099402905972452162)
XLA Ops:
  0.0 0.0 copy-start
  0.0 1.5 %first.1 = (bf16[16,1024]{1,0:T(8,128)(2,1)S(1)}, f32[48,128]{1,0:T(8,128)S(1)}, f32[48,128]{1,0:T(8,128)S(1)}, bf16[4,48,768]{2,1,0:T(8,128)(2,1)S(1)}, bf16[2,...) custom-call(bf16[4,48,768]{2,1,0:T(8,128)(2,1)} %bitcast.2, ...), custom_call_target="tpu_custom_call" | custom-call | tf_op jit(solution)/shard_map/first/pallas_call | solution.py:306
  1.5 4.1 %collective-permute-start.6 = (bf16[16,1024]{1,0:T(8,128)(2,1)S(1)}, bf16[16,1024]{1,0:T(8,128)(2,1)S(1)}, u32[]{:S(2)}, u32[]{:S(2)}) collective-permute-start(bf16[16,1024]{1,0:T(8,128)(2,1)S(1)} %get-tuple-element.24), channel_id=1, source_target_pairs={{0,4},{1,5},{2,6},{3,7},{4,0},{5,1},{6,2},{7,3},{8,12},{9,13},{10,... | collective-permute-start | bytes 98312 | tf_op jit(solution)/shard_map/ppermute | solution.py:297
  5.6 2.2 %collective-permute-done.6 = bf16[16,1024]{1,0:T(8,128)(2,1)S(1)} collective-permute-done((bf16[16,1024]{1,0:T(8,128)(2,1)S(1)}, bf16[16,1024]{1,0:T(8,128)(2,1)S(1)}, u32[]{:S(2)}, u32[]{:S(2)}) %collective-permute-start.6) | collective-permute-done | bytes 32800 | tf_op jit(solution)/shard_map/ppermute | solution.py:297
  7.9 1.6 %collective-permute-start.7 = (bf16[32,1024]{1,0:T(8,128)(2,1)S(1)}, bf16[32,1024]{1,0:T(8,128)(2,1)S(1)}, u32[]{:S(2)}, u32[]{:S(2)}) collective-permute-start(bf16[32,1024]{1,0:T(8,128)(2,1)S(1)} %constant_dynamic-update-slice_fusion.first), channel_id=1, source_target_pairs={{0,2},{1,3},{2,0},{3,1},{4,6},{5,7},{6,4},{7,5},{8,10},{9,11},{10,... | collective-permute-start | bytes 196616 | tf_op jit(solution)/shard_map/ppermute | solution.py:297
  10.1 2.1 %collective-permute-done.7.second = bf16[32,1024]{1,0:T(8,128)(2,1)S(1)} collective-permute-done((bf16[32,1024]{1,0:T(8,128)(2,1)S(1)}, bf16[32,1024]{1,0:T(8,128)(2,1)S(1)}, u32[]{:S(2)}, u32[]{:S(2)}) %collective-permute-start.7) | collective-permute-done | bytes 65568 | tf_op jit(solution)/shard_map/ppermute | solution.py:297
  12.2 0.0 copy-done
  12.2 0.2 select.1
  12.3 0.1 collective-permute-start.8
  12.4 1.7 %collective-permute-start = (f32[48,128]{1,0:T(8,128)S(1)}, f32[48,128]{1,0:T(8,128)S(1)}, u32[]{:S(2)}, u32[]{:S(2)}) collective-permute-start(f32[48,128]{1,0:T(8,128)S(1)} %get-tuple-element.21), channel_id=1, source_target_pairs={{0,8},{1,9},{2,10},{3,11},{4,12},{5,13},{6,14},{7,15},{8,0},{9,1},... | collective-permute-start | bytes 73736 | tf_op jit(solution)/shard_map/ppermute | solution.py:297
  14.1 0.8 %collective-permute-done.partner = f32[48,128]{1,0:T(8,128)S(1)} collective-permute-done((f32[48,128]{1,0:T(8,128)S(1)}, f32[48,128]{1,0:T(8,128)S(1)}, u32[]{:S(2)}, u32[]{:S(2)}) %collective-permute-start) | collective-permute-done | bytes 24608 | tf_op jit(solution)/shard_map/ppermute | solution.py:297
  15.0 0.2 coeffs.1
  15.2 0.4 %collective-permute-start.1 = (f32[64,128]{1,0:T(8,128)S(1)}, f32[64,128]{1,0:T(8,128)S(1)}, u32[]{:S(2)}, u32[]{:S(2)}) collective-permute-start(f32[64,128]{1,0:T(8,128)S(1)} %coeffs.1), channel_id=1, source_target_pairs={{0,24},{1,25},{2,26},{3,27},{4,28},{5,29},{6,30},{7,31},{8,16},{9,... | collective-permute-start | bytes 98312 | tf_op jit(solution)/shard_map/ppermute | solution.py:297
  15.6 3.0 %collective-permute-done.1 = f32[64,128]{1,0:T(8,128)S(1)} collective-permute-done((f32[64,128]{1,0:T(8,128)S(1)}, f32[64,128]{1,0:T(8,128)S(1)}, u32[]{:S(2)}, u32[]{:S(2)}) %collective-permute-start.1) | collective-permute-done | bytes 32800 | tf_op jit(solution)/shard_map/ppermute | solution.py:297
  18.5 1.5 %collective-permute-start.2 = (f32[64,128]{1,0:T(8,128)S(1)}, f32[64,128]{1,0:T(8,128)S(1)}, u32[]{:S(2)}, u32[]{:S(2)}) collective-permute-start(f32[64,128]{1,0:T(8,128)S(1)} %add.12), channel_id=1, source_target_pairs={{0,9},{1,8},{2,11},{3,10},{4,13},{5,12},{6,15},{7,14},{8,1},{9,0},... | collective-permute-start | bytes 98312 | tf_op jit(solution)/shard_map/ppermute | solution.py:297
  20.0 0.2 collective-permute-start.10
  20.2 0.0 collective-permute-done.8.refs_5_
  20.2 0.3 %collective-permute-start.9 = (bf16[48,1024]{1,0:T(8,128)(2,1)S(1)}, bf16[48,1024]{1,0:T(8,128)(2,1)S(1)}, u32[]{:S(2)}, u32[]{:S(2)}) collective-permute-start(bf16[48,1024]{1,0:T(8,128)(2,1)S(1)} %collective-permute-done.8.refs_5_), channel_id=1, source_target_pairs={{0,8},{1,9},{2,10},{3,11},{4,12},{5,13},{6,14},{7,15},{8,0},{9,1},... | collective-permute-start | bytes 294920 | tf_op jit(solution)/shard_map/ppermute | solution.py:297
  20.5 1.4 %collective-permute-done.2 = f32[64,128]{1,0:T(8,128)S(1)} collective-permute-done((f32[64,128]{1,0:T(8,128)S(1)}, f32[64,128]{1,0:T(8,128)S(1)}, u32[]{:S(2)}, u32[]{:S(2)}) %collective-permute-start.2) | collective-permute-done | bytes 32800 | tf_op jit(solution)/shard_map/ppermute | solution.py:297
  21.9 1.4 %collective-permute-start.3 = (f32[64,128]{1,0:T(8,128)S(1)}, f32[64,128]{1,0:T(8,128)S(1)}, u32[]{:S(2)}, u32[]{:S(2)}) collective-permute-start(f32[64,128]{1,0:T(8,128)S(1)} %add.13), channel_id=1, source_target_pairs={{0,10},{1,11},{2,8},{3,9},{4,14},{5,15},{6,12},{7,13},{8,2},{9,3},... | collective-permute-start | bytes 98312 | tf_op jit(solution)/shard_map/ppermute | solution.py:297
  23.3 2.0 %collective-permute-done.3 = f32[64,128]{1,0:T(8,128)S(1)} collective-permute-done((f32[64,128]{1,0:T(8,128)S(1)}, f32[64,128]{1,0:T(8,128)S(1)}, u32[]{:S(2)}, u32[]{:S(2)}) %collective-permute-start.3) | collective-permute-done | bytes 32800 | tf_op jit(solution)/shard_map/ppermute | solution.py:297
  25.2 2.4 %collective-permute-start.4 = (f32[64,128]{1,0:T(8,128)S(1)}, f32[64,128]{1,0:T(8,128)S(1)}, u32[]{:S(2)}, u32[]{:S(2)}) collective-permute-start(f32[64,128]{1,0:T(8,128)S(1)} %add.14), channel_id=1, source_target_pairs={{0,12},{1,13},{2,14},{3,15},{4,8},{5,9},{6,10},{7,11},{8,4},{9,5},... | collective-permute-start | bytes 98312 | tf_op jit(solution)/shard_map/ppermute | solution.py:297
  27.7 1.8 %collective-permute-done.4 = f32[64,128]{1,0:T(8,128)S(1)} collective-permute-done((f32[64,128]{1,0:T(8,128)S(1)}, f32[64,128]{1,0:T(8,128)S(1)}, u32[]{:S(2)}, u32[]{:S(2)}) %collective-permute-start.4) | collective-permute-done | bytes 32800 | tf_op jit(solution)/shard_map/ppermute | solution.py:297
  29.5 0.3 %collective-permute-start.5 = (f32[64,128]{1,0:T(8,128)S(1)}, f32[64,128]{1,0:T(8,128)S(1)}, u32[]{:S(2)}, u32[]{:S(2)}) collective-permute-start(f32[64,128]{1,0:T(8,128)S(1)} %add.15.refs_0_), channel_id=1, source_target_pairs={{0,8},{1,9},{2,10},{3,11},{4,12},{5,13},{6,14},{7,15},{8,0},{9,1},... | collective-permute-start | bytes 98312 | tf_op jit(solution)/shard_map/ppermute | solution.py:297
  29.8 0.0 collective-permute-done.10.refs_7_
  29.8 0.0 collective-permute-done.9.refs_6_
  29.8 0.5 %shard_map.82 = (bf16[2,48,768]{2,1,0:T(8,128)(2,1)S(1)}, f32[2,48,768]{2,1,0:T(8,128)S(1)}) custom-call(s32[1]{0:T(128)S(6)} %copy.10.offset, s32[4]{0:T(128)S(4)} %get-tuple-element.18.places, f32[4]{0:T(128)S(4)} %get-tuple-element.19.rate, f32[64,128]{1,0:T(8,128)S(1)} %add.15.refs_0_, bf16[2,64,768]{2,1,0:T(8,128)(2,1)S(1)} %get-tuple-element.23.refs_1_, ...), custom_call_target="tpu_custom_call" | custom-call | tf_op jit(solution)/shard_map/pallas_call | solution.py:366
  30.3 0.4 %collective-permute-done.5.refs_0_ = f32[64,128]{1,0:T(8,128)S(1)} collective-permute-done((f32[64,128]{1,0:T(8,128)S(1)}, f32[64,128]{1,0:T(8,128)S(1)}, u32[]{:S(2)}, u32[]{:S(2)}) %collective-permute-start.5) | collective-permute-done | bytes 32800 | tf_op jit(solution)/shard_map/ppermute | solution.py:297
  30.7 1.1 %shard_map.83 = bf16[4,48,768]{2,1,0:T(8,128)(2,1)} custom-call(s32[1]{0:T(128)S(6)} %copy.10.offset, s32[4]{0:T(128)S(4)} %get-tuple-element.18.places, f32[4]{0:T(128)S(4)} %get-tuple-element.19.rate, f32[64,128]{1,0:T(8,128)S(1)} %collective-permute-done.5.refs_0_, bf16[2,64,768]{2,1,0:T(8,128)(2,1)S(1)} %get-tuple-element.23.refs_1_, ...), custom_call_target="tpu_custom_call" | custom-call | tf_op jit(solution)/shard_map/pallas_call | solution.py:366
  (6 shorter events, 0.0 us)
Async XLA Ops:
  0.0 12.2 %copy-start = (f32[4,64,64]{2,1,0:T(8,128)S(1)}, f32[4,64,64]{2,1,0:T(8,128)}, u32[]{:S(2)}) copy-start(f32[4,64,64]{2,1,0:T(8,128)} %driving.1) | copy-start | bytes 196612
  1.5 6.4 %collective-permute-start.6 = (bf16[16,1024]{1,0:T(8,128)(2,1)S(1)}, bf16[16,1024]{1,0:T(8,128)(2,1)S(1)}, u32[]{:S(2)}, u32[]{:S(2)}) collective-permute-start(bf16[16,1024]{1,0:T(8,128)(2,1)S(1)} %get-tuple-element.24), channel_id=1, source_target_pairs={{0,4},{1,5},{2,6},{3,7},{4,0},{5,1},{6,2},{7,3},{8,12},{9,13},{10,... | collective-permute-start | bytes 98312 | tf_op jit(solution)/shard_map/ppermute | solution.py:297
  7.9 4.3 %collective-permute-start.7 = (bf16[32,1024]{1,0:T(8,128)(2,1)S(1)}, bf16[32,1024]{1,0:T(8,128)(2,1)S(1)}, u32[]{:S(2)}, u32[]{:S(2)}) collective-permute-start(bf16[32,1024]{1,0:T(8,128)(2,1)S(1)} %constant_dynamic-update-slice_fusion.first), channel_id=1, source_target_pairs={{0,2},{1,3},{2,0},{3,1},{4,6},{5,7},{6,4},{7,5},{8,10},{9,11},{10,... | collective-permute-start | bytes 196616 | tf_op jit(solution)/shard_map/ppermute | solution.py:297
  12.3 7.8 %collective-permute-start.8 = (bf16[48,1024]{1,0:T(8,128)(2,1)S(1)}, bf16[48,1024]{1,0:T(8,128)(2,1)S(1)}, u32[]{:S(2)}, u32[]{:S(2)}) collective-permute-start(bf16[48,1024]{1,0:T(8,128)(2,1)S(1)} %get-tuple-element.28), channel_id=1, source_target_pairs={{0,24},{1,25},{2,26},{3,27},{4,28},{5,29},{6,30},{7,31},{8,16},{9,... | collective-permute-start | bytes 294920 | tf_op jit(solution)/shard_map/ppermute | solution.py:297
  12.4 2.6 %collective-permute-start = (f32[48,128]{1,0:T(8,128)S(1)}, f32[48,128]{1,0:T(8,128)S(1)}, u32[]{:S(2)}, u32[]{:S(2)}) collective-permute-start(f32[48,128]{1,0:T(8,128)S(1)} %get-tuple-element.21), channel_id=1, source_target_pairs={{0,8},{1,9},{2,10},{3,11},{4,12},{5,13},{6,14},{7,15},{8,0},{9,1},... | collective-permute-start | bytes 73736 | tf_op jit(solution)/shard_map/ppermute | solution.py:297
  15.2 3.3 %collective-permute-start.1 = (f32[64,128]{1,0:T(8,128)S(1)}, f32[64,128]{1,0:T(8,128)S(1)}, u32[]{:S(2)}, u32[]{:S(2)}) collective-permute-start(f32[64,128]{1,0:T(8,128)S(1)} %coeffs.1), channel_id=1, source_target_pairs={{0,24},{1,25},{2,26},{3,27},{4,28},{5,29},{6,30},{7,31},{8,16},{9,... | collective-permute-start | bytes 98312 | tf_op jit(solution)/shard_map/ppermute | solution.py:297
  18.5 3.3 %collective-permute-start.2 = (f32[64,128]{1,0:T(8,128)S(1)}, f32[64,128]{1,0:T(8,128)S(1)}, u32[]{:S(2)}, u32[]{:S(2)}) collective-permute-start(f32[64,128]{1,0:T(8,128)S(1)} %add.12), channel_id=1, source_target_pairs={{0,9},{1,8},{2,11},{3,10},{4,13},{5,12},{6,15},{7,14},{8,1},{9,0},... | collective-permute-start | bytes 98312 | tf_op jit(solution)/shard_map/ppermute | solution.py:297
  20.0 9.8 %collective-permute-start.10 = (bf16[48,1024]{1,0:T(8,128)(2,1)S(1)}, bf16[48,1024]{1,0:T(8,128)(2,1)S(1)}, u32[]{:S(2)}, u32[]{:S(2)}) collective-permute-start(bf16[48,1024]{1,0:T(8,128)(2,1)S(1)} %get-tuple-element.28), channel_id=1, source_target_pairs={{0,8},{1,9},{2,10},{3,11},{4,12},{5,13},{6,14},{7,15},{8,0},{9,1},... | collective-permute-start | bytes 294920 | tf_op jit(solution)/shard_map/ppermute | solution.py:297
  20.2 9.7 %collective-permute-start.9 = (bf16[48,1024]{1,0:T(8,128)(2,1)S(1)}, bf16[48,1024]{1,0:T(8,128)(2,1)S(1)}, u32[]{:S(2)}, u32[]{:S(2)}) collective-permute-start(bf16[48,1024]{1,0:T(8,128)(2,1)S(1)} %collective-permute-done.8.refs_5_), channel_id=1, source_target_pairs={{0,8},{1,9},{2,10},{3,11},{4,12},{5,13},{6,14},{7,15},{8,0},{9,1},... | collective-permute-start | bytes 294920 | tf_op jit(solution)/shard_map/ppermute | solution.py:297
  21.9 3.3 %collective-permute-start.3 = (f32[64,128]{1,0:T(8,128)S(1)}, f32[64,128]{1,0:T(8,128)S(1)}, u32[]{:S(2)}, u32[]{:S(2)}) collective-permute-start(f32[64,128]{1,0:T(8,128)S(1)} %add.13), channel_id=1, source_target_pairs={{0,10},{1,11},{2,8},{3,9},{4,14},{5,15},{6,12},{7,13},{8,2},{9,3},... | collective-permute-start | bytes 98312 | tf_op jit(solution)/shard_map/ppermute | solution.py:297
  25.2 4.2 %collective-permute-start.4 = (f32[64,128]{1,0:T(8,128)S(1)}, f32[64,128]{1,0:T(8,128)S(1)}, u32[]{:S(2)}, u32[]{:S(2)}) collective-permute-start(f32[64,128]{1,0:T(8,128)S(1)} %add.14), channel_id=1, source_target_pairs={{0,12},{1,13},{2,14},{3,15},{4,8},{5,9},{6,10},{7,11},{8,4},{9,5},... | collective-permute-start | bytes 98312 | tf_op jit(solution)/shard_map/ppermute | solution.py:297
  29.5 1.2 %collective-permute-start.5 = (f32[64,128]{1,0:T(8,128)S(1)}, f32[64,128]{1,0:T(8,128)S(1)}, u32[]{:S(2)}, u32[]{:S(2)}) collective-permute-start(f32[64,128]{1,0:T(8,128)S(1)} %add.15.refs_0_), channel_id=1, source_target_pairs={{0,8},{1,9},{2,10},{3,11},{4,12},{5,13},{6,14},{7,15},{8,0},{9,1},... | collective-permute-start | bytes 98312 | tf_op jit(solution)/shard_map/ppermute | solution.py:297

commit v4 on v3

--- a/solution.py
+++ b/solution.py
@@ -292,16 +292,20 @@
     def mask_of(group_bits, row_bits, col_bits):
         return (group_bits * row_count + row_bits) * col_count + col_bits
 
-    def exchange(value, mask):
+    def exchange(value, mask, odd_mask=None):
+        masks = (mask, mask if odd_mask is None else odd_mask)
         count = groups * row_count * col_count
-        return lax.ppermute(value, AXES, [(i, i ^ mask) for i in range(count)])
+        pairs = [(i, i ^ masks[i.bit_count() % 2]) for i in range(count)]
+        return lax.ppermute(value, AXES, pairs)
 
     flip = mask_of(1, 0, 0)
     across = [mask_of(1 << k, 0, 0) ^ flip for k in range(1, groups.bit_length() - 1)]
     across += [mask_of(0, 0, 1 << k) ^ flip for k in range(col_count.bit_length() - 1)]
     row_bits = [1 << k for k in reversed(range(row_count.bit_length() - 1))]
     along = [mask_of(0, bit, 0) ^ flip for bit in row_bits]
-    rounds = across + along[::-1]
+    along = along[::-1]
+    rounds = across + along
+    odd_rounds = across[:1] + along[:1] + across[1:] + along[1:]
 
     averaged, keep, send, tile, spread, rows, places, rate = pl.pallas_call(
         functools.partial(first_kernel, groups, col_count),
@@ -338,8 +342,8 @@
         out_specs=VMEM,
         name="coeffs",
     )(offset, in_vmem(keep), in_vmem(partner), in_vmem(rows))
-    for mask in rounds:
-        mine = mine + exchange(mine, mask)
+    for masks in zip(rounds, odd_rounds):
+        mine = mine + exchange(mine, masks[0], masks[1])
     other = exchange(mine, flip)
 
     strips = [averaged]

time: 31.9 us -> 31.9 us (level)
  no operation moved by 1% of the time
where the time goes in v4:
time: 31.9 us; the launch traced here: 31.8 us
  starting transfers between devices  14 us (44%)
  waiting for transfers between devices  13.6 us (43%)
  Pallas kernels  3.46 us (11%)
  between operations  0.7 us (2%)
    ppermute x11, starting transfers between devices, exchange(): return lax.ppermute(value, AXES, pairs)  14 us
    ppermute x11, waiting for transfers between devices, exchange(): return lax.ppermute(value, AXES, pairs)  13.6 us
    pallas_call x2, Pallas kernels, finish(): pl.pallas_call(functools.partial(final_kernel, full_rows, groups, name ==...  1.58 us
    pallas_call x1, Pallas kernels, per_device(): pl.pallas_call(functools.partial(first_kernel, groups, col_count), out_sh...  1.5 us
  transfers between devices with their start and end apart: 11, of which 8 were waited for; matrix products, arithmetic and copies ran while one was open for 0% of the time, Pallas kernels for 2%

profile of v4, /device:TPU:0, one launch (start us, length us, event | category | flops | bytes accessed | tf_op | source)
XLA Modules:
  0.0 31.8 jit_solution(12531303506944007298)
XLA Ops:
  0.0 0.0 copy-start
  0.0 1.5 %first.1 = (bf16[16,1024]{1,0:T(8,128)(2,1)S(1)}, f32[48,128]{1,0:T(8,128)S(1)}, f32[48,128]{1,0:T(8,128)S(1)}, bf16[4,48,768]{2,1,0:T(8,128)(2,1)S(1)}, bf16[2,...) custom-call(bf16[4,48,768]{2,1,0:T(8,128)(2,1)} %bitcast.2, ...), custom_call_target="tpu_custom_call" | custom-call | tf_op jit(solution)/shard_map/first/pallas_call | solution.py:310
  1.5 4.1 %collective-permute-start.6 = (bf16[16,1024]{1,0:T(8,128)(2,1)S(1)}, bf16[16,1024]{1,0:T(8,128)(2,1)S(1)}, u32[]{:S(2)}, u32[]{:S(2)}) collective-permute-start(bf16[16,1024]{1,0:T(8,128)(2,1)S(1)} %get-tuple-element.24), channel_id=1, source_target_pairs={{0,4},{1,5},{2,6},{3,7},{4,0},{5,1},{6,2},{7,3},{8,12},{9,13},{10,... | collective-permute-start | bytes 98312 | tf_op jit(solution)/shard_map/ppermute | solution.py:299
  5.6 2.2 %collective-permute-done.6 = bf16[16,1024]{1,0:T(8,128)(2,1)S(1)} collective-permute-done((bf16[16,1024]{1,0:T(8,128)(2,1)S(1)}, bf16[16,1024]{1,0:T(8,128)(2,1)S(1)}, u32[]{:S(2)}, u32[]{:S(2)}) %collective-permute-start.6) | collective-permute-done | bytes 32800 | tf_op jit(solution)/shard_map/ppermute | solution.py:299
  7.9 1.6 %collective-permute-start.7 = (bf16[32,1024]{1,0:T(8,128)(2,1)S(1)}, bf16[32,1024]{1,0:T(8,128)(2,1)S(1)}, u32[]{:S(2)}, u32[]{:S(2)}) collective-permute-start(bf16[32,1024]{1,0:T(8,128)(2,1)S(1)} %constant_dynamic-update-slice_fusion.first), channel_id=1, source_target_pairs={{0,2},{1,3},{2,0},{3,1},{4,6},{5,7},{6,4},{7,5},{8,10},{9,11},{10,... | collective-permute-start | bytes 196616 | tf_op jit(solution)/shard_map/ppermute | solution.py:299
  10.1 2.1 %collective-permute-done.7.second = bf16[32,1024]{1,0:T(8,128)(2,1)S(1)} collective-permute-done((bf16[32,1024]{1,0:T(8,128)(2,1)S(1)}, bf16[32,1024]{1,0:T(8,128)(2,1)S(1)}, u32[]{:S(2)}, u32[]{:S(2)}) %collective-permute-start.7) | collective-permute-done | bytes 65568 | tf_op jit(solution)/shard_map/ppermute | solution.py:299
  12.2 0.0 copy-done
  12.2 0.2 select.1
  12.3 0.1 collective-permute-start.8
  12.4 1.7 %collective-permute-start = (f32[48,128]{1,0:T(8,128)S(1)}, f32[48,128]{1,0:T(8,128)S(1)}, u32[]{:S(2)}, u32[]{:S(2)}) collective-permute-start(f32[48,128]{1,0:T(8,128)S(1)} %get-tuple-element.21), channel_id=1, source_target_pairs={{0,8},{1,9},{2,10},{3,11},{4,12},{5,13},{6,14},{7,15},{8,0},{9,1},... | collective-permute-start | bytes 73736 | tf_op jit(solution)/shard_map/ppermute | solution.py:299
  14.1 0.8 %collective-permute-done.partner = f32[48,128]{1,0:T(8,128)S(1)} collective-permute-done((f32[48,128]{1,0:T(8,128)S(1)}, f32[48,128]{1,0:T(8,128)S(1)}, u32[]{:S(2)}, u32[]{:S(2)}) %collective-permute-start) | collective-permute-done | bytes 24608 | tf_op jit(solution)/shard_map/ppermute | solution.py:299
  15.0 0.2 coeffs.1
  15.2 0.4 %collective-permute-start.1 = (f32[64,128]{1,0:T(8,128)S(1)}, f32[64,128]{1,0:T(8,128)S(1)}, u32[]{:S(2)}, u32[]{:S(2)}) collective-permute-start(f32[64,128]{1,0:T(8,128)S(1)} %coeffs.1), channel_id=1, source_target_pairs={{0,24},{1,25},{2,26},{3,27},{4,28},{5,29},{6,30},{7,31},{8,16},{9,... | collective-permute-start | bytes 98312 | tf_op jit(solution)/shard_map/ppermute | solution.py:299
  15.6 3.0 %collective-permute-done.1 = f32[64,128]{1,0:T(8,128)S(1)} collective-permute-done((f32[64,128]{1,0:T(8,128)S(1)}, f32[64,128]{1,0:T(8,128)S(1)}, u32[]{:S(2)}, u32[]{:S(2)}) %collective-permute-start.1) | collective-permute-done | bytes 32800 | tf_op jit(solution)/shard_map/ppermute | solution.py:299
  18.5 1.5 %collective-permute-start.2 = (f32[64,128]{1,0:T(8,128)S(1)}, f32[64,128]{1,0:T(8,128)S(1)}, u32[]{:S(2)}, u32[]{:S(2)}) collective-permute-start(f32[64,128]{1,0:T(8,128)S(1)} %add.12), channel_id=1, source_target_pairs={{0,9},{1,11},{2,8},{3,10},{4,14},{5,12},{6,15},{7,13},{8,2},{9,0},... | collective-permute-start | bytes 98312 | tf_op jit(solution)/shard_map/ppermute | solution.py:299
  20.0 0.1 collective-permute-start.10
  20.1 0.0 collective-permute-done.8.refs_5_
  20.1 0.4 %collective-permute-start.9 = (bf16[48,1024]{1,0:T(8,128)(2,1)S(1)}, bf16[48,1024]{1,0:T(8,128)(2,1)S(1)}, u32[]{:S(2)}, u32[]{:S(2)}) collective-permute-start(bf16[48,1024]{1,0:T(8,128)(2,1)S(1)} %collective-permute-done.8.refs_5_), channel_id=1, source_target_pairs={{0,8},{1,9},{2,10},{3,11},{4,12},{5,13},{6,14},{7,15},{8,0},{9,1},... | collective-permute-start | bytes 294920 | tf_op jit(solution)/shard_map/ppermute | solution.py:299
  20.5 1.4 %collective-permute-done.2 = f32[64,128]{1,0:T(8,128)S(1)} collective-permute-done((f32[64,128]{1,0:T(8,128)S(1)}, f32[64,128]{1,0:T(8,128)S(1)}, u32[]{:S(2)}, u32[]{:S(2)}) %collective-permute-start.2) | collective-permute-done | bytes 32800 | tf_op jit(solution)/shard_map/ppermute | solution.py:299
  21.9 1.4 %collective-permute-start.3 = (f32[64,128]{1,0:T(8,128)S(1)}, f32[64,128]{1,0:T(8,128)S(1)}, u32[]{:S(2)}, u32[]{:S(2)}) collective-permute-start(f32[64,128]{1,0:T(8,128)S(1)} %add.13), channel_id=1, source_target_pairs={{0,10},{1,8},{2,11},{3,9},{4,13},{5,15},{6,12},{7,14},{8,1},{9,3},... | collective-permute-start | bytes 98312 | tf_op jit(solution)/shard_map/ppermute | solution.py:299
  23.3 2.0 %collective-permute-done.3 = f32[64,128]{1,0:T(8,128)S(1)} collective-permute-done((f32[64,128]{1,0:T(8,128)S(1)}, f32[64,128]{1,0:T(8,128)S(1)}, u32[]{:S(2)}, u32[]{:S(2)}) %collective-permute-start.3) | collective-permute-done | bytes 32800 | tf_op jit(solution)/shard_map/ppermute | solution.py:299
  25.2 2.4 %collective-permute-start.4 = (f32[64,128]{1,0:T(8,128)S(1)}, f32[64,128]{1,0:T(8,128)S(1)}, u32[]{:S(2)}, u32[]{:S(2)}) collective-permute-start(f32[64,128]{1,0:T(8,128)S(1)} %add.14), channel_id=1, source_target_pairs={{0,12},{1,13},{2,14},{3,15},{4,8},{5,9},{6,10},{7,11},{8,4},{9,5},... | collective-permute-start | bytes 98312 | tf_op jit(solution)/shard_map/ppermute | solution.py:299
  27.7 1.8 %collective-permute-done.4 = f32[64,128]{1,0:T(8,128)S(1)} collective-permute-done((f32[64,128]{1,0:T(8,128)S(1)}, f32[64,128]{1,0:T(8,128)S(1)}, u32[]{:S(2)}, u32[]{:S(2)}) %collective-permute-start.4) | collective-permute-done | bytes 32800 | tf_op jit(solution)/shard_map/ppermute | solution.py:299
  29.5 0.3 %collective-permute-start.5 = (f32[64,128]{1,0:T(8,128)S(1)}, f32[64,128]{1,0:T(8,128)S(1)}, u32[]{:S(2)}, u32[]{:S(2)}) collective-permute-start(f32[64,128]{1,0:T(8,128)S(1)} %add.15.refs_0_), channel_id=1, source_target_pairs={{0,8},{1,9},{2,10},{3,11},{4,12},{5,13},{6,14},{7,15},{8,0},{9,1},... | collective-permute-start | bytes 98312 | tf_op jit(solution)/shard_map/ppermute | solution.py:299
  29.8 0.0 collective-permute-done.10.refs_7_
  29.8 0.0 collective-permute-done.9.refs_6_
  29.8 0.5 %shard_map.82 = (bf16[2,48,768]{2,1,0:T(8,128)(2,1)S(1)}, f32[2,48,768]{2,1,0:T(8,128)S(1)}) custom-call(s32[1]{0:T(128)S(6)} %copy.10.offset, s32[4]{0:T(128)S(4)} %get-tuple-element.18.places, f32[4]{0:T(128)S(4)} %get-tuple-element.19.rate, f32[64,128]{1,0:T(8,128)S(1)} %add.15.refs_0_, bf16[2,64,768]{2,1,0:T(8,128)(2,1)S(1)} %get-tuple-element.23.refs_1_, ...), custom_call_target="tpu_custom_call" | custom-call | tf_op jit(solution)/shard_map/pallas_call | solution.py:370
  30.3 0.4 %collective-permute-done.5.refs_0_ = f32[64,128]{1,0:T(8,128)S(1)} collective-permute-done((f32[64,128]{1,0:T(8,128)S(1)}, f32[64,128]{1,0:T(8,128)S(1)}, u32[]{:S(2)}, u32[]{:S(2)}) %collective-permute-start.5) | collective-permute-done | bytes 32800 | tf_op jit(solution)/shard_map/ppermute | solution.py:299
  30.7 1.1 %shard_map.83 = bf16[4,48,768]{2,1,0:T(8,128)(2,1)} custom-call(s32[1]{0:T(128)S(6)} %copy.10.offset, s32[4]{0:T(128)S(4)} %get-tuple-element.18.places, f32[4]{0:T(128)S(4)} %get-tuple-element.19.rate, f32[64,128]{1,0:T(8,128)S(1)} %collective-permute-done.5.refs_0_, bf16[2,64,768]{2,1,0:T(8,128)(2,1)S(1)} %get-tuple-element.23.refs_1_, ...), custom_call_target="tpu_custom_call" | custom-call | tf_op jit(solution)/shard_map/pallas_call | solution.py:370
  (6 shorter events, 0.0 us)
Async XLA Ops:
  0.0 12.2 %copy-start = (f32[4,64,64]{2,1,0:T(8,128)S(1)}, f32[4,64,64]{2,1,0:T(8,128)}, u32[]{:S(2)}) copy-start(f32[4,64,64]{2,1,0:T(8,128)} %driving.1) | copy-start | bytes 196612
  1.5 6.4 %collective-permute-start.6 = (bf16[16,1024]{1,0:T(8,128)(2,1)S(1)}, bf16[16,1024]{1,0:T(8,128)(2,1)S(1)}, u32[]{:S(2)}, u32[]{:S(2)}) collective-permute-start(bf16[16,1024]{1,0:T(8,128)(2,1)S(1)} %get-tuple-element.24), channel_id=1, source_target_pairs={{0,4},{1,5},{2,6},{3,7},{4,0},{5,1},{6,2},{7,3},{8,12},{9,13},{10,... | collective-permute-start | bytes 98312 | tf_op jit(solution)/shard_map/ppermute | solution.py:299
  7.9 4.3 %collective-permute-start.7 = (bf16[32,1024]{1,0:T(8,128)(2,1)S(1)}, bf16[32,1024]{1,0:T(8,128)(2,1)S(1)}, u32[]{:S(2)}, u32[]{:S(2)}) collective-permute-start(bf16[32,1024]{1,0:T(8,128)(2,1)S(1)} %constant_dynamic-update-slice_fusion.first), channel_id=1, source_target_pairs={{0,2},{1,3},{2,0},{3,1},{4,6},{5,7},{6,4},{7,5},{8,10},{9,11},{10,... | collective-permute-start | bytes 196616 | tf_op jit(solution)/shard_map/ppermute | solution.py:299
  12.3 7.7 %collective-permute-start.8 = (bf16[48,1024]{1,0:T(8,128)(2,1)S(1)}, bf16[48,1024]{1,0:T(8,128)(2,1)S(1)}, u32[]{:S(2)}, u32[]{:S(2)}) collective-permute-start(bf16[48,1024]{1,0:T(8,128)(2,1)S(1)} %get-tuple-element.28), channel_id=1, source_target_pairs={{0,24},{1,25},{2,26},{3,27},{4,28},{5,29},{6,30},{7,31},{8,16},{9,... | collective-permute-start | bytes 294920 | tf_op jit(solution)/shard_map/ppermute | solution.py:299
  12.4 2.6 %collective-permute-start = (f32[48,128]{1,0:T(8,128)S(1)}, f32[48,128]{1,0:T(8,128)S(1)}, u32[]{:S(2)}, u32[]{:S(2)}) collective-permute-start(f32[48,128]{1,0:T(8,128)S(1)} %get-tuple-element.21), channel_id=1, source_target_pairs={{0,8},{1,9},{2,10},{3,11},{4,12},{5,13},{6,14},{7,15},{8,0},{9,1},... | collective-permute-start | bytes 73736 | tf_op jit(solution)/shard_map/ppermute | solution.py:299
  15.2 3.3 %collective-permute-start.1 = (f32[64,128]{1,0:T(8,128)S(1)}, f32[64,128]{1,0:T(8,128)S(1)}, u32[]{:S(2)}, u32[]{:S(2)}) collective-permute-start(f32[64,128]{1,0:T(8,128)S(1)} %coeffs.1), channel_id=1, source_target_pairs={{0,24},{1,25},{2,26},{3,27},{4,28},{5,29},{6,30},{7,31},{8,16},{9,... | collective-permute-start | bytes 98312 | tf_op jit(solution)/shard_map/ppermute | solution.py:299
  18.5 3.3 %collective-permute-start.2 = (f32[64,128]{1,0:T(8,128)S(1)}, f32[64,128]{1,0:T(8,128)S(1)}, u32[]{:S(2)}, u32[]{:S(2)}) collective-permute-start(f32[64,128]{1,0:T(8,128)S(1)} %add.12), channel_id=1, source_target_pairs={{0,9},{1,11},{2,8},{3,10},{4,14},{5,12},{6,15},{7,13},{8,2},{9,0},... | collective-permute-start | bytes 98312 | tf_op jit(solution)/shard_map/ppermute | solution.py:299
  20.0 9.8 %collective-permute-start.10 = (bf16[48,1024]{1,0:T(8,128)(2,1)S(1)}, bf16[48,1024]{1,0:T(8,128)(2,1)S(1)}, u32[]{:S(2)}, u32[]{:S(2)}) collective-permute-start(bf16[48,1024]{1,0:T(8,128)(2,1)S(1)} %get-tuple-element.28), channel_id=1, source_target_pairs={{0,8},{1,9},{2,10},{3,11},{4,12},{5,13},{6,14},{7,15},{8,0},{9,1},... | collective-permute-start | bytes 294920 | tf_op jit(solution)/shard_map/ppermute | solution.py:299
  20.1 9.7 %collective-permute-start.9 = (bf16[48,1024]{1,0:T(8,128)(2,1)S(1)}, bf16[48,1024]{1,0:T(8,128)(2,1)S(1)}, u32[]{:S(2)}, u32[]{:S(2)}) collective-permute-start(bf16[48,1024]{1,0:T(8,128)(2,1)S(1)} %collective-permute-done.8.refs_5_), channel_id=1, source_target_pairs={{0,8},{1,9},{2,10},{3,11},{4,12},{5,13},{6,14},{7,15},{8,0},{9,1},... | collective-permute-start | bytes 294920 | tf_op jit(solution)/shard_map/ppermute | solution.py:299
  21.9 3.3 %collective-permute-start.3 = (f32[64,128]{1,0:T(8,128)S(1)}, f32[64,128]{1,0:T(8,128)S(1)}, u32[]{:S(2)}, u32[]{:S(2)}) collective-permute-start(f32[64,128]{1,0:T(8,128)S(1)} %add.13), channel_id=1, source_target_pairs={{0,10},{1,8},{2,11},{3,9},{4,13},{5,15},{6,12},{7,14},{8,1},{9,3},... | collective-permute-start | bytes 98312 | tf_op jit(solution)/shard_map/ppermute | solution.py:299
  25.2 4.2 %collective-permute-start.4 = (f32[64,128]{1,0:T(8,128)S(1)}, f32[64,128]{1,0:T(8,128)S(1)}, u32[]{:S(2)}, u32[]{:S(2)}) collective-permute-start(f32[64,128]{1,0:T(8,128)S(1)} %add.14), channel_id=1, source_target_pairs={{0,12},{1,13},{2,14},{3,15},{4,8},{5,9},{6,10},{7,11},{8,4},{9,5},... | collective-permute-start | bytes 98312 | tf_op jit(solution)/shard_map/ppermute | solution.py:299
  29.5 1.2 %collective-permute-start.5 = (f32[64,128]{1,0:T(8,128)S(1)}, f32[64,128]{1,0:T(8,128)S(1)}, u32[]{:S(2)}, u32[]{:S(2)}) collective-permute-start(f32[64,128]{1,0:T(8,128)S(1)} %add.15.refs_0_), channel_id=1, source_target_pairs={{0,8},{1,9},{2,10},{3,11},{4,12},{5,13},{6,14},{7,15},{8,0},{9,1},... | collective-permute-start | bytes 98312 | tf_op jit(solution)/shard_map/ppermute | solution.py:299

commit v5 on v4

--- a/solution.py
+++ b/solution.py
@@ -104,10 +104,12 @@
     def project(blocks, table):
         left = lax.broadcasted_iota(jnp.int32, table.shape, 1) < BASIS
         zero = jnp.zeros_like(table)
-        first, second = jnp.where(left, table, zero), jnp.where(left, zero, table)
+        both = jnp.concatenate([jnp.where(left, table, zero), jnp.where(left, zero, table)], 0)
+        pairs = [jnp.concatenate(blocks[k : k + 2], axis=1) for k in range(0, levels, 2)]
+        values = dot(jnp.concatenate(pairs, axis=0), both)
+        height = blocks[0].shape[0]
         for pair in range(levels // 2):
-            span = pl.ds(0, blocks[0].shape[0])
-            projected[pair, span] = dot(blocks[2 * pair], first) + dot(blocks[2 * pair + 1], second)
+            projected[pair, pl.ds(0, height)] = values[pair * height : (pair + 1) * height]
 
     @pl.when(jnp.logical_not(is_parent))
     def _():
@@ -205,7 +207,7 @@
     half = parity_of_device()
     pair = half if own_half else 1 - half
     if own_half:
-        tile, block_0, block_1, block_2, result, later_base, left, base = refs[4:]
+        tile, selected, block_0, block_1, block_2, result, later_base, left, base = refs[4:]
     else:
         earlier, base, out_hbm, left, result, sems = refs[4:]
     _, tile_rows, tile_cols = base.shape
@@ -235,20 +237,23 @@
 
     if own_half:
 
-        @pl.when(is_parent)
-        def _():
+        def feed(blocks):
             cell = lax.broadcasted_iota(jnp.int32, (tile_rows, third_cols), 0)
             strip = lax.rem(row * tile_rows + cell - offset[0] + full_rows, full_rows)
             covered = strip < full_rows // 3
             for goal, goal_pair in ((base, half), (later_base, 1 - half)):
                 for side in range(2):
                     level = 2 * goal_pair + side
-                    for third, block in enumerate((block_0, block_1, block_2)):
+                    for third, block in enumerate(blocks):
                         span = slice(third * third_cols, (third + 1) * third_cols)
                         lanes = pl.ds(pl.multiple_of(level * third_cols, 128), third_cols)
                         arrived = block[:, lanes].astype(jnp.float32)
                         own = tile[level, :, span].astype(jnp.float32)
                         goal[side, :, span] = jnp.where(covered, arrived, own)
+
+        even = half == 0
+        pl.when(is_parent & even)(lambda: feed((block_0, block_1, selected)))
+        pl.when(is_parent & jnp.logical_not(even))(lambda: feed((block_1, block_0, block_2)))
 
         @pl.when(jnp.logical_not(is_parent))
         def _():
@@ -346,10 +351,11 @@
         mine = mine + exchange(mine, masks[0], masks[1])
     other = exchange(mine, flip)
 
-    strips = [averaged]
+    pair = exchange(averaged, flip)
+    strips = [jnp.where(parity_of_device() == lax.axis_index("grp") % 2, averaged, pair)]
     for step, bit in enumerate(row_bits):
         held = strips[0] if step == 0 else jnp.concatenate(strips, 0)
-        strips = [held, exchange(held, mask_of(0, bit, 0))]
+        strips = [held, exchange(held, mask_of(0, bit, 0) ^ flip)]
     selected, weights, target = pl.pallas_call(
         functools.partial(select_kernel, full_rows, groups, len(row_bits), amplitude),
         out_shape=(
@@ -377,7 +383,7 @@
 
     two_levels = (2, tile_rows, tile_cols)
     earlier = finish(
-        "final_own", mine, (tile, block_0, block_1, block_2),
+        "final_own", mine, (tile, selected, block_0, block_1, block_2),
         (pltpu.VMEM(two_levels, bf16), pltpu.VMEM(two_levels, f32)), (VMEM, VMEM),
         [pltpu.VMEM(two_levels, f32)],
     )

time: 31.9 us -> 32.7 us (1.025)
  starting transfers between devices: 14 us -> 15.3 us
  waiting for transfers between devices: 13.6 us -> 13.1 us
    ppermute x11 -> x12, starting transfers between devices: 14 us -> 15.3 us  [exchange(): return lax.ppermute(value, AXES, pairs)]
    ppermute x11 -> x12, waiting for transfers between devices: 13.6 us -> 13.1 us  [exchange(): return lax.ppermute(value, AXES, pairs)]
  transfers between devices with their start and end apart: 11 -> 12, of which waited for: 8 -> 9; matrix products, arithmetic and copies ran while one was open for 0% -> 0% of each run, Pallas kernels for 2% -> 2%
where the time goes in v5:
time: 32.7 us; the launch traced here: 32.6 us
  starting transfers between devices  15.3 us (47%)
  waiting for transfers between devices  13.1 us (40%)
  Pallas kernels  3.45 us (11%)
  between operations  0.69 us (2%)
    ppermute x12, starting transfers between devices, exchange(): return lax.ppermute(value, AXES, pairs)  15.3 us
    ppermute x12, waiting for transfers between devices, exchange(): return lax.ppermute(value, AXES, pairs)  13.1 us
    pallas_call x2, Pallas kernels, finish(): pl.pallas_call(functools.partial(final_kernel, full_rows, groups, name ==...  1.59 us
    pallas_call x1, Pallas kernels, per_device(): pl.pallas_call(functools.partial(first_kernel, groups, col_count), out_sh...  1.49 us
  transfers between devices with their start and end apart: 12, of which 9 were waited for; matrix products, arithmetic and copies ran while one was open for 0% of the time, Pallas kernels for 2%

profile of v5, /device:TPU:0, one launch (start us, length us, event | category | flops | bytes accessed | tf_op | source)
XLA Modules:
  0.0 32.6 jit_solution(10204070812850219739)
XLA Ops:
  0.0 0.0 copy-start
  0.0 1.5 %first.1 = (bf16[16,1024]{1,0:T(8,128)(2,1)S(1)}, f32[48,128]{1,0:T(8,128)S(1)}, f32[48,128]{1,0:T(8,128)S(1)}, bf16[4,48,768]{2,1,0:T(8,128)(2,1)S(1)}, bf16[2,...) custom-call(bf16[4,48,768]{2,1,0:T(8,128)(2,1)} %bitcast.2, ...), custom_call_target="tpu_custom_call" | custom-call | tf_op jit(solution)/shard_map/first/pallas_call | solution.py:315
  1.5 0.6 %collective-permute-start.6 = (bf16[16,1024]{1,0:T(8,128)(2,1)S(1)}, bf16[16,1024]{1,0:T(8,128)(2,1)S(1)}, u32[]{:S(2)}, u32[]{:S(2)}) collective-permute-start(bf16[16,1024]{1,0:T(8,128)(2,1)S(1)} %get-tuple-element.24), channel_id=1, source_target_pairs={{0,8},{1,9},{2,10},{3,11},{4,12},{5,13},{6,14},{7,15},{8,0},{9,1},... | collective-permute-start | bytes 98312 | tf_op jit(solution)/shard_map/ppermute | solution.py:304
  2.1 0.9 %collective-permute-done.6 = bf16[16,1024]{1,0:T(8,128)(2,1)S(1)} collective-permute-done((bf16[16,1024]{1,0:T(8,128)(2,1)S(1)}, bf16[16,1024]{1,0:T(8,128)(2,1)S(1)}, u32[]{:S(2)}, u32[]{:S(2)}) %collective-permute-start.6) | collective-permute-done | bytes 32800 | tf_op jit(solution)/shard_map/ppermute | solution.py:304
  2.9 3.7 %collective-permute-start.7 = (bf16[16,1024]{1,0:T(8,128)(2,1)S(1)}, bf16[16,1024]{1,0:T(8,128)(2,1)S(1)}, u32[]{:S(2)}, u32[]{:S(2)}) collective-permute-start(bf16[16,1024]{1,0:T(8,128)(2,1)S(1)} %broadcast_select_fusion), channel_id=1, source_target_pairs={{0,12},{1,13},{2,14},{3,15},{4,8},{5,9},{6,10},{7,11},{8,4},{9,5},... | collective-permute-start | bytes 98312 | tf_op jit(solution)/shard_map/ppermute | solution.py:304
  6.6 1.6 %collective-permute-done.7 = bf16[16,1024]{1,0:T(8,128)(2,1)S(1)} collective-permute-done((bf16[16,1024]{1,0:T(8,128)(2,1)S(1)}, bf16[16,1024]{1,0:T(8,128)(2,1)S(1)}, u32[]{:S(2)}, u32[]{:S(2)}) %collective-permute-start.7) | collective-permute-done | bytes 32800 | tf_op jit(solution)/shard_map/ppermute | solution.py:304
  8.2 1.7 %collective-permute-start.8 = (bf16[32,1024]{1,0:T(8,128)(2,1)S(1)}, bf16[32,1024]{1,0:T(8,128)(2,1)S(1)}, u32[]{:S(2)}, u32[]{:S(2)}) collective-permute-start(bf16[32,1024]{1,0:T(8,128)(2,1)S(1)} %pad_maximum_fusion.first), channel_id=1, source_target_pairs={{0,10},{1,11},{2,8},{3,9},{4,14},{5,15},{6,12},{7,13},{8,2},{9,3},... | collective-permute-start | bytes 196616 | tf_op jit(solution)/shard_map/ppermute | solution.py:304
  10.6 1.6 %collective-permute-done.8.second = bf16[32,1024]{1,0:T(8,128)(2,1)S(1)} collective-permute-done((bf16[32,1024]{1,0:T(8,128)(2,1)S(1)}, bf16[32,1024]{1,0:T(8,128)(2,1)S(1)}, u32[]{:S(2)}, u32[]{:S(2)}) %collective-permute-start.8) | collective-permute-done | bytes 65568 | tf_op jit(solution)/shard_map/ppermute | solution.py:304
  12.2 0.0 copy-done
  12.2 0.2 select.3
  12.4 1.8 %collective-permute-start.9 = (bf16[48,1024]{1,0:T(8,128)(2,1)S(1)}, bf16[48,1024]{1,0:T(8,128)(2,1)S(1)}, u32[]{:S(2)}, u32[]{:S(2)}) collective-permute-start(bf16[48,1024]{1,0:T(8,128)(2,1)S(1)} %get-tuple-element.28.refs_5_), channel_id=1, source_target_pairs={{0,24},{1,25},{2,26},{3,27},{4,28},{5,29},{6,30},{7,31},{8,16},{9,... | collective-permute-start | bytes 294920 | tf_op jit(solution)/shard_map/ppermute | solution.py:304
  14.2 0.4 %collective-permute-start = (f32[48,128]{1,0:T(8,128)S(1)}, f32[48,128]{1,0:T(8,128)S(1)}, u32[]{:S(2)}, u32[]{:S(2)}) collective-permute-start(f32[48,128]{1,0:T(8,128)S(1)} %get-tuple-element.21), channel_id=1, source_target_pairs={{0,8},{1,9},{2,10},{3,11},{4,12},{5,13},{6,14},{7,15},{8,0},{9,1},... | collective-permute-start | bytes 73736 | tf_op jit(solution)/shard_map/ppermute | solution.py:304
  14.6 0.8 %collective-permute-done.partner = f32[48,128]{1,0:T(8,128)S(1)} collective-permute-done((f32[48,128]{1,0:T(8,128)S(1)}, f32[48,128]{1,0:T(8,128)S(1)}, u32[]{:S(2)}, u32[]{:S(2)}) %collective-permute-start) | collective-permute-done | bytes 24608 | tf_op jit(solution)/shard_map/ppermute | solution.py:304
  15.4 0.2 coeffs.1
  15.6 0.1 collective-permute-start.1
  15.7 3.3 %collective-permute-done.1 = f32[64,128]{1,0:T(8,128)S(1)} collective-permute-done((f32[64,128]{1,0:T(8,128)S(1)}, f32[64,128]{1,0:T(8,128)S(1)}, u32[]{:S(2)}, u32[]{:S(2)}) %collective-permute-start.1) | collective-permute-done | bytes 32800 | tf_op jit(solution)/shard_map/ppermute | solution.py:304
  19.0 1.5 %collective-permute-start.2 = (f32[64,128]{1,0:T(8,128)S(1)}, f32[64,128]{1,0:T(8,128)S(1)}, u32[]{:S(2)}, u32[]{:S(2)}) collective-permute-start(f32[64,128]{1,0:T(8,128)S(1)} %add.16), channel_id=1, source_target_pairs={{0,9},{1,11},{2,8},{3,10},{4,14},{5,12},{6,15},{7,13},{8,2},{9,0},... | collective-permute-start | bytes 98312 | tf_op jit(solution)/shard_map/ppermute | solution.py:304
  20.5 0.4 %collective-permute-start.11 = (bf16[48,1024]{1,0:T(8,128)(2,1)S(1)}, bf16[48,1024]{1,0:T(8,128)(2,1)S(1)}, u32[]{:S(2)}, u32[]{:S(2)}) collective-permute-start(bf16[48,1024]{1,0:T(8,128)(2,1)S(1)} %get-tuple-element.28.refs_5_), channel_id=1, source_target_pairs={{0,8},{1,9},{2,10},{3,11},{4,12},{5,13},{6,14},{7,15},{8,0},{9,1},... | collective-permute-start | bytes 294920 | tf_op jit(solution)/shard_map/ppermute | solution.py:304
  20.9 0.0 collective-permute-done.9.refs_6_
  20.9 0.1 collective-permute-start.10
  21.0 1.4 %collective-permute-done.2 = f32[64,128]{1,0:T(8,128)S(1)} collective-permute-done((f32[64,128]{1,0:T(8,128)S(1)}, f32[64,128]{1,0:T(8,128)S(1)}, u32[]{:S(2)}, u32[]{:S(2)}) %collective-permute-start.2) | collective-permute-done | bytes 32800 | tf_op jit(solution)/shard_map/ppermute | solution.py:304
  22.3 1.7 %collective-permute-start.3 = (f32[64,128]{1,0:T(8,128)S(1)}, f32[64,128]{1,0:T(8,128)S(1)}, u32[]{:S(2)}, u32[]{:S(2)}) collective-permute-start(f32[64,128]{1,0:T(8,128)S(1)} %add.17), channel_id=1, source_target_pairs={{0,10},{1,8},{2,11},{3,9},{4,13},{5,15},{6,12},{7,14},{8,1},{9,3},... | collective-permute-start | bytes 98312 | tf_op jit(solution)/shard_map/ppermute | solution.py:304
  24.1 1.6 %collective-permute-done.3 = f32[64,128]{1,0:T(8,128)S(1)} collective-permute-done((f32[64,128]{1,0:T(8,128)S(1)}, f32[64,128]{1,0:T(8,128)S(1)}, u32[]{:S(2)}, u32[]{:S(2)}) %collective-permute-start.3) | collective-permute-done | bytes 32800 | tf_op jit(solution)/shard_map/ppermute | solution.py:304
  25.7 3.0 %collective-permute-start.4 = (f32[64,128]{1,0:T(8,128)S(1)}, f32[64,128]{1,0:T(8,128)S(1)}, u32[]{:S(2)}, u32[]{:S(2)}) collective-permute-start(f32[64,128]{1,0:T(8,128)S(1)} %add.18), channel_id=1, source_target_pairs={{0,12},{1,13},{2,14},{3,15},{4,8},{5,9},{6,10},{7,11},{8,4},{9,5},... | collective-permute-start | bytes 98312 | tf_op jit(solution)/shard_map/ppermute | solution.py:304
  28.7 1.6 %collective-permute-done.4 = f32[64,128]{1,0:T(8,128)S(1)} collective-permute-done((f32[64,128]{1,0:T(8,128)S(1)}, f32[64,128]{1,0:T(8,128)S(1)}, u32[]{:S(2)}, u32[]{:S(2)}) %collective-permute-start.4) | collective-permute-done | bytes 32800 | tf_op jit(solution)/shard_map/ppermute | solution.py:304
  30.3 0.3 %collective-permute-start.5 = (f32[64,128]{1,0:T(8,128)S(1)}, f32[64,128]{1,0:T(8,128)S(1)}, u32[]{:S(2)}, u32[]{:S(2)}) collective-permute-start(f32[64,128]{1,0:T(8,128)S(1)} %add.19.refs_0_), channel_id=1, source_target_pairs={{0,8},{1,9},{2,10},{3,11},{4,12},{5,13},{6,14},{7,15},{8,0},{9,1},... | collective-permute-start | bytes 98312 | tf_op jit(solution)/shard_map/ppermute | solution.py:304
  30.6 0.0 collective-permute-done.11.refs_8_
  30.6 0.0 collective-permute-done.10.refs_7_
  30.6 0.5 %shard_map.82 = (bf16[2,48,768]{2,1,0:T(8,128)(2,1)S(1)}, f32[2,48,768]{2,1,0:T(8,128)S(1)}) custom-call(s32[1]{0:T(128)S(6)} %copy.9.offset, s32[4]{0:T(128)S(4)} %get-tuple-element.18.places, f32[4]{0:T(128)S(4)} %get-tuple-element.19.rate, f32[64,128]{1,0:T(8,128)S(1)} %add.19.refs_0_, bf16[2,64,768]{2,1,0:T(8,128)(2,1)S(1)} %get-tuple-element.23.refs_1_, ...), custom_call_target="tpu_custom_call" | custom-call | tf_op jit(solution)/shard_map/pallas_call | solution.py:376
  31.1 0.4 %collective-permute-done.5.refs_0_ = f32[64,128]{1,0:T(8,128)S(1)} collective-permute-done((f32[64,128]{1,0:T(8,128)S(1)}, f32[64,128]{1,0:T(8,128)S(1)}, u32[]{:S(2)}, u32[]{:S(2)}) %collective-permute-start.5) | collective-permute-done | bytes 32800 | tf_op jit(solution)/shard_map/ppermute | solution.py:304
  31.5 1.1 %shard_map.83 = bf16[4,48,768]{2,1,0:T(8,128)(2,1)} custom-call(s32[1]{0:T(128)S(6)} %copy.9.offset, s32[4]{0:T(128)S(4)} %get-tuple-element.18.places, f32[4]{0:T(128)S(4)} %get-tuple-element.19.rate, f32[64,128]{1,0:T(8,128)S(1)} %collective-permute-done.5.refs_0_, bf16[2,64,768]{2,1,0:T(8,128)(2,1)S(1)} %get-tuple-element.23.refs_1_, ...), custom_call_target="tpu_custom_call" | custom-call | tf_op jit(solution)/shard_map/pallas_call | solution.py:376
  (6 shorter events, 0.0 us)
Async XLA Ops:
  0.0 12.2 %copy-start = (f32[4,64,64]{2,1,0:T(8,128)S(1)}, f32[4,64,64]{2,1,0:T(8,128)}, u32[]{:S(2)}) copy-start(f32[4,64,64]{2,1,0:T(8,128)} %driving.1) | copy-start | bytes 196612
  1.5 1.4 %collective-permute-start.6 = (bf16[16,1024]{1,0:T(8,128)(2,1)S(1)}, bf16[16,1024]{1,0:T(8,128)(2,1)S(1)}, u32[]{:S(2)}, u32[]{:S(2)}) collective-permute-start(bf16[16,1024]{1,0:T(8,128)(2,1)S(1)} %get-tuple-element.24), channel_id=1, source_target_pairs={{0,8},{1,9},{2,10},{3,11},{4,12},{5,13},{6,14},{7,15},{8,0},{9,1},... | collective-permute-start | bytes 98312 | tf_op jit(solution)/shard_map/ppermute | solution.py:304
  2.9 5.3 %collective-permute-start.7 = (bf16[16,1024]{1,0:T(8,128)(2,1)S(1)}, bf16[16,1024]{1,0:T(8,128)(2,1)S(1)}, u32[]{:S(2)}, u32[]{:S(2)}) collective-permute-start(bf16[16,1024]{1,0:T(8,128)(2,1)S(1)} %broadcast_select_fusion), channel_id=1, source_target_pairs={{0,12},{1,13},{2,14},{3,15},{4,8},{5,9},{6,10},{7,11},{8,4},{9,5},... | collective-permute-start | bytes 98312 | tf_op jit(solution)/shard_map/ppermute | solution.py:304
  8.2 4.0 %collective-permute-start.8 = (bf16[32,1024]{1,0:T(8,128)(2,1)S(1)}, bf16[32,1024]{1,0:T(8,128)(2,1)S(1)}, u32[]{:S(2)}, u32[]{:S(2)}) collective-permute-start(bf16[32,1024]{1,0:T(8,128)(2,1)S(1)} %pad_maximum_fusion.first), channel_id=1, source_target_pairs={{0,10},{1,11},{2,8},{3,9},{4,14},{5,15},{6,12},{7,13},{8,2},{9,3},... | collective-permute-start | bytes 196616 | tf_op jit(solution)/shard_map/ppermute | solution.py:304
  12.4 8.5 %collective-permute-start.9 = (bf16[48,1024]{1,0:T(8,128)(2,1)S(1)}, bf16[48,1024]{1,0:T(8,128)(2,1)S(1)}, u32[]{:S(2)}, u32[]{:S(2)}) collective-permute-start(bf16[48,1024]{1,0:T(8,128)(2,1)S(1)} %get-tuple-element.28.refs_5_), channel_id=1, source_target_pairs={{0,24},{1,25},{2,26},{3,27},{4,28},{5,29},{6,30},{7,31},{8,16},{9,... | collective-permute-start | bytes 294920 | tf_op jit(solution)/shard_map/ppermute | solution.py:304
  14.2 1.2 %collective-permute-start = (f32[48,128]{1,0:T(8,128)S(1)}, f32[48,128]{1,0:T(8,128)S(1)}, u32[]{:S(2)}, u32[]{:S(2)}) collective-permute-start(f32[48,128]{1,0:T(8,128)S(1)} %get-tuple-element.21), channel_id=1, source_target_pairs={{0,8},{1,9},{2,10},{3,11},{4,12},{5,13},{6,14},{7,15},{8,0},{9,1},... | collective-permute-start | bytes 73736 | tf_op jit(solution)/shard_map/ppermute | solution.py:304
  15.6 3.3 %collective-permute-start.1 = (f32[64,128]{1,0:T(8,128)S(1)}, f32[64,128]{1,0:T(8,128)S(1)}, u32[]{:S(2)}, u32[]{:S(2)}) collective-permute-start(f32[64,128]{1,0:T(8,128)S(1)} %coeffs.1), channel_id=1, source_target_pairs={{0,24},{1,25},{2,26},{3,27},{4,28},{5,29},{6,30},{7,31},{8,16},{9,... | collective-permute-start | bytes 98312 | tf_op jit(solution)/shard_map/ppermute | solution.py:304
  19.0 3.3 %collective-permute-start.2 = (f32[64,128]{1,0:T(8,128)S(1)}, f32[64,128]{1,0:T(8,128)S(1)}, u32[]{:S(2)}, u32[]{:S(2)}) collective-permute-start(f32[64,128]{1,0:T(8,128)S(1)} %add.16), channel_id=1, source_target_pairs={{0,9},{1,11},{2,8},{3,10},{4,14},{5,12},{6,15},{7,13},{8,2},{9,0},... | collective-permute-start | bytes 98312 | tf_op jit(solution)/shard_map/ppermute | solution.py:304
  20.5 10.2 %collective-permute-start.11 = (bf16[48,1024]{1,0:T(8,128)(2,1)S(1)}, bf16[48,1024]{1,0:T(8,128)(2,1)S(1)}, u32[]{:S(2)}, u32[]{:S(2)}) collective-permute-start(bf16[48,1024]{1,0:T(8,128)(2,1)S(1)} %get-tuple-element.28.refs_5_), channel_id=1, source_target_pairs={{0,8},{1,9},{2,10},{3,11},{4,12},{5,13},{6,14},{7,15},{8,0},{9,1},... | collective-permute-start | bytes 294920 | tf_op jit(solution)/shard_map/ppermute | solution.py:304
  20.9 9.7 %collective-permute-start.10 = (bf16[48,1024]{1,0:T(8,128)(2,1)S(1)}, bf16[48,1024]{1,0:T(8,128)(2,1)S(1)}, u32[]{:S(2)}, u32[]{:S(2)}) collective-permute-start(bf16[48,1024]{1,0:T(8,128)(2,1)S(1)} %collective-permute-done.9.refs_6_), channel_id=1, source_target_pairs={{0,8},{1,9},{2,10},{3,11},{4,12},{5,13},{6,14},{7,15},{8,0},{9,1},... | collective-permute-start | bytes 294920 | tf_op jit(solution)/shard_map/ppermute | solution.py:304
  22.3 3.3 %collective-permute-start.3 = (f32[64,128]{1,0:T(8,128)S(1)}, f32[64,128]{1,0:T(8,128)S(1)}, u32[]{:S(2)}, u32[]{:S(2)}) collective-permute-start(f32[64,128]{1,0:T(8,128)S(1)} %add.17), channel_id=1, source_target_pairs={{0,10},{1,8},{2,11},{3,9},{4,13},{5,15},{6,12},{7,14},{8,1},{9,3},... | collective-permute-start | bytes 98312 | tf_op jit(solution)/shard_map/ppermute | solution.py:304
  25.7 4.6 %collective-permute-start.4 = (f32[64,128]{1,0:T(8,128)S(1)}, f32[64,128]{1,0:T(8,128)S(1)}, u32[]{:S(2)}, u32[]{:S(2)}) collective-permute-start(f32[64,128]{1,0:T(8,128)S(1)} %add.18), channel_id=1, source_target_pairs={{0,12},{1,13},{2,14},{3,15},{4,8},{5,9},{6,10},{7,11},{8,4},{9,5},... | collective-permute-start | bytes 98312 | tf_op jit(solution)/shard_map/ppermute | solution.py:304
  30.3 1.2 %collective-permute-start.5 = (f32[64,128]{1,0:T(8,128)S(1)}, f32[64,128]{1,0:T(8,128)S(1)}, u32[]{:S(2)}, u32[]{:S(2)}) collective-permute-start(f32[64,128]{1,0:T(8,128)S(1)} %add.19.refs_0_), channel_id=1, source_target_pairs={{0,8},{1,9},{2,10},{3,11},{4,12},{5,13},{6,14},{7,15},{8,0},{9,1},... | collective-permute-start | bytes 98312 | tf_op jit(solution)/shard_map/ppermute | solution.py:304

commit v6 on v5

--- a/solution.py
+++ b/solution.py
@@ -164,7 +164,9 @@
 
     table = jnp.concatenate([weights(group == groups - 1), weights((group ^ 1) == groups - 1)], 0)
     high, low = split(jnp.concatenate([mine[...], partner[...]], axis=0))
-    out[...] = dot(table, high, ((0,), (0,))) + dot(table, low, ((0,), (0,)))
+    out[...] = dot(
+        jnp.concatenate([table, table], 0), jnp.concatenate([high, low], 0), ((0,), (0,))
+    )
 
 
 def select_kernel(
@@ -348,7 +350,7 @@
         name="coeffs",
     )(offset, in_vmem(keep), in_vmem(partner), in_vmem(rows))
     for masks in zip(rounds, odd_rounds):
-        mine = mine + exchange(mine, masks[0], masks[1])
+        mine = mine + exchange(mine, masks[1], masks[0])
     other = exchange(mine, flip)
 
     pair = exchange(averaged, flip)

time: 32.7 us -> 32.7 us (level)
  no operation moved by 1% of the time
where the time goes in v6:
time: 32.7 us; the launch traced here: 32.6 us
  starting transfers between devices  15.3 us (47%)
  waiting for transfers between devices  13.1 us (40%)
  Pallas kernels  3.44 us (11%)
  between operations  0.69 us (2%)
    ppermute x12, starting transfers between devices, exchange(): return lax.ppermute(value, AXES, pairs)  15.3 us
    ppermute x12, waiting for transfers between devices, exchange(): return lax.ppermute(value, AXES, pairs)  13.1 us
    pallas_call x2, Pallas kernels, finish(): pl.pallas_call(functools.partial(final_kernel, full_rows, groups, name ==...  1.58 us
    pallas_call x1, Pallas kernels, per_device(): pl.pallas_call(functools.partial(first_kernel, groups, col_count), out_sh...  1.49 us
  transfers between devices with their start and end apart: 12, of which 9 were waited for; matrix products, arithmetic and copies ran while one was open for 0% of the time, Pallas kernels for 2%

profile of v6, /device:TPU:0, one launch (start us, length us, event | category | flops | bytes accessed | tf_op | source)
XLA Modules:
  0.0 32.6 jit_solution(3761999916123112865)
XLA Ops:
  0.0 0.0 copy-start
  0.0 1.5 %first.1 = (bf16[16,1024]{1,0:T(8,128)(2,1)S(1)}, f32[48,128]{1,0:T(8,128)S(1)}, f32[48,128]{1,0:T(8,128)S(1)}, bf16[4,48,768]{2,1,0:T(8,128)(2,1)S(1)}, bf16[2,...) custom-call(bf16[4,48,768]{2,1,0:T(8,128)(2,1)} %bitcast.2, ...), custom_call_target="tpu_custom_call" | custom-call | tf_op jit(solution)/shard_map/first/pallas_call | solution.py:317
  1.5 0.6 %collective-permute-start.6 = (bf16[16,1024]{1,0:T(8,128)(2,1)S(1)}, bf16[16,1024]{1,0:T(8,128)(2,1)S(1)}, u32[]{:S(2)}, u32[]{:S(2)}) collective-permute-start(bf16[16,1024]{1,0:T(8,128)(2,1)S(1)} %get-tuple-element.24), channel_id=1, source_target_pairs={{0,8},{1,9},{2,10},{3,11},{4,12},{5,13},{6,14},{7,15},{8,0},{9,1},... | collective-permute-start | bytes 98312 | tf_op jit(solution)/shard_map/ppermute | solution.py:306
  2.1 0.9 %collective-permute-done.6 = bf16[16,1024]{1,0:T(8,128)(2,1)S(1)} collective-permute-done((bf16[16,1024]{1,0:T(8,128)(2,1)S(1)}, bf16[16,1024]{1,0:T(8,128)(2,1)S(1)}, u32[]{:S(2)}, u32[]{:S(2)}) %collective-permute-start.6) | collective-permute-done | bytes 32800 | tf_op jit(solution)/shard_map/ppermute | solution.py:306
  2.9 3.7 %collective-permute-start.7 = (bf16[16,1024]{1,0:T(8,128)(2,1)S(1)}, bf16[16,1024]{1,0:T(8,128)(2,1)S(1)}, u32[]{:S(2)}, u32[]{:S(2)}) collective-permute-start(bf16[16,1024]{1,0:T(8,128)(2,1)S(1)} %broadcast_select_fusion), channel_id=1, source_target_pairs={{0,12},{1,13},{2,14},{3,15},{4,8},{5,9},{6,10},{7,11},{8,4},{9,5},... | collective-permute-start | bytes 98312 | tf_op jit(solution)/shard_map/ppermute | solution.py:306
  6.6 1.6 %collective-permute-done.7 = bf16[16,1024]{1,0:T(8,128)(2,1)S(1)} collective-permute-done((bf16[16,1024]{1,0:T(8,128)(2,1)S(1)}, bf16[16,1024]{1,0:T(8,128)(2,1)S(1)}, u32[]{:S(2)}, u32[]{:S(2)}) %collective-permute-start.7) | collective-permute-done | bytes 32800 | tf_op jit(solution)/shard_map/ppermute | solution.py:306
  8.2 1.7 %collective-permute-start.8 = (bf16[32,1024]{1,0:T(8,128)(2,1)S(1)}, bf16[32,1024]{1,0:T(8,128)(2,1)S(1)}, u32[]{:S(2)}, u32[]{:S(2)}) collective-permute-start(bf16[32,1024]{1,0:T(8,128)(2,1)S(1)} %pad_maximum_fusion.first), channel_id=1, source_target_pairs={{0,10},{1,11},{2,8},{3,9},{4,14},{5,15},{6,12},{7,13},{8,2},{9,3},... | collective-permute-start | bytes 196616 | tf_op jit(solution)/shard_map/ppermute | solution.py:306
  10.6 1.6 %collective-permute-done.8.second = bf16[32,1024]{1,0:T(8,128)(2,1)S(1)} collective-permute-done((bf16[32,1024]{1,0:T(8,128)(2,1)S(1)}, bf16[32,1024]{1,0:T(8,128)(2,1)S(1)}, u32[]{:S(2)}, u32[]{:S(2)}) %collective-permute-start.8) | collective-permute-done | bytes 65568 | tf_op jit(solution)/shard_map/ppermute | solution.py:306
  12.2 0.0 copy-done
  12.2 0.2 select.3
  12.4 1.8 %collective-permute-start.9 = (bf16[48,1024]{1,0:T(8,128)(2,1)S(1)}, bf16[48,1024]{1,0:T(8,128)(2,1)S(1)}, u32[]{:S(2)}, u32[]{:S(2)}) collective-permute-start(bf16[48,1024]{1,0:T(8,128)(2,1)S(1)} %get-tuple-element.28.refs_5_), channel_id=1, source_target_pairs={{0,24},{1,25},{2,26},{3,27},{4,28},{5,29},{6,30},{7,31},{8,16},{9,... | collective-permute-start | bytes 294920 | tf_op jit(solution)/shard_map/ppermute | solution.py:306
  14.2 0.4 %collective-permute-start = (f32[48,128]{1,0:T(8,128)S(1)}, f32[48,128]{1,0:T(8,128)S(1)}, u32[]{:S(2)}, u32[]{:S(2)}) collective-permute-start(f32[48,128]{1,0:T(8,128)S(1)} %get-tuple-element.21), channel_id=1, source_target_pairs={{0,8},{1,9},{2,10},{3,11},{4,12},{5,13},{6,14},{7,15},{8,0},{9,1},... | collective-permute-start | bytes 73736 | tf_op jit(solution)/shard_map/ppermute | solution.py:306
  14.6 0.8 %collective-permute-done.partner = f32[48,128]{1,0:T(8,128)S(1)} collective-permute-done((f32[48,128]{1,0:T(8,128)S(1)}, f32[48,128]{1,0:T(8,128)S(1)}, u32[]{:S(2)}, u32[]{:S(2)}) %collective-permute-start) | collective-permute-done | bytes 24608 | tf_op jit(solution)/shard_map/ppermute | solution.py:306
  15.4 0.2 coeffs.1
  15.6 0.1 collective-permute-start.1
  15.7 3.3 %collective-permute-done.1 = f32[64,128]{1,0:T(8,128)S(1)} collective-permute-done((f32[64,128]{1,0:T(8,128)S(1)}, f32[64,128]{1,0:T(8,128)S(1)}, u32[]{:S(2)}, u32[]{:S(2)}) %collective-permute-start.1) | collective-permute-done | bytes 32800 | tf_op jit(solution)/shard_map/ppermute | solution.py:306
  19.0 1.7 %collective-permute-start.2 = (f32[64,128]{1,0:T(8,128)S(1)}, f32[64,128]{1,0:T(8,128)S(1)}, u32[]{:S(2)}, u32[]{:S(2)}) collective-permute-start(f32[64,128]{1,0:T(8,128)S(1)} %add.16), channel_id=1, source_target_pairs={{0,10},{1,8},{2,11},{3,9},{4,13},{5,15},{6,12},{7,14},{8,1},{9,3},... | collective-permute-start | bytes 98312 | tf_op jit(solution)/shard_map/ppermute | solution.py:306
  20.7 0.0 collective-permute-start.11
  20.7 0.0 collective-permute-done.9.refs_6_
  20.7 0.5 %collective-permute-start.10 = (bf16[48,1024]{1,0:T(8,128)(2,1)S(1)}, bf16[48,1024]{1,0:T(8,128)(2,1)S(1)}, u32[]{:S(2)}, u32[]{:S(2)}) collective-permute-start(bf16[48,1024]{1,0:T(8,128)(2,1)S(1)} %collective-permute-done.9.refs_6_), channel_id=1, source_target_pairs={{0,8},{1,9},{2,10},{3,11},{4,12},{5,13},{6,14},{7,15},{8,0},{9,1},... | collective-permute-start | bytes 294920 | tf_op jit(solution)/shard_map/ppermute | solution.py:306
  21.2 1.1 %collective-permute-done.2 = f32[64,128]{1,0:T(8,128)S(1)} collective-permute-done((f32[64,128]{1,0:T(8,128)S(1)}, f32[64,128]{1,0:T(8,128)S(1)}, u32[]{:S(2)}, u32[]{:S(2)}) %collective-permute-start.2) | collective-permute-done | bytes 32800 | tf_op jit(solution)/shard_map/ppermute | solution.py:306
  22.3 1.5 %collective-permute-start.3 = (f32[64,128]{1,0:T(8,128)S(1)}, f32[64,128]{1,0:T(8,128)S(1)}, u32[]{:S(2)}, u32[]{:S(2)}) collective-permute-start(f32[64,128]{1,0:T(8,128)S(1)} %add.17), channel_id=1, source_target_pairs={{0,9},{1,11},{2,8},{3,10},{4,14},{5,12},{6,15},{7,13},{8,2},{9,0},... | collective-permute-start | bytes 98312 | tf_op jit(solution)/shard_map/ppermute | solution.py:306
  23.8 1.9 %collective-permute-done.3 = f32[64,128]{1,0:T(8,128)S(1)} collective-permute-done((f32[64,128]{1,0:T(8,128)S(1)}, f32[64,128]{1,0:T(8,128)S(1)}, u32[]{:S(2)}, u32[]{:S(2)}) %collective-permute-start.3) | collective-permute-done | bytes 32800 | tf_op jit(solution)/shard_map/ppermute | solution.py:306
  25.7 3.0 %collective-permute-start.4 = (f32[64,128]{1,0:T(8,128)S(1)}, f32[64,128]{1,0:T(8,128)S(1)}, u32[]{:S(2)}, u32[]{:S(2)}) collective-permute-start(f32[64,128]{1,0:T(8,128)S(1)} %add.18), channel_id=1, source_target_pairs={{0,12},{1,13},{2,14},{3,15},{4,8},{5,9},{6,10},{7,11},{8,4},{9,5},... | collective-permute-start | bytes 98312 | tf_op jit(solution)/shard_map/ppermute | solution.py:306
  28.7 1.6 %collective-permute-done.4 = f32[64,128]{1,0:T(8,128)S(1)} collective-permute-done((f32[64,128]{1,0:T(8,128)S(1)}, f32[64,128]{1,0:T(8,128)S(1)}, u32[]{:S(2)}, u32[]{:S(2)}) %collective-permute-start.4) | collective-permute-done | bytes 32800 | tf_op jit(solution)/shard_map/ppermute | solution.py:306
  30.3 0.3 %collective-permute-start.5 = (f32[64,128]{1,0:T(8,128)S(1)}, f32[64,128]{1,0:T(8,128)S(1)}, u32[]{:S(2)}, u32[]{:S(2)}) collective-permute-start(f32[64,128]{1,0:T(8,128)S(1)} %add.19.refs_0_), channel_id=1, source_target_pairs={{0,8},{1,9},{2,10},{3,11},{4,12},{5,13},{6,14},{7,15},{8,0},{9,1},... | collective-permute-start | bytes 98312 | tf_op jit(solution)/shard_map/ppermute | solution.py:306
  30.6 0.0 collective-permute-done.11.refs_8_
  30.6 0.0 collective-permute-done.10.refs_7_
  30.6 0.5 %shard_map.82 = (bf16[2,48,768]{2,1,0:T(8,128)(2,1)S(1)}, f32[2,48,768]{2,1,0:T(8,128)S(1)}) custom-call(s32[1]{0:T(128)S(6)} %copy.9.offset, s32[4]{0:T(128)S(4)} %get-tuple-element.18.places, f32[4]{0:T(128)S(4)} %get-tuple-element.19.rate, f32[64,128]{1,0:T(8,128)S(1)} %add.19.refs_0_, bf16[2,64,768]{2,1,0:T(8,128)(2,1)S(1)} %get-tuple-element.23.refs_1_, ...), custom_call_target="tpu_custom_call" | custom-call | tf_op jit(solution)/shard_map/pallas_call | solution.py:378
  31.1 0.4 %collective-permute-done.5.refs_0_ = f32[64,128]{1,0:T(8,128)S(1)} collective-permute-done((f32[64,128]{1,0:T(8,128)S(1)}, f32[64,128]{1,0:T(8,128)S(1)}, u32[]{:S(2)}, u32[]{:S(2)}) %collective-permute-start.5) | collective-permute-done | bytes 32800 | tf_op jit(solution)/shard_map/ppermute | solution.py:306
  31.5 1.1 %shard_map.83 = bf16[4,48,768]{2,1,0:T(8,128)(2,1)} custom-call(s32[1]{0:T(128)S(6)} %copy.9.offset, s32[4]{0:T(128)S(4)} %get-tuple-element.18.places, f32[4]{0:T(128)S(4)} %get-tuple-element.19.rate, f32[64,128]{1,0:T(8,128)S(1)} %collective-permute-done.5.refs_0_, bf16[2,64,768]{2,1,0:T(8,128)(2,1)S(1)} %get-tuple-element.23.refs_1_, ...), custom_call_target="tpu_custom_call" | custom-call | tf_op jit(solution)/shard_map/pallas_call | solution.py:378
  (6 shorter events, 0.0 us)
Async XLA Ops:
  0.0 12.2 %copy-start = (f32[4,64,64]{2,1,0:T(8,128)S(1)}, f32[4,64,64]{2,1,0:T(8,128)}, u32[]{:S(2)}) copy-start(f32[4,64,64]{2,1,0:T(8,128)} %driving.1) | copy-start | bytes 196612
  1.5 1.4 %collective-permute-start.6 = (bf16[16,1024]{1,0:T(8,128)(2,1)S(1)}, bf16[16,1024]{1,0:T(8,128)(2,1)S(1)}, u32[]{:S(2)}, u32[]{:S(2)}) collective-permute-start(bf16[16,1024]{1,0:T(8,128)(2,1)S(1)} %get-tuple-element.24), channel_id=1, source_target_pairs={{0,8},{1,9},{2,10},{3,11},{4,12},{5,13},{6,14},{7,15},{8,0},{9,1},... | collective-permute-start | bytes 98312 | tf_op jit(solution)/shard_map/ppermute | solution.py:306
  2.9 5.3 %collective-permute-start.7 = (bf16[16,1024]{1,0:T(8,128)(2,1)S(1)}, bf16[16,1024]{1,0:T(8,128)(2,1)S(1)}, u32[]{:S(2)}, u32[]{:S(2)}) collective-permute-start(bf16[16,1024]{1,0:T(8,128)(2,1)S(1)} %broadcast_select_fusion), channel_id=1, source_target_pairs={{0,12},{1,13},{2,14},{3,15},{4,8},{5,9},{6,10},{7,11},{8,4},{9,5},... | collective-permute-start | bytes 98312 | tf_op jit(solution)/shard_map/ppermute | solution.py:306
  8.2 4.0 %collective-permute-start.8 = (bf16[32,1024]{1,0:T(8,128)(2,1)S(1)}, bf16[32,1024]{1,0:T(8,128)(2,1)S(1)}, u32[]{:S(2)}, u32[]{:S(2)}) collective-permute-start(bf16[32,1024]{1,0:T(8,128)(2,1)S(1)} %pad_maximum_fusion.first), channel_id=1, source_target_pairs={{0,10},{1,11},{2,8},{3,9},{4,14},{5,15},{6,12},{7,13},{8,2},{9,3},... | collective-permute-start | bytes 196616 | tf_op jit(solution)/shard_map/ppermute | solution.py:306
  12.4 8.3 %collective-permute-start.9 = (bf16[48,1024]{1,0:T(8,128)(2,1)S(1)}, bf16[48,1024]{1,0:T(8,128)(2,1)S(1)}, u32[]{:S(2)}, u32[]{:S(2)}) collective-permute-start(bf16[48,1024]{1,0:T(8,128)(2,1)S(1)} %get-tuple-element.28.refs_5_), channel_id=1, source_target_pairs={{0,24},{1,25},{2,26},{3,27},{4,28},{5,29},{6,30},{7,31},{8,16},{9,... | collective-permute-start | bytes 294920 | tf_op jit(solution)/shard_map/ppermute | solution.py:306
  14.2 1.2 %collective-permute-start = (f32[48,128]{1,0:T(8,128)S(1)}, f32[48,128]{1,0:T(8,128)S(1)}, u32[]{:S(2)}, u32[]{:S(2)}) collective-permute-start(f32[48,128]{1,0:T(8,128)S(1)} %get-tuple-element.21), channel_id=1, source_target_pairs={{0,8},{1,9},{2,10},{3,11},{4,12},{5,13},{6,14},{7,15},{8,0},{9,1},... | collective-permute-start | bytes 73736 | tf_op jit(solution)/shard_map/ppermute | solution.py:306
  15.6 3.4 %collective-permute-start.1 = (f32[64,128]{1,0:T(8,128)S(1)}, f32[64,128]{1,0:T(8,128)S(1)}, u32[]{:S(2)}, u32[]{:S(2)}) collective-permute-start(f32[64,128]{1,0:T(8,128)S(1)} %coeffs.1), channel_id=1, source_target_pairs={{0,24},{1,25},{2,26},{3,27},{4,28},{5,29},{6,30},{7,31},{8,16},{9,... | collective-permute-start | bytes 98312 | tf_op jit(solution)/shard_map/ppermute | solution.py:306
  19.0 3.3 %collective-permute-start.2 = (f32[64,128]{1,0:T(8,128)S(1)}, f32[64,128]{1,0:T(8,128)S(1)}, u32[]{:S(2)}, u32[]{:S(2)}) collective-permute-start(f32[64,128]{1,0:T(8,128)S(1)} %add.16), channel_id=1, source_target_pairs={{0,10},{1,8},{2,11},{3,9},{4,13},{5,15},{6,12},{7,14},{8,1},{9,3},... | collective-permute-start | bytes 98312 | tf_op jit(solution)/shard_map/ppermute | solution.py:306
  20.7 9.9 %collective-permute-start.11 = (bf16[48,1024]{1,0:T(8,128)(2,1)S(1)}, bf16[48,1024]{1,0:T(8,128)(2,1)S(1)}, u32[]{:S(2)}, u32[]{:S(2)}) collective-permute-start(bf16[48,1024]{1,0:T(8,128)(2,1)S(1)} %get-tuple-element.28.refs_5_), channel_id=1, source_target_pairs={{0,8},{1,9},{2,10},{3,11},{4,12},{5,13},{6,14},{7,15},{8,0},{9,1},... | collective-permute-start | bytes 294920 | tf_op jit(solution)/shard_map/ppermute | solution.py:306
  20.7 9.9 %collective-permute-start.10 = (bf16[48,1024]{1,0:T(8,128)(2,1)S(1)}, bf16[48,1024]{1,0:T(8,128)(2,1)S(1)}, u32[]{:S(2)}, u32[]{:S(2)}) collective-permute-start(bf16[48,1024]{1,0:T(8,128)(2,1)S(1)} %collective-permute-done.9.refs_6_), channel_id=1, source_target_pairs={{0,8},{1,9},{2,10},{3,11},{4,12},{5,13},{6,14},{7,15},{8,0},{9,1},... | collective-permute-start | bytes 294920 | tf_op jit(solution)/shard_map/ppermute | solution.py:306
  22.3 3.3 %collective-permute-start.3 = (f32[64,128]{1,0:T(8,128)S(1)}, f32[64,128]{1,0:T(8,128)S(1)}, u32[]{:S(2)}, u32[]{:S(2)}) collective-permute-start(f32[64,128]{1,0:T(8,128)S(1)} %add.17), channel_id=1, source_target_pairs={{0,9},{1,11},{2,8},{3,10},{4,14},{5,12},{6,15},{7,13},{8,2},{9,0},... | collective-permute-start | bytes 98312 | tf_op jit(solution)/shard_map/ppermute | solution.py:306
  25.7 4.6 %collective-permute-start.4 = (f32[64,128]{1,0:T(8,128)S(1)}, f32[64,128]{1,0:T(8,128)S(1)}, u32[]{:S(2)}, u32[]{:S(2)}) collective-permute-start(f32[64,128]{1,0:T(8,128)S(1)} %add.18), channel_id=1, source_target_pairs={{0,12},{1,13},{2,14},{3,15},{4,8},{5,9},{6,10},{7,11},{8,4},{9,5},... | collective-permute-start | bytes 98312 | tf_op jit(solution)/shard_map/ppermute | solution.py:306
  30.3 1.2 %collective-permute-start.5 = (f32[64,128]{1,0:T(8,128)S(1)}, f32[64,128]{1,0:T(8,128)S(1)}, u32[]{:S(2)}, u32[]{:S(2)}) collective-permute-start(f32[64,128]{1,0:T(8,128)S(1)} %add.19.refs_0_), channel_id=1, source_target_pairs={{0,8},{1,9},{2,10},{3,11},{4,12},{5,13},{6,14},{7,15},{8,0},{9,1},... | collective-permute-start | bytes 98312 | tf_op jit(solution)/shard_map/ppermute | solution.py:306

commit v7 on v6

--- a/solution.py
+++ b/solution.py
@@ -229,13 +229,13 @@
     is_left = lax.broadcasted_iota(jnp.int32, (tile_rows, 2 * BASIS), 1) < BASIS
     for side in range(2):
         high, low = split(turned * rate[2 * pair + side])
-        low = pltpu.roll(low.astype(jnp.float32), BASIS, 1).astype(jnp.bfloat16)
         here = is_left if side == 0 else ~is_left
+        zero = jnp.zeros_like(high)
+        high, low = jnp.where(here, high, zero), jnp.where(here, low, zero)
         span = pl.ds(side * tile_rows, tile_rows)
-        left[span, : 2 * BASIS] = jnp.where(here, high, low)
-        left[span, 2 * BASIS :] = jnp.where(here, high, jnp.zeros_like(high))
+        left[span, :] = jnp.concatenate([high, low, high], axis=1)
     high, low = spread[0], spread[1]
-    increment = dot(left[...], jnp.concatenate([high, high, low, low], axis=0))
+    increment = dot(left[...], jnp.concatenate([high, high, high, high, low, low], axis=0))
 
     if own_half:
 
@@ -350,7 +350,7 @@
         name="coeffs",
     )(offset, in_vmem(keep), in_vmem(partner), in_vmem(rows))
     for masks in zip(rounds, odd_rounds):
-        mine = mine + exchange(mine, masks[1], masks[0])
+        mine = mine + exchange(mine, masks[0], masks[1])
     other = exchange(mine, flip)
 
     pair = exchange(averaged, flip)
@@ -380,7 +380,7 @@
             out_shape=out_shape,
             in_specs=[SMEM] * 3 + [VMEM] * len(values),
             out_specs=out_spec,
-            scratch_shapes=[pltpu.VMEM((2 * tile_rows, 4 * BASIS), bf16), *scratch],
+            scratch_shapes=[pltpu.VMEM((2 * tile_rows, 6 * BASIS), bf16), *scratch],
         )(offset, places, rate, *(in_vmem(value) for value in values))
 
     two_levels = (2, tile_rows, tile_cols)

time: 32.7 us -> 32.7 us (level)
  no operation moved by 1% of the time
where the time goes in v7:
time: 32.7 us; the launch traced here: 32.6 us
  starting transfers between devices  15.3 us (47%)
  waiting for transfers between devices  13.2 us (40%)
  Pallas kernels  3.39 us (10%)
  between operations  0.69 us (2%)
    ppermute x12, starting transfers between devices, exchange(): return lax.ppermute(value, AXES, pairs)  15.3 us
    ppermute x12, waiting for transfers between devices, exchange(): return lax.ppermute(value, AXES, pairs)  13.2 us
    pallas_call x2, Pallas kernels, finish(): pl.pallas_call(functools.partial(final_kernel, full_rows, groups, name ==...  1.53 us
    pallas_call x1, Pallas kernels, per_device(): pl.pallas_call(functools.partial(first_kernel, groups, col_count), out_sh...  1.49 us
  transfers between devices with their start and end apart: 12, of which 9 were waited for; matrix products, arithmetic and copies ran while one was open for 0% of the time, Pallas kernels for 2%

profile of v7, /device:TPU:0, one launch (start us, length us, event | category | flops | bytes accessed | tf_op | source)
XLA Modules:
  0.0 32.6 jit_solution(9102079686117934151)
XLA Ops:
  0.0 0.0 copy-start
  0.0 1.5 %first.1 = (bf16[16,1024]{1,0:T(8,128)(2,1)S(1)}, f32[48,128]{1,0:T(8,128)S(1)}, f32[48,128]{1,0:T(8,128)S(1)}, bf16[4,48,768]{2,1,0:T(8,128)(2,1)S(1)}, bf16[2,...) custom-call(bf16[4,48,768]{2,1,0:T(8,128)(2,1)} %bitcast.2, ...), custom_call_target="tpu_custom_call" | custom-call | tf_op jit(solution)/shard_map/first/pallas_call | solution.py:317
  1.5 0.6 %collective-permute-start.6 = (bf16[16,1024]{1,0:T(8,128)(2,1)S(1)}, bf16[16,1024]{1,0:T(8,128)(2,1)S(1)}, u32[]{:S(2)}, u32[]{:S(2)}) collective-permute-start(bf16[16,1024]{1,0:T(8,128)(2,1)S(1)} %get-tuple-element.24), channel_id=1, source_target_pairs={{0,8},{1,9},{2,10},{3,11},{4,12},{5,13},{6,14},{7,15},{8,0},{9,1},... | collective-permute-start | bytes 98312 | tf_op jit(solution)/shard_map/ppermute | solution.py:306
  2.1 0.9 %collective-permute-done.6 = bf16[16,1024]{1,0:T(8,128)(2,1)S(1)} collective-permute-done((bf16[16,1024]{1,0:T(8,128)(2,1)S(1)}, bf16[16,1024]{1,0:T(8,128)(2,1)S(1)}, u32[]{:S(2)}, u32[]{:S(2)}) %collective-permute-start.6) | collective-permute-done | bytes 32800 | tf_op jit(solution)/shard_map/ppermute | solution.py:306
  2.9 3.7 %collective-permute-start.7 = (bf16[16,1024]{1,0:T(8,128)(2,1)S(1)}, bf16[16,1024]{1,0:T(8,128)(2,1)S(1)}, u32[]{:S(2)}, u32[]{:S(2)}) collective-permute-start(bf16[16,1024]{1,0:T(8,128)(2,1)S(1)} %broadcast_select_fusion), channel_id=1, source_target_pairs={{0,12},{1,13},{2,14},{3,15},{4,8},{5,9},{6,10},{7,11},{8,4},{9,5},... | collective-permute-start | bytes 98312 | tf_op jit(solution)/shard_map/ppermute | solution.py:306
  6.6 1.6 %collective-permute-done.7 = bf16[16,1024]{1,0:T(8,128)(2,1)S(1)} collective-permute-done((bf16[16,1024]{1,0:T(8,128)(2,1)S(1)}, bf16[16,1024]{1,0:T(8,128)(2,1)S(1)}, u32[]{:S(2)}, u32[]{:S(2)}) %collective-permute-start.7) | collective-permute-done | bytes 32800 | tf_op jit(solution)/shard_map/ppermute | solution.py:306
  8.2 1.7 %collective-permute-start.8 = (bf16[32,1024]{1,0:T(8,128)(2,1)S(1)}, bf16[32,1024]{1,0:T(8,128)(2,1)S(1)}, u32[]{:S(2)}, u32[]{:S(2)}) collective-permute-start(bf16[32,1024]{1,0:T(8,128)(2,1)S(1)} %pad_maximum_fusion.first), channel_id=1, source_target_pairs={{0,10},{1,11},{2,8},{3,9},{4,14},{5,15},{6,12},{7,13},{8,2},{9,3},... | collective-permute-start | bytes 196616 | tf_op jit(solution)/shard_map/ppermute | solution.py:306
  10.6 1.6 %collective-permute-done.8.second = bf16[32,1024]{1,0:T(8,128)(2,1)S(1)} collective-permute-done((bf16[32,1024]{1,0:T(8,128)(2,1)S(1)}, bf16[32,1024]{1,0:T(8,128)(2,1)S(1)}, u32[]{:S(2)}, u32[]{:S(2)}) %collective-permute-start.8) | collective-permute-done | bytes 65568 | tf_op jit(solution)/shard_map/ppermute | solution.py:306
  12.2 0.0 copy-done
  12.2 0.2 select.3
  12.4 1.8 %collective-permute-start.9 = (bf16[48,1024]{1,0:T(8,128)(2,1)S(1)}, bf16[48,1024]{1,0:T(8,128)(2,1)S(1)}, u32[]{:S(2)}, u32[]{:S(2)}) collective-permute-start(bf16[48,1024]{1,0:T(8,128)(2,1)S(1)} %get-tuple-element.28.refs_5_), channel_id=1, source_target_pairs={{0,24},{1,25},{2,26},{3,27},{4,28},{5,29},{6,30},{7,31},{8,16},{9,... | collective-permute-start | bytes 294920 | tf_op jit(solution)/shard_map/ppermute | solution.py:306
  14.2 0.4 %collective-permute-start = (f32[48,128]{1,0:T(8,128)S(1)}, f32[48,128]{1,0:T(8,128)S(1)}, u32[]{:S(2)}, u32[]{:S(2)}) collective-permute-start(f32[48,128]{1,0:T(8,128)S(1)} %get-tuple-element.21), channel_id=1, source_target_pairs={{0,8},{1,9},{2,10},{3,11},{4,12},{5,13},{6,14},{7,15},{8,0},{9,1},... | collective-permute-start | bytes 73736 | tf_op jit(solution)/shard_map/ppermute | solution.py:306
  14.6 0.8 %collective-permute-done.partner = f32[48,128]{1,0:T(8,128)S(1)} collective-permute-done((f32[48,128]{1,0:T(8,128)S(1)}, f32[48,128]{1,0:T(8,128)S(1)}, u32[]{:S(2)}, u32[]{:S(2)}) %collective-permute-start) | collective-permute-done | bytes 24608 | tf_op jit(solution)/shard_map/ppermute | solution.py:306
  15.4 0.2 coeffs.1
  15.6 0.1 collective-permute-start.1
  15.7 3.3 %collective-permute-done.1 = f32[64,128]{1,0:T(8,128)S(1)} collective-permute-done((f32[64,128]{1,0:T(8,128)S(1)}, f32[64,128]{1,0:T(8,128)S(1)}, u32[]{:S(2)}, u32[]{:S(2)}) %collective-permute-start.1) | collective-permute-done | bytes 32800 | tf_op jit(solution)/shard_map/ppermute | solution.py:306
  19.0 1.5 %collective-permute-start.2 = (f32[64,128]{1,0:T(8,128)S(1)}, f32[64,128]{1,0:T(8,128)S(1)}, u32[]{:S(2)}, u32[]{:S(2)}) collective-permute-start(f32[64,128]{1,0:T(8,128)S(1)} %add.16), channel_id=1, source_target_pairs={{0,9},{1,11},{2,8},{3,10},{4,14},{5,12},{6,15},{7,13},{8,2},{9,0},... | collective-permute-start | bytes 98312 | tf_op jit(solution)/shard_map/ppermute | solution.py:306
  20.5 0.4 %collective-permute-start.11 = (bf16[48,1024]{1,0:T(8,128)(2,1)S(1)}, bf16[48,1024]{1,0:T(8,128)(2,1)S(1)}, u32[]{:S(2)}, u32[]{:S(2)}) collective-permute-start(bf16[48,1024]{1,0:T(8,128)(2,1)S(1)} %get-tuple-element.28.refs_5_), channel_id=1, source_target_pairs={{0,8},{1,9},{2,10},{3,11},{4,12},{5,13},{6,14},{7,15},{8,0},{9,1},... | collective-permute-start | bytes 294920 | tf_op jit(solution)/shard_map/ppermute | solution.py:306
  20.9 0.0 collective-permute-done.9.refs_6_
  20.9 0.1 collective-permute-start.10
  21.0 1.4 %collective-permute-done.2 = f32[64,128]{1,0:T(8,128)S(1)} collective-permute-done((f32[64,128]{1,0:T(8,128)S(1)}, f32[64,128]{1,0:T(8,128)S(1)}, u32[]{:S(2)}, u32[]{:S(2)}) %collective-permute-start.2) | collective-permute-done | bytes 32800 | tf_op jit(solution)/shard_map/ppermute | solution.py:306
  22.3 1.7 %collective-permute-start.3 = (f32[64,128]{1,0:T(8,128)S(1)}, f32[64,128]{1,0:T(8,128)S(1)}, u32[]{:S(2)}, u32[]{:S(2)}) collective-permute-start(f32[64,128]{1,0:T(8,128)S(1)} %add.17), channel_id=1, source_target_pairs={{0,10},{1,8},{2,11},{3,9},{4,13},{5,15},{6,12},{7,14},{8,1},{9,3},... | collective-permute-start | bytes 98312 | tf_op jit(solution)/shard_map/ppermute | solution.py:306
  24.1 1.6 %collective-permute-done.3 = f32[64,128]{1,0:T(8,128)S(1)} collective-permute-done((f32[64,128]{1,0:T(8,128)S(1)}, f32[64,128]{1,0:T(8,128)S(1)}, u32[]{:S(2)}, u32[]{:S(2)}) %collective-permute-start.3) | collective-permute-done | bytes 32800 | tf_op jit(solution)/shard_map/ppermute | solution.py:306
  25.7 3.0 %collective-permute-start.4 = (f32[64,128]{1,0:T(8,128)S(1)}, f32[64,128]{1,0:T(8,128)S(1)}, u32[]{:S(2)}, u32[]{:S(2)}) collective-permute-start(f32[64,128]{1,0:T(8,128)S(1)} %add.18), channel_id=1, source_target_pairs={{0,12},{1,13},{2,14},{3,15},{4,8},{5,9},{6,10},{7,11},{8,4},{9,5},... | collective-permute-start | bytes 98312 | tf_op jit(solution)/shard_map/ppermute | solution.py:306
  28.7 1.6 %collective-permute-done.4 = f32[64,128]{1,0:T(8,128)S(1)} collective-permute-done((f32[64,128]{1,0:T(8,128)S(1)}, f32[64,128]{1,0:T(8,128)S(1)}, u32[]{:S(2)}, u32[]{:S(2)}) %collective-permute-start.4) | collective-permute-done | bytes 32800 | tf_op jit(solution)/shard_map/ppermute | solution.py:306
  30.3 0.3 %collective-permute-start.5 = (f32[64,128]{1,0:T(8,128)S(1)}, f32[64,128]{1,0:T(8,128)S(1)}, u32[]{:S(2)}, u32[]{:S(2)}) collective-permute-start(f32[64,128]{1,0:T(8,128)S(1)} %add.19.refs_0_), channel_id=1, source_target_pairs={{0,8},{1,9},{2,10},{3,11},{4,12},{5,13},{6,14},{7,15},{8,0},{9,1},... | collective-permute-start | bytes 98312 | tf_op jit(solution)/shard_map/ppermute | solution.py:306
  30.6 0.0 collective-permute-done.11.refs_8_
  30.6 0.0 collective-permute-done.10.refs_7_
  30.6 0.5 %shard_map.82 = (bf16[2,48,768]{2,1,0:T(8,128)(2,1)S(1)}, f32[2,48,768]{2,1,0:T(8,128)S(1)}) custom-call(s32[1]{0:T(128)S(6)} %copy.9.offset, s32[4]{0:T(128)S(4)} %get-tuple-element.18.places, f32[4]{0:T(128)S(4)} %get-tuple-element.19.rate, f32[64,128]{1,0:T(8,128)S(1)} %add.19.refs_0_, bf16[2,64,768]{2,1,0:T(8,128)(2,1)S(1)} %get-tuple-element.23.refs_1_, ...), custom_call_target="tpu_custom_call" | custom-call | tf_op jit(solution)/shard_map/pallas_call | solution.py:378
  31.1 0.4 %collective-permute-done.5.refs_0_ = f32[64,128]{1,0:T(8,128)S(1)} collective-permute-done((f32[64,128]{1,0:T(8,128)S(1)}, f32[64,128]{1,0:T(8,128)S(1)}, u32[]{:S(2)}, u32[]{:S(2)}) %collective-permute-start.5) | collective-permute-done | bytes 32800 | tf_op jit(solution)/shard_map/ppermute | solution.py:306
  31.5 1.1 %shard_map.83 = bf16[4,48,768]{2,1,0:T(8,128)(2,1)} custom-call(s32[1]{0:T(128)S(6)} %copy.9.offset, s32[4]{0:T(128)S(4)} %get-tuple-element.18.places, f32[4]{0:T(128)S(4)} %get-tuple-element.19.rate, f32[64,128]{1,0:T(8,128)S(1)} %collective-permute-done.5.refs_0_, bf16[2,64,768]{2,1,0:T(8,128)(2,1)S(1)} %get-tuple-element.23.refs_1_, ...), custom_call_target="tpu_custom_call" | custom-call | tf_op jit(solution)/shard_map/pallas_call | solution.py:378
  (6 shorter events, 0.0 us)
Async XLA Ops:
  0.0 12.2 %copy-start = (f32[4,64,64]{2,1,0:T(8,128)S(1)}, f32[4,64,64]{2,1,0:T(8,128)}, u32[]{:S(2)}) copy-start(f32[4,64,64]{2,1,0:T(8,128)} %driving.1) | copy-start | bytes 196612
  1.5 1.4 %collective-permute-start.6 = (bf16[16,1024]{1,0:T(8,128)(2,1)S(1)}, bf16[16,1024]{1,0:T(8,128)(2,1)S(1)}, u32[]{:S(2)}, u32[]{:S(2)}) collective-permute-start(bf16[16,1024]{1,0:T(8,128)(2,1)S(1)} %get-tuple-element.24), channel_id=1, source_target_pairs={{0,8},{1,9},{2,10},{3,11},{4,12},{5,13},{6,14},{7,15},{8,0},{9,1},... | collective-permute-start | bytes 98312 | tf_op jit(solution)/shard_map/ppermute | solution.py:306
  2.9 5.3 %collective-permute-start.7 = (bf16[16,1024]{1,0:T(8,128)(2,1)S(1)}, bf16[16,1024]{1,0:T(8,128)(2,1)S(1)}, u32[]{:S(2)}, u32[]{:S(2)}) collective-permute-start(bf16[16,1024]{1,0:T(8,128)(2,1)S(1)} %broadcast_select_fusion), channel_id=1, source_target_pairs={{0,12},{1,13},{2,14},{3,15},{4,8},{5,9},{6,10},{7,11},{8,4},{9,5},... | collective-permute-start | bytes 98312 | tf_op jit(solution)/shard_map/ppermute | solution.py:306
  8.2 4.0 %collective-permute-start.8 = (bf16[32,1024]{1,0:T(8,128)(2,1)S(1)}, bf16[32,1024]{1,0:T(8,128)(2,1)S(1)}, u32[]{:S(2)}, u32[]{:S(2)}) collective-permute-start(bf16[32,1024]{1,0:T(8,128)(2,1)S(1)} %pad_maximum_fusion.first), channel_id=1, source_target_pairs={{0,10},{1,11},{2,8},{3,9},{4,14},{5,15},{6,12},{7,13},{8,2},{9,3},... | collective-permute-start | bytes 196616 | tf_op jit(solution)/shard_map/ppermute | solution.py:306
  12.4 8.5 %collective-permute-start.9 = (bf16[48,1024]{1,0:T(8,128)(2,1)S(1)}, bf16[48,1024]{1,0:T(8,128)(2,1)S(1)}, u32[]{:S(2)}, u32[]{:S(2)}) collective-permute-start(bf16[48,1024]{1,0:T(8,128)(2,1)S(1)} %get-tuple-element.28.refs_5_), channel_id=1, source_target_pairs={{0,24},{1,25},{2,26},{3,27},{4,28},{5,29},{6,30},{7,31},{8,16},{9,... | collective-permute-start | bytes 294920 | tf_op jit(solution)/shard_map/ppermute | solution.py:306
  14.2 1.2 %collective-permute-start = (f32[48,128]{1,0:T(8,128)S(1)}, f32[48,128]{1,0:T(8,128)S(1)}, u32[]{:S(2)}, u32[]{:S(2)}) collective-permute-start(f32[48,128]{1,0:T(8,128)S(1)} %get-tuple-element.21), channel_id=1, source_target_pairs={{0,8},{1,9},{2,10},{3,11},{4,12},{5,13},{6,14},{7,15},{8,0},{9,1},... | collective-permute-start | bytes 73736 | tf_op jit(solution)/shard_map/ppermute | solution.py:306
  15.6 3.4 %collective-permute-start.1 = (f32[64,128]{1,0:T(8,128)S(1)}, f32[64,128]{1,0:T(8,128)S(1)}, u32[]{:S(2)}, u32[]{:S(2)}) collective-permute-start(f32[64,128]{1,0:T(8,128)S(1)} %coeffs.1), channel_id=1, source_target_pairs={{0,24},{1,25},{2,26},{3,27},{4,28},{5,29},{6,30},{7,31},{8,16},{9,... | collective-permute-start | bytes 98312 | tf_op jit(solution)/shard_map/ppermute | solution.py:306
  19.0 3.3 %collective-permute-start.2 = (f32[64,128]{1,0:T(8,128)S(1)}, f32[64,128]{1,0:T(8,128)S(1)}, u32[]{:S(2)}, u32[]{:S(2)}) collective-permute-start(f32[64,128]{1,0:T(8,128)S(1)} %add.16), channel_id=1, source_target_pairs={{0,9},{1,11},{2,8},{3,10},{4,14},{5,12},{6,15},{7,13},{8,2},{9,0},... | collective-permute-start | bytes 98312 | tf_op jit(solution)/shard_map/ppermute | solution.py:306
  20.5 10.2 %collective-permute-start.11 = (bf16[48,1024]{1,0:T(8,128)(2,1)S(1)}, bf16[48,1024]{1,0:T(8,128)(2,1)S(1)}, u32[]{:S(2)}, u32[]{:S(2)}) collective-permute-start(bf16[48,1024]{1,0:T(8,128)(2,1)S(1)} %get-tuple-element.28.refs_5_), channel_id=1, source_target_pairs={{0,8},{1,9},{2,10},{3,11},{4,12},{5,13},{6,14},{7,15},{8,0},{9,1},... | collective-permute-start | bytes 294920 | tf_op jit(solution)/shard_map/ppermute | solution.py:306
  20.9 9.7 %collective-permute-start.10 = (bf16[48,1024]{1,0:T(8,128)(2,1)S(1)}, bf16[48,1024]{1,0:T(8,128)(2,1)S(1)}, u32[]{:S(2)}, u32[]{:S(2)}) collective-permute-start(bf16[48,1024]{1,0:T(8,128)(2,1)S(1)} %collective-permute-done.9.refs_6_), channel_id=1, source_target_pairs={{0,8},{1,9},{2,10},{3,11},{4,12},{5,13},{6,14},{7,15},{8,0},{9,1},... | collective-permute-start | bytes 294920 | tf_op jit(solution)/shard_map/ppermute | solution.py:306
  22.3 3.3 %collective-permute-start.3 = (f32[64,128]{1,0:T(8,128)S(1)}, f32[64,128]{1,0:T(8,128)S(1)}, u32[]{:S(2)}, u32[]{:S(2)}) collective-permute-start(f32[64,128]{1,0:T(8,128)S(1)} %add.17), channel_id=1, source_target_pairs={{0,10},{1,8},{2,11},{3,9},{4,13},{5,15},{6,12},{7,14},{8,1},{9,3},... | collective-permute-start | bytes 98312 | tf_op jit(solution)/shard_map/ppermute | solution.py:306
  25.7 4.6 %collective-permute-start.4 = (f32[64,128]{1,0:T(8,128)S(1)}, f32[64,128]{1,0:T(8,128)S(1)}, u32[]{:S(2)}, u32[]{:S(2)}) collective-permute-start(f32[64,128]{1,0:T(8,128)S(1)} %add.18), channel_id=1, source_target_pairs={{0,12},{1,13},{2,14},{3,15},{4,8},{5,9},{6,10},{7,11},{8,4},{9,5},... | collective-permute-start | bytes 98312 | tf_op jit(solution)/shard_map/ppermute | solution.py:306
  30.3 1.2 %collective-permute-start.5 = (f32[64,128]{1,0:T(8,128)S(1)}, f32[64,128]{1,0:T(8,128)S(1)}, u32[]{:S(2)}, u32[]{:S(2)}) collective-permute-start(f32[64,128]{1,0:T(8,128)S(1)} %add.19.refs_0_), channel_id=1, source_target_pairs={{0,8},{1,9},{2,10},{3,11},{4,12},{5,13},{6,14},{7,15},{8,0},{9,1},... | collective-permute-start | bytes 98312 | tf_op jit(solution)/shard_map/ppermute | solution.py:306
